TPU v7x, 512 devices: a whole 4x8x8 slice. The times are simulated.
512 devices in a mesh: gx: 8 (over z), gy: 8 (over y), gz: 8 (over x, core).
Axes of the slice: x: 4, y: 8, z: 8, core: 2. Of those that a mesh axis runs over, the one named last changes fastest.
Arguments:
- right_side: float32 [512, 512, 512], P('gx', 'gy', 'gz'), may hold values from -6 to 6
- guess: float32 [512, 512, 512], P('gx', 'gy', 'gz'), may hold values from -6 to 6
Outputs:
- solution: float32 [512, 512, 512], P('gx', 'gy', 'gz')
- residual: float32 [512, 512, 512], P('gx', 'gy', 'gz')
All inputs are finite; a program needn't handle non-finite values.
Results may differ from a plain program's by a relative error of at most 0.0003.
Values sent between devices are 32-bit elements.
A program may use at most 256 MiB of HBM per device.

v0:
```python
import jax
import jax.numpy as jnp
from jax import lax
from jax.experimental import pallas as pl
from jax.experimental.pallas import tpu as pltpu
from jax.sharding import PartitionSpec as P

LEVELS = 7
COARSE_SWEEPS = 4
GATHER = 3
LANES = 128
AXES = ("gx", "gy", "gz")


def rows_of(count):
    return max(8, count)


def lane_iota(rows):
    return lax.broadcasted_iota(jnp.int32, (rows, LANES), 1)


def row_iota(rows):
    return lax.broadcasted_iota(jnp.int32, (rows, LANES), 0)


def loop(count, body):
    if count == 1:
        body(0)
    else:
        def step(i, carry):
            body(i)
            return carry
        lax.fori_loop(0, count, step, 0)


def exact_dot(value, matrix):
    first = value.astype(jnp.bfloat16)
    rest = value - first.astype(jnp.float32)
    second = rest.astype(jnp.bfloat16)
    third = (rest - second.astype(jnp.float32)).astype(jnp.bfloat16)
    dot = lambda part: jnp.dot(part, matrix, preferred_element_type=jnp.float32)
    return (dot(third) + dot(second)) + dot(first)


def widest(count, most):
    return max(size for size in range(1, count + 1) if count % size == 0 and (size <= most or size == 1))


class Level:
    def __init__(self, number, dims, places, counts, v, s, w, d):
        self.number, self.dims, self.places, self.counts = number, dims, places, counts
        self.v, self.s, self.w, self.d = v, s, w, d
        self.rows = rows_of(dims[1])
        self.scale = 4.0 ** number
        self.inverse = 0.25 ** number
        self.chunk = min(dims[0], max(2, 32 * 8 // self.rows))

    def prepare(self):
        x, y, z = self.dims
        row, lane = row_iota(self.rows), lane_iota(self.rows)
        valid = (row < y) & (lane < z)
        at_y, at_z = self.places[1] * y + row, self.places[2] * z + lane
        one = lambda at, total: (at == 0).astype(jnp.float32) + (at == total - 1).astype(jnp.float32)
        base = 6.0 + one(at_y, self.counts[1] * y) + one(at_z, self.counts[2] * z)
        for wall in range(2):
            self.d[wall] = jnp.where(valid, base + wall, 0.0)
            for parity in range(2):
                self.w[2 * wall + parity] = jnp.where(valid & ((row + lane) % 2 == parity), 1.0 / (base + wall), 0.0)
        self.v[...] = jnp.zeros_like(self.v)

    def wall(self, plane):
        at = self.places[0] * self.dims[0] + plane
        last = self.counts[0] * self.dims[0] - 1
        if isinstance(at, int):
            return int(at in (0, last))
        return jnp.where((at == 0) | (at == last), 1, 0)

    def total(self, start, face):
        count, rows, z = self.chunk, self.rows, self.dims[2]
        slab = self.v[pl.ds(start, count + 2), pl.ds(8, rows), :]
        centre = slab[1:-1]
        total = slab[2:] + slab[:-2]
        total = total + self.v[pl.ds(start + 1, count), pl.ds(9, rows), :] + self.v[pl.ds(start + 1, count), pl.ds(7, rows), :]
        lane = lane_iota(rows)
        out = []
        for i in range(count):
            c = centre[i]
            if face is None:
                z_sum = pltpu.roll(c, 1, 1) + pltpu.roll(c, LANES - 1, 1)
            else:
                g = pltpu.roll(face[...], LANES - (start + i), 1)
                if z != 64:
                    g_high = pltpu.roll(g, LANES + z - 64, 1) if z < 64 else g
                    high = jnp.where(lane == z, g_high, c)
                else:
                    high = jnp.where(lane == 64, g, c)
                z_sum = jnp.where(lane == 0, g, pltpu.roll(c, 1, 1)) + pltpu.roll(high, LANES - 1, 1)
            out.append(total[i] + z_sum)
        return out, [centre[i] for i in range(count)]

    def sweep(self, colour, face=None, zero=False):
        def body(step):
            start = step * self.chunk
            if not zero:
                totals, centres = self.total(start, face)
            results = []
            for i in range(self.chunk):
                weight = self.w[2 * self.wall(start + i) + (i + colour) % 2]
                given = self.scale * self.s[start + i]
                if zero:
                    results.append(given * weight)
                else:
                    results.append(jnp.where(weight > 0, (given + totals[i]) * weight, centres[i]))
            for i in range(self.chunk):
                self.v[start + i + 1, pl.ds(8, self.rows), :] = results[i]
        loop(self.dims[0] // self.chunk, body)

    def remainder(self, start, face):
        totals, centres = self.total(start, face)
        out = []
        for i in range(self.chunk):
            d = self.d[self.wall(start + i)]
            out.append(jnp.where(d > 0, self.s[start + i] - (d * centres[i] - totals[i]) * self.inverse, 0.0))
        return out

    def restrict_to(self, target, pairs, face=None):
        rows, z = self.rows, self.dims[2]
        coarse_rows = rows_of(self.dims[1] // 2)
        half = self.chunk // 2
        source_lane = lax.broadcasted_iota(jnp.int32, (LANES, LANES), 0)
        target_lane = lax.broadcasted_iota(jnp.int32, (LANES, LANES), 1)
        halve = jnp.where((source_lane // 2 == target_lane) & (source_lane < z), 0.125, 0.0).astype(jnp.bfloat16)
        if rows < 16:
            pairs[...] = jnp.zeros_like(pairs)

        def first(step):
            r = self.remainder(step * self.chunk, face)
            for i in range(half):
                pairs[step * half + i, pl.ds(0, rows), :] = r[2 * i] + r[2 * i + 1]
        loop(self.dims[0] // self.chunk, first)

        planes = self.dims[0] // 2
        many = min(planes, max(1, 256 // coarse_rows))

        def second(step):
            at = pl.ds(step * many, many)
            q = pairs[at, pl.ds(0, coarse_rows, stride=2), :] + pairs[at, pl.ds(1, coarse_rows, stride=2), :]
            q = exact_dot(q.reshape(many * coarse_rows, LANES), halve)
            target[at] = q.reshape(many, coarse_rows, LANES)
        loop(planes // many, second)

    def reflect(self):
        x, y, z = self.dims
        v = self.v

        def low_x():
            v[0] = -v[1]

        def high_x():
            v[x + 1] = -v[x]

        def low_y():
            for_all = pl.ds(1, x)
            v[for_all, pl.ds(7, 1), :] = -v[for_all, pl.ds(8, 1), :]

        def high_y():
            for_all = pl.ds(1, x)
            v[for_all, pl.ds(8 + y, 1), :] = -v[for_all, pl.ds(7 + y, 1), :]

        for axis, low, high in ((0, low_x, high_x), (1, low_y, high_y)):
            if isinstance(self.counts[axis], int) and isinstance(self.places[axis], int):
                low()
                high()
            else:
                pl.when(self.places[axis] == 0)(low)
                pl.when(self.places[axis] == self.counts[axis] - 1)(high)


def lift(v, dims, places, counts, fine, spread, high_lane, face=None):
    x, y, z = dims
    rows = rows_of(y)
    k = lax.broadcasted_iota(jnp.int32, (LANES, LANES), 0)
    f = lax.broadcasted_iota(jnp.int32, (LANES, LANES), 1)
    inside = f < 2 * z
    own = ((f // 2 == k) & inside).astype(jnp.float32)
    beside = ((f // 2 + 2 * (f % 2) - 1 == k) & inside & (k < z)).astype(jnp.float32)
    low_wall = jnp.where(places[2] == 0, 1.0, 0.0)
    high_wall = jnp.where(places[2] == counts[2] - 1, 1.0, 0.0)
    at_low, at_high = f == 0, f == 2 * z - 1
    beside = beside + jnp.where(at_low & (k == 0), -low_wall, 0.0) + jnp.where(at_low & (k == LANES - 1), 1.0 - low_wall, 0.0)
    beside = beside + jnp.where(at_high & (k == z - 1), -high_wall, 0.0) + jnp.where(at_high & (k == high_lane), 1.0 - high_wall, 0.0)
    both = (0.25 * (own + beside)).astype(jnp.bfloat16)
    own = (0.25 * own).astype(jnp.bfloat16)
    tall = rows + 16
    lane = lane_iota(rows)
    valid = row_iota(rows) < y

    many = widest(x + 2, 832 // tall)

    def first(step):
        at = pl.ds(step * many, many)
        spread[at] = exact_dot(v[at].reshape(many * tall, LANES), own).reshape(many, tall, LANES)
    loop((x + 2) // many, first)

    group = widest(x, 256 // rows)

    def second(step):
        es = []
        for i in range(group):
            plane = step * group + i
            e = v[plane + 1, pl.ds(8, rows), :]
            if face is not None:
                e = jnp.where(lane < z, e, pltpu.roll(face[...], (LANES - 1) - plane, 1))
            es.append(e)
        centres = exact_dot(jnp.concatenate(es, axis=0), both)
        for i in range(group):
            plane = step * group + i
            centre = centres[i * rows:(i + 1) * rows]
            ys = (spread[plane + 1, pl.ds(7, rows), :], spread[plane + 1, pl.ds(9, rows), :])
            for up_x in range(2):
                xs = centre + spread[plane + 2 * up_x, pl.ds(8, rows), :]
                for up_y in range(2):
                    q = xs + ys[up_y]
                    if y < rows:
                        q = jnp.where(valid, q, 0.0)
                    at = (2 * plane + up_x + 1, pl.ds(8 + up_y, rows, stride=2), slice(None))
                    fine.v[at] = fine.v[at] + q
    loop(x // group, second)


def solve_kernel(counts, blocks, coarse, uses, refs):
    right_side, guess, out_v, out_r = refs[:4]
    refs = list(refs[4:])
    take = lambda: refs.pop(0)
    places = tuple(lax.axis_index(axis) for axis in AXES)
    levels = []
    for number, dims in enumerate(blocks[:GATHER]):
        levels.append(Level(number, dims, places, counts, take(), take(), take(), take()))
    for number, dims in enumerate(coarse):
        levels.append(Level(GATHER + number, dims, (0, 0, 0), (1, 1, 1), take(), take(), take(), take()))
    exchange = [(take(), take(), take(), take(), take()) for _ in range(GATHER)]
    pairs = [take() for _ in range(LEVELS - 1)]
    spreads = [take() for _ in range(LEVELS - 1)]
    block_s, block_v, packet, packets, gather_send, gather_recv = refs

    for level in levels:
        level.prepare()
    for number in range(GATHER):
        exchange[number][4][...] = jnp.zeros_like(exchange[number][4])
    z0 = blocks[0][2]
    top = levels[0]

    def load(x):
        top.v[x + 1, pl.ds(8, top.rows), pl.ds(0, z0)] = guess[x]
        top.s[x] = jnp.concatenate([right_side[x], jnp.zeros((top.rows, LANES - z0), jnp.float32)], axis=1)
    loop(blocks[0][0] // 4, lambda step: [load(4 * step + i) for i in range(4)])

    turn = [0] * GATHER
    sent = []

    def swap(number):
        level = levels[number]
        out, into, send, recv, face = exchange[number]
        n, v, (x, y, z) = turn[number], level.v, level.dims
        turn[number] += 1
        def folded(value):
            half = value.shape[0] // 2
            return jnp.where(lane_iota(half) < 64, value[:half], pltpu.roll(value[half:], 64, 1))

        def unfolded(value):
            low = lane_iota(value.shape[0]) < 64
            return jnp.concatenate([jnp.where(low, value, 0.0), jnp.where(low, pltpu.roll(value, 64, 1), 0.0)], axis=0)
        halves = (y // 2, y // 2, x // 2, x // 2, y, y)
        out[n, 0, pl.ds(0, y // 2)] = folded(v[x, pl.ds(8, y), :])
        out[n, 1, pl.ds(0, y // 2)] = folded(v[1, pl.ds(8, y), :])
        out[n, 2, pl.ds(0, x // 2)] = folded(v[pl.ds(1, x), 7 + y, :])
        out[n, 3, pl.ds(0, x // 2)] = folded(v[pl.ds(1, x), 8, :])
        lane = lane_iota(y)
        many = min(x, 16)

        def columns(step, carry):
            last, leading = carry
            for i in range(many):
                plane = step * many + i
                c = v[plane + 1, pl.ds(8, y), :]
                turned = pltpu.roll(c, plane + 64, 1)
                last = jnp.where(lane == (plane + 63 + z) % LANES, turned, last)
                leading = jnp.where(lane == plane + 64, turned, leading)
            return last, leading
        zero = jnp.zeros((y, LANES), jnp.float32)
        last, leading = lax.fori_loop(0, x // many, columns, (zero, zero))
        out[n, 4, pl.ds(0, y)] = last
        out[n, 5, pl.ds(0, y)] = leading

        copies = []
        for axis in range(3):
            for way in range(2):
                side = 2 * axis + way
                other = places[axis] + (1 - 2 * way)
                copy = pltpu.make_async_remote_copy(
                    src_ref=out.at[n, side, pl.ds(0, halves[side])], dst_ref=into.at[n, side, pl.ds(0, halves[side])],
                    send_sem=send.at[n, side], recv_sem=recv.at[n, side],
                    device_id={AXES[axis]: other}, device_id_type=pl.DeviceIdType.MESH)
                has_target = other < counts[axis] if way == 0 else other >= 0
                has_origin = places[axis] > 0 if way == 0 else places[axis] < counts[axis] - 1
                pl.when(has_target)(copy.start)
                sent.append((has_target, copy))
                copies.append((has_origin, copy))

        def land(side):
            got = into.at[n, side]
            if side == 0:
                v[0, pl.ds(8, y), :] = unfolded(got[pl.ds(0, y // 2)])
            elif side == 1:
                v[x + 1, pl.ds(8, y), :] = unfolded(got[pl.ds(0, y // 2)])
            elif side == 2:
                v[pl.ds(1, x), 7, :] = unfolded(got[pl.ds(0, x // 2)])
            elif side == 3:
                v[pl.ds(1, x), 8 + y, :] = unfolded(got[pl.ds(0, x // 2)])
            elif side == 4:
                face[...] = jnp.where(lane < 64, pltpu.roll(got[pl.ds(0, y)], (65 - z) % LANES, 1), face[...])
            else:
                face[...] = jnp.where(lane >= 64, got[pl.ds(0, y)], face[...])
        for side, (has_origin, copy) in enumerate(copies):
            @pl.when(has_origin)
            def _(side=side, copy=copy):
                copy.wait_recv()
                land(side)
        return face

    for number in range(GATHER):
        level = levels[number]
        if number == 0:
            level.sweep(0, swap(0))
        else:
            level.sweep(0, zero=True)
        level.sweep(1, swap(number))
        target = levels[number + 1].s if number + 1 < GATHER else block_s
        level.restrict_to(target, pairs[number], swap(number))

    bx, by, bz = blocks[GATHER]
    packed = block_s[0]
    for x in range(1, bx):
        packed = packed + pltpu.roll(block_s[x], x * bz, 1)
    packet[...] = packed
    total = counts[0] * counts[1] * counts[2]
    me = (places[0] * counts[1] + places[1]) * counts[2] + places[2]

    def gather_copy(source, target, offset):
        return pltpu.make_async_remote_copy(
            src_ref=packet, dst_ref=packets.at[source],
            send_sem=gather_send.at[target], recv_sem=gather_recv.at[source],
            device_id=(target // (counts[1] * counts[2]), target // counts[2] % counts[1], target % counts[2]),
            device_id_type=pl.DeviceIdType.MESH)

    def post(offset, carry):
        gather_copy(me, lax.rem(me + offset, total), offset).start()
        return carry
    lax.fori_loop(1, total, post, 0)
    packets[me] = packed

    def arrive(offset, carry):
        source = lax.rem(me + total - offset, total)
        gather_copy(source, lax.rem(me + offset, total), offset).wait_recv()
        return carry
    lax.fori_loop(1, total, arrive, 0)
    whole = levels[GATHER]
    lane = lane_iota(by)

    def unpack(step):
        px, py = step // counts[1], step % counts[1]
        for x in range(bx):
            row = jnp.zeros((by, LANES), jnp.float32)
            for pz in range(counts[2]):
                shifted = pltpu.roll(packets[step * counts[2] + pz], (pz * bz - x * bz) % LANES, 1)
                row = jnp.where((lane >= pz * bz) & (lane < pz * bz + bz), shifted, row)
            whole.s[px * bx + x, pl.ds(pl.multiple_of(py * by, 8), by), :] = row
    loop(counts[0] * counts[1], unpack)

    for number in range(GATHER, LEVELS - 1):
        level = levels[number]
        level.sweep(0, zero=True)
        level.sweep(1)
        level.restrict_to(levels[number + 1].s, pairs[number])
    level = levels[LEVELS - 1]
    level.sweep(0, zero=True)
    level.sweep(1)
    for _ in range(COARSE_SWEEPS - 1):
        level.sweep(0)
        level.sweep(1)
    for number in reversed(range(GATHER, LEVELS - 1)):
        level, below = levels[number], levels[number + 1]
        below.reflect()
        lift(below.v, below.dims, (0, 0, 0), (1, 1, 1), level, spreads[number], below.dims[2])
        level.sweep(0)
        level.sweep(1)

    whole.reflect()
    shift = lax.rem(LANES - places[2] * bz, LANES)
    for x in range(bx + 2):
        part = whole.v[places[0] * bx + x, pl.ds(pl.multiple_of(places[1] * by, 8), by + 16), :]
        block_v[x] = pltpu.roll(part, shift, 1)
    lift(block_v, blocks[GATHER], places, counts, levels[GATHER - 1], spreads[GATHER - 1], bz)
    for number in reversed(range(GATHER)):
        level = levels[number]
        level.sweep(0, swap(number))
        level.sweep(1, swap(number))
        face = swap(number)
        if number > 0:
            level.reflect()
            lift(level.v, level.dims, places, counts, levels[number - 1], spreads[number - 1], 63, face)

    def finish(step):
        r = top.remainder(step * top.chunk, face)
        for i in range(top.chunk):
            at = step * top.chunk + i
            out_r[at] = r[i][:, :z0]
            out_v[at] = top.v[at + 1, pl.ds(8, top.rows), pl.ds(0, z0)]
    loop(blocks[0][0] // top.chunk, finish)

    for has_target, copy in sent:
        pl.when(has_target)(copy.wait_send)

    def leave(offset, carry):
        gather_copy(me, lax.rem(me + offset, total), offset).wait_send()
        return carry
    lax.fori_loop(1, total, leave, 0)


def solution(mesh):
    counts = tuple(mesh.shape[axis] for axis in AXES)

    def per_device(right_side, guess):
        shape = right_side.shape
        blocks = [tuple(side >> level for side in shape) for level in range(GATHER + 1)]
        whole = tuple(side * count for side, count in zip(blocks[GATHER], counts))
        coarse = [tuple(side >> level for side in whole) for level in range(LEVELS - GATHER)]
        grids = blocks[:GATHER] + coarse
        scratch = []
        vmem = lambda *dims: scratch.append(pltpu.VMEM(dims, jnp.float32))
        for x, y, z in grids:
            vmem(x + 2, rows_of(y) + 16, LANES)
            vmem(x, rows_of(y), LANES)
            vmem(4, rows_of(y), LANES)
            vmem(2, rows_of(y), LANES)
        for number, (x, y, z) in enumerate(blocks[:GATHER]):
            turns = 6 if number == 0 else 5
            side = max(x, y)
            vmem(turns, 6, side, LANES)
            vmem(turns, 6, side, LANES)
            scratch.append(pltpu.SemaphoreType.DMA((turns, 6)))
            scratch.append(pltpu.SemaphoreType.DMA((turns, 6)))
            vmem(y, LANES)
        for x, y, z in grids[:-1]:
            vmem(x // 2, max(16, y), LANES)
        for number in range(LEVELS - 1):
            x, y, z = blocks[number + 1] if number < GATHER else grids[number + 1]
            vmem(x + 2, rows_of(y) + 16, LANES)
        bx, by, bz = blocks[GATHER]
        vmem(bx, by, LANES)
        vmem(bx + 2, by + 16, LANES)
        vmem(by, LANES)
        total = counts[0] * counts[1] * counts[2]
        vmem(total, by, LANES)
        scratch.append(pltpu.SemaphoreType.DMA((total,)))
        scratch.append(pltpu.SemaphoreType.DMA((total,)))

        def kernel(*refs):
            solve_kernel(counts, blocks, coarse, None, refs)

        whole_block = pl.BlockSpec(memory_space=pltpu.VMEM)
        return pl.pallas_call(
            kernel,
            out_shape=(jax.ShapeDtypeStruct(shape, jnp.float32),) * 2,
            in_specs=[whole_block] * 2,
            out_specs=(whole_block,) * 2,
            scratch_shapes=scratch,
            compiler_params=pltpu.CompilerParams(has_side_effects=True, vmem_limit_bytes=60 * 2**20),
            name="vcycle",
        )(right_side, guess)

    spec = P(*AXES)
    return jax.shard_map(per_device, mesh=mesh, in_specs=(spec, spec), out_specs=(spec, spec), check_vma=False)
```

profile of v0, /device:TPU:1, one launch (start us, length us, event | category | flops | bytes accessed | tf_op | source)
XLA Modules:
  0.0 236.8 jit_solution(16277412829101151449)
XLA Ops:
  0.6 231.5 %vcycle.1 = (f32[64,64,64]{2,1,0:T(8,128)}, f32[64,64,64]{2,1,0:T(8,128)}) custom-call(f32[64,64,64]{2,1,0:T(8,128)} %refs_0_.1, f32[64,64,64]{2,1,0:T(8,128)} %refs_1_.1), custom_call_target="tpu_custom_call" | custom-call | tf_op jit(solution)/shard_map/vcycle/pallas_call | solution.py:473
  232.1 0.0 copy-start
  232.1 3.3 %copy.6 = f32[64,64,64]{2,1,0:T(8,128)} copy(f32[64,64,64]{2,1,0:T(8,128)} %get-tuple-element.4) | data formatting | bytes 2097152
  235.4 0.0 copy-done
  235.5 1.3 copy.7
Async XLA Ops:
  232.1 3.3 %copy-start = (f32[64,64,64]{2,1,0:T(8,128)S(1)}, f32[64,64,64]{2,1,0:T(8,128)}, u32[]{:S(2)}) copy-start(f32[64,64,64]{2,1,0:T(8,128)} %get-tuple-element.5) | copy-start | bytes 3145732
where the time goes:
time: 238 us; the launch traced here: 237 us
  Pallas kernels  231 us (97%)
  local copies, waits for them, and re-layouts  4.63 us (2%)
    pallas_call x1, Pallas kernels, per_device(): pl.pallas_call(kernel, out_shape=(jax.ShapeDtypeStruct(shape, jnp.float32...  231 us

commit v1 on v0

--- a/solution.py
+++ b/solution.py
@@ -7,7 +7,7 @@
 
 LEVELS = 7
 COARSE_SWEEPS = 4
-GATHER = 3
+GATHER = 4
 LANES = 128
 AXES = ("gx", "gy", "gz")
 
@@ -242,10 +242,23 @@
     exchange = [(take(), take(), take(), take(), take()) for _ in range(GATHER)]
     pairs = [take() for _ in range(LEVELS - 1)]
     spreads = [take() for _ in range(LEVELS - 1)]
-    block_s, block_v, packet, packets, gather_send, gather_recv = refs
-
+    block_s, block_v, packet, line, joined, packets, line_send, line_recv, gather_send, gather_recv = refs
+
+    barrier = pltpu.get_barrier_semaphore()
+
+    def greet(device):
+        pl.semaphore_signal(barrier, inc=1, device_id=device, device_id_type=pl.DeviceIdType.MESH)
+
+    def greet_plane(offset, carry):
+        other = lax.rem(places[0] * counts[1] + places[1] + offset, counts[0] * counts[1])
+        greet({AXES[0]: other // counts[1], AXES[1]: other % counts[1]})
+        return carry
+    lax.fori_loop(1, counts[0] * counts[1], greet_plane, 0)
+    for offset in range(1, counts[2]):
+        greet({AXES[2]: lax.rem(places[2] + offset, counts[2])})
     for level in levels:
         level.prepare()
+    block_v[...] = jnp.zeros_like(block_v)
     for number in range(GATHER):
         exchange[number][4][...] = jnp.zeros_like(exchange[number][4])
     z0 = blocks[0][2]
@@ -256,6 +269,7 @@
         top.s[x] = jnp.concatenate([right_side[x], jnp.zeros((top.rows, LANES - z0), jnp.float32)], axis=1)
     loop(blocks[0][0] // 4, lambda step: [load(4 * step + i) for i in range(4)])
 
+    pl.semaphore_wait(barrier, counts[0] * counts[1] + counts[2] - 2)
     turn = [0] * GATHER
     sent = []
 
@@ -271,11 +285,14 @@
         def unfolded(value):
             low = lane_iota(value.shape[0]) < 64
             return jnp.concatenate([jnp.where(low, value, 0.0), jnp.where(low, pltpu.roll(value, 64, 1), 0.0)], axis=0)
-        halves = (y // 2, y // 2, x // 2, x // 2, y, y)
-        out[n, 0, pl.ds(0, y // 2)] = folded(v[x, pl.ds(8, y), :])
-        out[n, 1, pl.ds(0, y // 2)] = folded(v[1, pl.ds(8, y), :])
-        out[n, 2, pl.ds(0, x // 2)] = folded(v[pl.ds(1, x), 7 + y, :])
-        out[n, 3, pl.ds(0, x // 2)] = folded(v[pl.ds(1, x), 8, :])
+        if x // 2 < 8:
+            folded = unfolded = lambda value: value
+        half_y, half_x = max(8, y // 2), max(8, x // 2)
+        halves = (half_y, half_y, half_x, half_x, y, y)
+        out[n, 0, pl.ds(0, half_y)] = folded(v[x, pl.ds(8, y), :])
+        out[n, 1, pl.ds(0, half_y)] = folded(v[1, pl.ds(8, y), :])
+        out[n, 2, pl.ds(0, half_x)] = folded(v[pl.ds(1, x), 7 + y, :])
+        out[n, 3, pl.ds(0, half_x)] = folded(v[pl.ds(1, x), 8, :])
         lane = lane_iota(y)
         many = min(x, 16)
 
@@ -311,13 +328,13 @@
         def land(side):
             got = into.at[n, side]
             if side == 0:
-                v[0, pl.ds(8, y), :] = unfolded(got[pl.ds(0, y // 2)])
+                v[0, pl.ds(8, y), :] = unfolded(got[pl.ds(0, half_y)])
             elif side == 1:
-                v[x + 1, pl.ds(8, y), :] = unfolded(got[pl.ds(0, y // 2)])
+                v[x + 1, pl.ds(8, y), :] = unfolded(got[pl.ds(0, half_y)])
             elif side == 2:
-                v[pl.ds(1, x), 7, :] = unfolded(got[pl.ds(0, x // 2)])
+                v[pl.ds(1, x), 7, :] = unfolded(got[pl.ds(0, half_x)])
             elif side == 3:
-                v[pl.ds(1, x), 8 + y, :] = unfolded(got[pl.ds(0, x // 2)])
+                v[pl.ds(1, x), 8 + y, :] = unfolded(got[pl.ds(0, half_x)])
             elif side == 4:
                 face[...] = jnp.where(lane < 64, pltpu.roll(got[pl.ds(0, y)], (65 - z) % LANES, 1), face[...])
             else:
@@ -340,43 +357,52 @@
         level.restrict_to(target, pairs[number], swap(number))
 
     bx, by, bz = blocks[GATHER]
-    packed = block_s[0]
-    for x in range(1, bx):
-        packed = packed + pltpu.roll(block_s[x], x * bz, 1)
-    packet[...] = packed
-    total = counts[0] * counts[1] * counts[2]
-    me = (places[0] * counts[1] + places[1]) * counts[2] + places[2]
-
-    def gather_copy(source, target, offset):
+    nx, ny, nz = counts
+    wide = LANES // bx
+    packed = jnp.zeros((rows_of(by), LANES), jnp.float32)
+    for x in range(bx):
+        packed = packed + pltpu.roll(block_s[x], x * wide + places[2] * bz, 1)
+    packet[...] = packed[:by]
+
+    def line_copy(source, target):
         return pltpu.make_async_remote_copy(
-            src_ref=packet, dst_ref=packets.at[source],
-            send_sem=gather_send.at[target], recv_sem=gather_recv.at[source],
-            device_id=(target // (counts[1] * counts[2]), target // counts[2] % counts[1], target % counts[2]),
-            device_id_type=pl.DeviceIdType.MESH)
+            src_ref=packet, dst_ref=line.at[source], send_sem=line_send.at[target], recv_sem=line_recv.at[source],
+            device_id={AXES[2]: target}, device_id_type=pl.DeviceIdType.MESH)
+
+    for offset in range(1, nz):
+        line_copy(places[2], lax.rem(places[2] + offset, nz)).start()
+    merged = packed[:by]
+    for offset in range(1, nz):
+        source = lax.rem(places[2] + nz - offset, nz)
+        line_copy(source, lax.rem(places[2] + offset, nz)).wait_recv()
+        merged = merged + line[source]
+    joined[...] = merged
+    total = nx * ny
+    me = places[0] * ny + places[1]
+
+    def plane_copy(source, target):
+        return pltpu.make_async_remote_copy(
+            src_ref=joined, dst_ref=packets.at[source], send_sem=gather_send.at[target], recv_sem=gather_recv.at[source],
+            device_id={AXES[0]: target // ny, AXES[1]: target % ny}, device_id_type=pl.DeviceIdType.MESH)
 
     def post(offset, carry):
-        gather_copy(me, lax.rem(me + offset, total), offset).start()
+        plane_copy(me, lax.rem(me + offset, total)).start()
         return carry
     lax.fori_loop(1, total, post, 0)
-    packets[me] = packed
+    packets[me] = merged
 
     def arrive(offset, carry):
-        source = lax.rem(me + total - offset, total)
-        gather_copy(source, lax.rem(me + offset, total), offset).wait_recv()
+        plane_copy(lax.rem(me + total - offset, total), lax.rem(me + offset, total)).wait_recv()
         return carry
     lax.fori_loop(1, total, arrive, 0)
     whole = levels[GATHER]
-    lane = lane_iota(by)
-
-    def unpack(step):
-        px, py = step // counts[1], step % counts[1]
-        for x in range(bx):
-            row = jnp.zeros((by, LANES), jnp.float32)
-            for pz in range(counts[2]):
-                shifted = pltpu.roll(packets[step * counts[2] + pz], (pz * bz - x * bz) % LANES, 1)
-                row = jnp.where((lane >= pz * bz) & (lane < pz * bz + bz), shifted, row)
-            whole.s[px * bx + x, pl.ds(pl.multiple_of(py * by, 8), by), :] = row
-    loop(counts[0] * counts[1], unpack)
+
+    def unpack(px):
+        for py in range(0, ny, 2):
+            pair = jnp.concatenate([packets[px * ny + py], packets[px * ny + py + 1]], axis=0)
+            for x in range(bx):
+                whole.s[px * bx + x, pl.ds(py * by, 2 * by), :] = pltpu.roll(pair, LANES - x * wide, 1) if x else pair
+    loop(nx, unpack)
 
     for number in range(GATHER, LEVELS - 1):
         level = levels[number]
@@ -398,9 +424,10 @@
 
     whole.reflect()
     shift = lax.rem(LANES - places[2] * bz, LANES)
+    odd = lax.rem(places[1], 2) == 1
     for x in range(bx + 2):
-        part = whole.v[places[0] * bx + x, pl.ds(pl.multiple_of(places[1] * by, 8), by + 16), :]
-        block_v[x] = pltpu.roll(part, shift, 1)
+        part = whole.v[places[0] * bx + x, pl.ds(pl.multiple_of(places[1] // 2 * 8, 8), 24), :]
+        block_v[x, pl.ds(0, 20)] = pltpu.roll(jnp.where(odd, part[4:], part[:20]), shift, 1)
     lift(block_v, blocks[GATHER], places, counts, levels[GATHER - 1], spreads[GATHER - 1], bz)
     for number in reversed(range(GATHER)):
         level = levels[number]
@@ -422,8 +449,11 @@
     for has_target, copy in sent:
         pl.when(has_target)(copy.wait_send)
 
+    for offset in range(1, nz):
+        line_copy(places[2], lax.rem(places[2] + offset, nz)).wait_send()
+
     def leave(offset, carry):
-        gather_copy(me, lax.rem(me + offset, total), offset).wait_send()
+        plane_copy(me, lax.rem(me + offset, total)).wait_send()
         return carry
     lax.fori_loop(1, total, leave, 0)
 
@@ -458,13 +488,15 @@
             x, y, z = blocks[number + 1] if number < GATHER else grids[number + 1]
             vmem(x + 2, rows_of(y) + 16, LANES)
         bx, by, bz = blocks[GATHER]
-        vmem(bx, by, LANES)
-        vmem(bx + 2, by + 16, LANES)
+        vmem(bx, rows_of(by), LANES)
+        vmem(bx + 2, rows_of(by) + 16, LANES)
         vmem(by, LANES)
-        total = counts[0] * counts[1] * counts[2]
+        vmem(counts[2], by, LANES)
+        vmem(by, LANES)
+        total = counts[0] * counts[1]
         vmem(total, by, LANES)
-        scratch.append(pltpu.SemaphoreType.DMA((total,)))
-        scratch.append(pltpu.SemaphoreType.DMA((total,)))
+        for many in (counts[2], counts[2], total, total):
+            scratch.append(pltpu.SemaphoreType.DMA((many,)))
 
         def kernel(*refs):
             solve_kernel(counts, blocks, coarse, None, refs)
@@ -476,7 +508,7 @@
             in_specs=[whole_block] * 2,
             out_specs=(whole_block,) * 2,
             scratch_shapes=scratch,
-            compiler_params=pltpu.CompilerParams(has_side_effects=True, vmem_limit_bytes=60 * 2**20),
+            compiler_params=pltpu.CompilerParams(collective_id=0, has_side_effects=True, vmem_limit_bytes=60 * 2**20),
             name="vcycle",
         )(right_side, guess)
 

time: 238 us -> 156 us (0.66)
  Pallas kernels: 231 us -> 150 us
    pallas_call x1, Pallas kernels: 231 us -> 150 us  [per_device(): pl.pallas_call(kernel, out_shape=(jax.ShapeDtypeStruct(shape, jnp.float32...]
where the time goes in v1:
time: 156 us; the launch traced here: 155 us
  Pallas kernels  150 us (96%)
  local copies, waits for them, and re-layouts  4.63 us (3%)
    pallas_call x1, Pallas kernels, per_device(): pl.pallas_call(kernel, out_shape=(jax.ShapeDtypeStruct(shape, jnp.float32...  150 us
    unnamed x4, local copies, waits for them, and re-layouts  4.63 us

profile of v1, /device:TPU:1, one launch (start us, length us, event | category | flops | bytes accessed | tf_op | source)
XLA Modules:
  0.0 155.3 jit_solution(1193394152743242503)
XLA Ops:
  0.6 150.0 %vcycle.1 = (f32[64,64,64]{2,1,0:T(8,128)}, f32[64,64,64]{2,1,0:T(8,128)}) custom-call(f32[64,64,64]{2,1,0:T(8,128)} %refs_0_.1, f32[64,64,64]{2,1,0:T(8,128)} %refs_1_.1), custom_call_target="tpu_custom_call" | custom-call | tf_op jit(solution)/shard_map/vcycle/pallas_call | solution.py:505
  150.7 0.0 copy-start
  150.7 3.3 %copy.6 = f32[64,64,64]{2,1,0:T(8,128)} copy(f32[64,64,64]{2,1,0:T(8,128)} %get-tuple-element.4) | data formatting | bytes 2097152
  154.0 0.0 copy-done
  154.0 1.3 copy.7
Async XLA Ops:
  150.7 3.3 %copy-start = (f32[64,64,64]{2,1,0:T(8,128)S(1)}, f32[64,64,64]{2,1,0:T(8,128)}, u32[]{:S(2)}) copy-start(f32[64,64,64]{2,1,0:T(8,128)} %get-tuple-element.5) | copy-start | bytes 3145732

commit v2 on v1

v2 whole, which is shorter than its diff:
```python
import itertools

import jax
import jax.numpy as jnp
from jax import lax
from jax.experimental import pallas as pl
from jax.experimental.pallas import tpu as pltpu
from jax.sharding import PartitionSpec as P

LEVELS = 7
COARSE_SWEEPS = 4
SHARED = 4
LANES = 128
EDGE = 8
AXES = ("gx", "gy", "gz")
MESH = pl.DeviceIdType.MESH
WAYS = [way for way in itertools.product((-1, 0, 1), repeat=3) if any(way)]
FINAL = {1: 1, 2: 2, 3: 3}
REACH = {level: radius + 3 for level, radius in FINAL.items()}


def rows_of(count):
    return max(8, -(-count // 8) * 8)


def lane_iota(rows):
    return lax.broadcasted_iota(jnp.int32, (rows, LANES), 1)


def row_iota(rows):
    return lax.broadcasted_iota(jnp.int32, (rows, LANES), 0)


def loop(count, body):
    if count == 1:
        body(0)
    else:
        def step(i, carry):
            body(i)
            return carry
        lax.fori_loop(0, count, step, 0)


def turn(value, amount):
    amount = amount % LANES
    return pltpu.roll(value, amount, 1) if amount else value


def exact_dot(value, matrix):
    first = value.astype(jnp.bfloat16)
    rest = value - first.astype(jnp.float32)
    second = rest.astype(jnp.bfloat16)
    third = (rest - second.astype(jnp.float32)).astype(jnp.bfloat16)
    dot = lambda part: jnp.dot(part, matrix, preferred_element_type=jnp.float32)
    return (dot(third) + dot(second)) + dot(first)


def widest(count, most, step=1):
    return max(size for size in range(step, count + 1, step) if count % size == 0 and (size <= most or size == step))


def signed(lane):
    return jnp.where(lane < 64, lane, lane - LANES)


class Grid:
    def __init__(self, number, dims, places, counts, v, s, w, d):
        self.number, self.dims, self.places, self.counts = number, dims, places, counts
        self.v, self.s, self.w, self.d = v, s, w, d
        self.reach = REACH.get(number, 0)
        self.ox, self.start, self.height, _, _ = layout(number, dims)
        self.sx, self.sy = (EDGE, 8) if self.reach else (0, 0)
        self.rows = rows_of(dims[1])

    def prepare(self):
        x, y, z = self.dims
        beyond = EDGE if self.reach else 0

        def base(height, start):
            row, lane = row_iota(height) + (start - 8), signed(lane_iota(height))
            at_y, at_z = self.places[1] * y + row, self.places[2] * z + lane
            last_y, last_z = self.counts[1] * y - 1, self.counts[2] * z - 1
            valid = (lane >= -beyond) & (lane < z + beyond) & (row >= -beyond) & (row < y + beyond)
            valid = valid & (at_y >= 0) & (at_y <= last_y) & (at_z >= 0) & (at_z <= last_z)
            one = lambda at, last: (at == 0).astype(jnp.float32) + (at == last).astype(jnp.float32)
            return valid, 6.0 + one(at_y, last_y) + one(at_z, last_z)
        valid, diagonal = base(self.height, self.start)
        for wall in range(2):
            self.w[wall] = jnp.where(valid, 1.0 / (diagonal + wall), 0.0)
        self.w[2] = jnp.zeros_like(diagonal)
        valid, diagonal = base(self.rows, 8)
        for wall in range(2):
            self.d[wall] = jnp.where(valid, diagonal + wall, 0.0)
        self.v[...] = jnp.zeros_like(self.v)
        if self.reach:
            self.s[...] = jnp.zeros_like(self.s)

    def wall(self, plane, beyond=False):
        at = self.places[0] * self.dims[0] + plane
        last = self.counts[0] * self.dims[0] - 1
        if isinstance(at, int):
            return int(at in (0, last))
        kind = jnp.where((at == 0) | (at == last), 1, 0)
        return jnp.where((at < 0) | (at > last), 2, kind) if beyond else kind

    def total(self, plane, count, start, height, face):
        z = self.dims[2]
        at = plane + self.ox
        slab = self.v[pl.ds(at - 1, count + 2), pl.ds(start, height), :]
        centre = slab[1:-1]
        total = slab[2:] + slab[:-2]
        total = total + self.v[pl.ds(at, count), pl.ds(start + 1, height), :] + self.v[pl.ds(at, count), pl.ds(start - 1, height), :]
        lane = lane_iota(height)
        out = []
        for i in range(count):
            c = centre[i]
            if face is None:
                z_sum = pltpu.roll(c, 1, 1) + pltpu.roll(c, LANES - 1, 1)
            else:
                g = pltpu.roll(face[...], LANES - (plane + i), 1)
                high = jnp.where(lane == 64, g, c)
                z_sum = jnp.where(lane == 0, g, pltpu.roll(c, 1, 1)) + pltpu.roll(high, LANES - 1, 1)
            out.append(total[i] + z_sum)
        return out, [centre[i] for i in range(count)]

    def sweep(self, colour, face=None, zero=False, beyond=0):
        start, height = self.start, self.height
        planes = self.dims[0] + 2 * beyond
        chunk = widest(planes, 112 * 8 // height, 2)
        parity = (row_iota(height) + lane_iota(height) + start) % 2

        def body(step):
            first = step * chunk - beyond
            if not zero:
                totals, centres = self.total(first, chunk, start, height, face)
            results = []
            for i in range(chunk):
                weight = self.w[self.wall(first + i, beyond > 0)]
                given = self.s[first + i + self.sx, pl.ds(start - 8 + self.sy, height), :]
                mine = parity == (i + colour + beyond) % 2
                if zero:
                    results.append(jnp.where(mine, given * weight, 0.0))
                else:
                    results.append(jnp.where(mine, (given + totals[i]) * weight, centres[i]))
            for i in range(chunk):
                self.v[first + i + self.ox, pl.ds(start, height), :] = results[i]
        loop(planes // chunk, body)

    def remainder(self, first, chunk, face):
        totals, centres = self.total(first, chunk, 8, self.rows, face)
        out = []
        for i in range(chunk):
            d = self.d[self.wall(first + i)]
            r = self.s[first + i + self.sx, pl.ds(self.sy, self.rows), :] - (d * centres[i] - totals[i])
            out.append(r if self.dims[1] == self.rows else jnp.where(d > 0, r, 0.0))
        return out

    def restrict_to(self, target, corner, pairs, face=None):
        rows, z = self.rows, self.dims[2]
        coarse_rows = rows_of(self.dims[1] // 2)
        chunk = widest(self.dims[0], 32 * 8 // rows, 2)
        half = chunk // 2
        source_lane = lax.broadcasted_iota(jnp.int32, (LANES, LANES), 0)
        target_lane = lax.broadcasted_iota(jnp.int32, (LANES, LANES), 1)
        halve = jnp.where((source_lane // 2 == target_lane) & (source_lane < z), 0.5, 0.0).astype(jnp.bfloat16)
        if rows < 16:
            pairs[...] = jnp.zeros_like(pairs)

        def first(step):
            r = self.remainder(step * chunk, chunk, face)
            for i in range(half):
                pairs[step * half + i, pl.ds(0, rows), :] = r[2 * i] + r[2 * i + 1]
        loop(self.dims[0] // chunk, first)

        planes = self.dims[0] // 2
        many = min(planes, max(1, 256 // coarse_rows))

        def second(step):
            at = pl.ds(step * many, many)
            q = pairs[at, pl.ds(0, coarse_rows, stride=2), :] + pairs[at, pl.ds(1, coarse_rows, stride=2), :]
            q = exact_dot(q.reshape(many * coarse_rows, LANES), halve)
            target[pl.ds(step * many + corner[0], many), pl.ds(corner[1], coarse_rows), :] = q.reshape(many, coarse_rows, LANES)
        loop(planes // many, second)

    def reflect(self):
        (x, y, z), v, ox = self.dims, self.v, self.ox
        margin = 3 if self.reach else 0
        for_all = pl.ds(ox - margin, x + 2 * margin)

        def low_x():
            v[ox - 1] = -v[ox]

        def high_x():
            v[ox + x] = -v[ox + x - 1]

        def low_y():
            v[for_all, pl.ds(7, 1), :] = -v[for_all, pl.ds(8, 1), :]

        def high_y():
            v[for_all, pl.ds(8 + y, 1), :] = -v[for_all, pl.ds(7 + y, 1), :]

        for axis, low, high in ((0, low_x, high_x), (1, low_y, high_y)):
            if isinstance(self.counts[axis], int) and isinstance(self.places[axis], int):
                low()
                high()
            else:
                pl.when(self.places[axis] == 0)(low)
                pl.when(self.places[axis] == self.counts[axis] - 1)(high)


def layout(number, dims):
    x, y, z = dims
    if number in REACH:
        reach = REACH[number]
        height = rows_of(y + 2 * reach)
        return EDGE, 8 - reach, height, x + 2 * EDGE, max(40, y + 24)
    if number == SHARED:
        return EDGE, 8, rows_of(y), x + 2 * EDGE, rows_of(y) + 24
    return 1, 8, rows_of(y), x + 2, rows_of(y) + 16


def below_zero(number):
    return -((FINAL[number] + 3) // 2) if number in REACH else 0


def lift_shape(number, coarse):
    low = below_zero(number)
    count = coarse[0] - 2 * low
    height = rows_of(coarse[1] - 2 * low)
    return low, count, height, count + 2, rows_of(8 + low + height + 1)


def lift(v, ox, dims, places, counts, fine, spread, centre):
    x, y, z = dims
    low, count, height, planes, tall = lift_shape(fine.number, dims)
    beyond = EDGE if fine.reach else 0
    k = signed(lax.broadcasted_iota(jnp.int32, (LANES, LANES), 0))
    f = signed(lax.broadcasted_iota(jnp.int32, (LANES, LANES), 1))
    at = places[2] * (2 * z) + f
    inside = (f >= -beyond) & (f < 2 * z + beyond) & (at >= 0) & (at < counts[2] * 2 * z)
    parent = (f + LANES) // 2 - LANES // 2
    near = parent + jnp.where((f + LANES) % 2 == 1, 1, -1)
    outside = (places[2] * z + near < 0) | (places[2] * z + near >= counts[2] * z)
    own = jnp.where((k == parent) & inside, 0.25, 0.0)
    beside = jnp.where((k == near) & inside, 0.25, 0.0)
    both = own + jnp.where(outside, -own, beside)
    matrix = jnp.concatenate([own, both], axis=1).astype(jnp.bfloat16)

    many = widest(planes, max(1, 832 // tall))

    def first(step):
        e = v[pl.ds(step * many + (ox + low - 1), many), pl.ds(0, tall), :]
        product = exact_dot(e.reshape(many * tall, LANES), matrix)
        at = pl.ds(step * many, many)
        spread[at] = product[:, :LANES].reshape(many, tall, LANES)
        centre[at] = product[:, LANES:].reshape(many, tall, LANES)
    loop(planes // many, first)

    group = widest(count, max(1, 256 // height))
    row = places[1] * y + row_iota(height) + low
    valid = (row >= 0) & (row < counts[1] * y) & (row_iota(height) + low < y + beyond)
    masked = beyond > 0 or y < height

    def second(step):
        for i in range(group):
            plane = step * group + i
            middle = centre[plane + 1, pl.ds(8 + low, height), :]
            ys = (spread[plane + 1, pl.ds(7 + low, height), :], spread[plane + 1, pl.ds(9 + low, height), :])
            if beyond:
                at = places[0] * x + plane + low
                here = valid & ((at >= 0) & (at < counts[0] * x))
            else:
                here = valid
            for up_x in range(2):
                xs = middle + spread[plane + 2 * up_x, pl.ds(8 + low, height), :]
                for up_y in range(2):
                    q = xs + ys[up_y]
                    if masked:
                        q = jnp.where(here, q, 0.0)
                    at = (2 * (plane + low) + up_x + fine.ox, pl.ds(8 + 2 * low + up_y, height, stride=2), slice(None))
                    fine.v[at] = fine.v[at] + q
    loop(count // group, second)


class Ring:
    def __init__(self, level, refs, sems):
        self.level, self.sems = level, sems
        self.body, self.parts = refs[0], refs[1:-len(WAYS)]
        self.got = dict(zip(WAYS, refs[-len(WAYS):]))
        self.places, self.counts = level.places, level.counts

    @staticmethod
    def sizes(n):
        each = LANES // n
        cut = n if n <= 16 else 8
        return each, max(1, n // each), cut, LANES // cut, max(1, n * cut // LANES)

    @staticmethod
    def shape(n, way):
        _, groups, _, _, cuts = Ring.sizes(n)
        return (1 if way[0] else cuts if way[2] else groups, 8 if way[1] else n, LANES)

    def exists(self, way, sign):
        found = None
        for axis in range(3):
            if way[axis]:
                other = self.places[axis] + sign * way[axis]
                one = (other >= 0) if sign * way[axis] < 0 else (other < self.counts[axis])
                found = one if found is None else found & one
        return found

    def clear(self):
        for way in WAYS:
            @pl.when(jnp.logical_not(self.exists(way, -1)))
            def _(way=way):
                self.got[way][...] = jnp.zeros_like(self.got[way])

    def copy(self, way):
        n = self.level.dims[0]
        shape = Ring.shape(n, way)
        source = self.body
        if way[2] and self.parts:
            source = self.parts[0] if way[2] < 0 else self.parts[1]
        groups = source.shape[0]
        group = 0 if way[0] <= 0 else groups - 1
        row = 0 if way[1] <= 0 else n - 8
        k = WAYS.index(way)
        return pltpu.make_async_remote_copy(
            src_ref=source.at[pl.ds(group, shape[0]), pl.ds(row, shape[1])], dst_ref=self.got[way],
            send_sem=self.sems[0].at[k], recv_sem=self.sems[1].at[k],
            device_id={name: self.places[axis] + way[axis] for axis, name in enumerate(AXES) if way[axis]}, device_id_type=MESH)

    def post(self):
        n, s = self.level.dims[0], self.level.s
        each, groups, cut, cuts_each, cuts = Ring.sizes(n)
        plane = lambda x: s[EDGE + x, pl.ds(8, n), :]
        for g in range(groups):
            value = plane(g * each)
            for i in range(1, min(each, n)):
                value = value + turn(plane(g * each + i), i * n)
            self.body[g] = value
        if self.parts:
            lane = lane_iota(n)
            for g in range(cuts):
                low = high = jnp.zeros((n, LANES), jnp.float32)
                for i in range(cuts_each):
                    moved = turn(plane(g * cuts_each + i), cut * i)
                    low = jnp.where(lane // cut == i, moved, low)
                    high = jnp.where((lane + (LANES - n + cut)) % LANES // cut == i, moved, high)
                self.parts[0][g] = low
                self.parts[1][g] = high
        for way in WAYS:
            pl.when(self.exists(way, 1))(self.copy(way).start)

    def land(self):
        n, s, reach = self.level.dims[0], self.level.s, self.level.reach
        each, groups, cut, cuts_each, cuts = Ring.sizes(n)
        for way in WAYS:
            pl.when(self.exists(way, -1))(self.copy(way).wait_recv)
        for to_x, to_y in itertools.product((-1, 0, 1), repeat=2):
            height = 8 if to_y else n
            row = {-1: 0, 0: 8, 1: 8 + n}[to_y]
            lane = lane_iota(height)
            body = self.got[(-to_x, -to_y, 0)] if to_x or to_y else None
            high = self.got[(-to_x, -to_y, -1)]
            low = self.got[(-to_x, -to_y, 1)]
            for x in {-1: range(n - reach, n), 0: range(n), 1: range(reach)}[to_x]:
                at = (EDGE + to_x * n + x, pl.ds(row, height), slice(None))
                g, h = x // each, x // cuts_each
                if to_x < 0:
                    g, h = g - (groups - 1), h - (cuts - 1)
                near = turn(body[g], -(x % each) * n) if body is not None else s[at]
                above = turn(high[h], n - cut * (x % cuts_each))
                under = turn(low[h], -n - cut * (x % cuts_each))
                s[at] = jnp.where(lane < n, near, jnp.where(lane < 64, above, under))

    def finish(self):
        for way in WAYS:
            pl.when(self.exists(way, 1))(self.copy(way).wait_send)


def solve_kernel(counts, blocks, coarse, refs):
    right_side, guess, out_v, out_r = refs[:4]
    refs = list(refs[4:])
    take = lambda count=1: [refs.pop(0) for _ in range(count)] if count > 1 else refs.pop(0)
    places = tuple(lax.axis_index(axis) for axis in AXES)
    levels = []
    for number in range(LEVELS):
        if number < SHARED:
            levels.append(Grid(number, blocks[number], places, counts, *take(4)))
        else:
            levels.append(Grid(number, coarse[number - SHARED], (0, 0, 0), (1, 1, 1), *take(4)))
    exchange = take(5)
    rings = {}
    for number in REACH:
        n = blocks[number][0]
        members = take(1 + (2 if Ring.sizes(n)[2] != n else 0) + len(WAYS))
        rings[number] = Ring(levels[number], members, take(2))
    pairs = take(LEVELS - 1)
    spreads = take(LEVELS - 1)
    centres = take(LEVELS - 1)
    block_s, block_v, packet, line, joined, packets, line_send, line_recv, gather_send, gather_recv = refs

    barrier = pltpu.get_barrier_semaphore()
    nx, ny, nz = counts

    def greet(device):
        pl.semaphore_signal(barrier, inc=1, device_id=device, device_id_type=MESH)

    def greet_plane(offset, carry):
        other = lax.rem(places[0] * ny + places[1] + offset, nx * ny)
        greet({AXES[0]: other // ny, AXES[1]: other % ny})
        return carry
    lax.fori_loop(1, nx * ny, greet_plane, 0)
    for offset in range(1, nz):
        greet({AXES[2]: lax.rem(places[2] + offset, nz)})
    skew = [way for way in WAYS if way[2] and (way[0] or way[1])]
    for way in skew:
        @pl.when(rings[1].exists(way, 1))
        def _(way=way):
            greet({name: places[axis] + way[axis] for axis, name in enumerate(AXES) if way[axis]})

    for level in levels:
        level.prepare()
    for ring in rings.values():
        ring.clear()
    block_v[...] = jnp.zeros_like(block_v)
    face = exchange[4]
    face[...] = jnp.zeros_like(face)
    z0 = blocks[0][2]
    top = levels[0]

    def load(x):
        top.v[x + 1, pl.ds(8, top.rows), pl.ds(0, z0)] = guess[x]
        top.s[x] = jnp.concatenate([right_side[x], jnp.zeros((top.rows, LANES - z0), jnp.float32)], axis=1)
    loop(blocks[0][0] // 4, lambda step: [load(4 * step + i) for i in range(4)])

    near = [jnp.where(place > 0, 1, 0) + jnp.where(place < count - 1, 1, 0) for place, count in zip(places, counts)]
    pl.semaphore_wait(barrier, nx * ny + nz - 2 + near[2] * ((near[0] + 1) * (near[1] + 1) - 1))
    turns = [0]
    sent = []

    def swap():
        level = top
        out, into, send, recv, face = exchange
        n, v, (x, y, z) = turns[0], level.v, level.dims
        turns[0] += 1

        def folded(value):
            half = value.shape[0] // 2
            return jnp.where(lane_iota(half) < 64, value[:half], pltpu.roll(value[half:], 64, 1))

        def unfolded(value):
            low = lane_iota(value.shape[0]) < 64
            return jnp.concatenate([jnp.where(low, value, 0.0), jnp.where(low, pltpu.roll(value, 64, 1), 0.0)], axis=0)
        halves = (y // 2, y // 2, x // 2, x // 2, y, y)
        out[n, 0, pl.ds(0, y // 2)] = folded(v[x, pl.ds(8, y), :])
        out[n, 1, pl.ds(0, y // 2)] = folded(v[1, pl.ds(8, y), :])
        out[n, 2, pl.ds(0, x // 2)] = folded(v[pl.ds(1, x), 7 + y, :])
        out[n, 3, pl.ds(0, x // 2)] = folded(v[pl.ds(1, x), 8, :])
        lane = lane_iota(y)
        many = min(x, 16)

        def columns(step, carry):
            last, leading = carry
            for i in range(many):
                plane = step * many + i
                c = v[plane + 1, pl.ds(8, y), :]
                turned = pltpu.roll(c, plane + 64, 1)
                last = jnp.where(lane == (plane + 63 + z) % LANES, turned, last)
                leading = jnp.where(lane == plane + 64, turned, leading)
            return last, leading
        zero = jnp.zeros((y, LANES), jnp.float32)
        last, leading = lax.fori_loop(0, x // many, columns, (zero, zero))
        out[n, 4, pl.ds(0, y)] = last
        out[n, 5, pl.ds(0, y)] = leading

        copies = []
        for axis in range(3):
            for way in range(2):
                side = 2 * axis + way
                other = places[axis] + (1 - 2 * way)
                copy = pltpu.make_async_remote_copy(
                    src_ref=out.at[n, side, pl.ds(0, halves[side])], dst_ref=into.at[n, side, pl.ds(0, halves[side])],
                    send_sem=send.at[n, side], recv_sem=recv.at[n, side],
                    device_id={AXES[axis]: other}, device_id_type=MESH)
                has_target = other < counts[axis] if way == 0 else other >= 0
                has_origin = places[axis] > 0 if way == 0 else places[axis] < counts[axis] - 1
                pl.when(has_target)(copy.start)
                sent.append((has_target, copy))
                copies.append((has_origin, copy))

        def land(side):
            got = into.at[n, side]
            if side == 0:
                v[0, pl.ds(8, y), :] = unfolded(got[pl.ds(0, y // 2)])
            elif side == 1:
                v[x + 1, pl.ds(8, y), :] = unfolded(got[pl.ds(0, y // 2)])
            elif side == 2:
                v[pl.ds(1, x), 7, :] = unfolded(got[pl.ds(0, x // 2)])
            elif side == 3:
                v[pl.ds(1, x), 8 + y, :] = unfolded(got[pl.ds(0, x // 2)])
            elif side == 4:
                face[...] = jnp.where(lane < 64, pltpu.roll(got[pl.ds(0, y)], (65 - z) % LANES, 1), face[...])
            else:
                face[...] = jnp.where(lane >= 64, got[pl.ds(0, y)], face[...])
        for side, (has_origin, copy) in enumerate(copies):
            @pl.when(has_origin)
            def _(side=side, copy=copy):
                copy.wait_recv()
                land(side)
        return face

    top.sweep(0, swap())
    top.sweep(1, swap())
    top.restrict_to(levels[1].s, (EDGE, 8), pairs[0], swap())
    for number in range(1, SHARED):
        level = levels[number]
        rings[number].post()
        rings[number].land()
        level.sweep(0, zero=True, beyond=level.reach)
        level.sweep(1, beyond=level.reach)
        if number + 1 < SHARED:
            level.restrict_to(levels[number + 1].s, (EDGE, 8), pairs[number])
        else:
            level.restrict_to(block_s, (0, 0), pairs[number])

    bx, by, bz = blocks[SHARED]
    wide = LANES // bx
    packed = jnp.zeros((rows_of(by), LANES), jnp.float32)
    for x in range(bx):
        packed = packed + pltpu.roll(block_s[x], x * wide + places[2] * bz, 1)
    packet[...] = packed[:by]

    def line_copy(source, target):
        return pltpu.make_async_remote_copy(
            src_ref=packet, dst_ref=line.at[source], send_sem=line_send.at[target], recv_sem=line_recv.at[source],
            device_id={AXES[2]: target}, device_id_type=MESH)

    for offset in range(1, nz):
        line_copy(places[2], lax.rem(places[2] + offset, nz)).start()
    merged = packed[:by]
    for offset in range(1, nz):
        source = lax.rem(places[2] + nz - offset, nz)
        line_copy(source, lax.rem(places[2] + offset, nz)).wait_recv()
        merged = merged + line[source]
    joined[...] = merged
    total = nx * ny
    me = places[0] * ny + places[1]

    def plane_copy(source, target):
        return pltpu.make_async_remote_copy(
            src_ref=joined, dst_ref=packets.at[source], send_sem=gather_send.at[target], recv_sem=gather_recv.at[source],
            device_id={AXES[0]: target // ny, AXES[1]: target % ny}, device_id_type=MESH)

    def post(offset, carry):
        plane_copy(me, lax.rem(me + offset, total)).start()
        return carry
    lax.fori_loop(1, total, post, 0)
    packets[me] = merged

    def arrive(offset, carry):
        plane_copy(lax.rem(me + total - offset, total), lax.rem(me + offset, total)).wait_recv()
        return carry
    lax.fori_loop(1, total, arrive, 0)
    whole = levels[SHARED]

    def unpack(px):
        for py in range(0, ny, 2):
            pair = jnp.concatenate([packets[px * ny + py], packets[px * ny + py + 1]], axis=0)
            for x in range(bx):
                whole.s[px * bx + x, pl.ds(py * by, 2 * by), :] = turn(pair, -x * wide)
    loop(nx, unpack)

    for number in range(SHARED, LEVELS - 1):
        level = levels[number]
        level.sweep(0, zero=True)
        level.sweep(1)
        level.restrict_to(levels[number + 1].s, (0, 0), pairs[number])
    level = levels[LEVELS - 1]
    level.sweep(0, zero=True)
    level.sweep(1)
    for _ in range(COARSE_SWEEPS - 1):
        level.sweep(0)
        level.sweep(1)
    for number in reversed(range(SHARED, LEVELS - 1)):
        level, below = levels[number], levels[number + 1]
        below.reflect()
        lift(below.v, below.ox, below.dims, (0, 0, 0), (1, 1, 1), level, spreads[number], centres[number])
        level.sweep(0)
        level.sweep(1)

    whole.reflect()
    shift = lax.rem(LANES - places[2] * bz, LANES)
    odd = lax.rem(places[1] + 1, 2) == 1
    for x in range(bx + 8):
        part = whole.v[places[0] * bx + (x - 4 + whole.ox), pl.ds(pl.multiple_of((places[1] + 1) // 2 * 8, 8), 24), :]
        block_v[x, pl.ds(4, 16)] = pltpu.roll(jnp.where(odd, part[4:20], part[:16]), shift, 1)
    lift(block_v, 4, blocks[SHARED], places, counts, levels[SHARED - 1], spreads[SHARED - 1], centres[SHARED - 1])
    for number in reversed(range(1, SHARED)):
        level = levels[number]
        level.sweep(0, beyond=level.reach - 2)
        level.sweep(1, beyond=level.reach - 2)
        level.reflect()
        lift(level.v, level.ox, level.dims, places, counts, levels[number - 1], spreads[number - 1], centres[number - 1])
    top.sweep(0, swap())
    top.sweep(1, swap())
    face = swap()
    chunk = widest(blocks[0][0], 32 * 8 // top.rows, 2)

    def finish(step):
        r = top.remainder(step * chunk, chunk, face)
        for i in range(chunk):
            at = step * chunk + i
            out_r[at] = r[i][:, :z0]
            out_v[at] = top.v[at + 1, pl.ds(8, top.rows), pl.ds(0, z0)]
    loop(blocks[0][0] // chunk, finish)

    for has_target, copy in sent:
        pl.when(has_target)(copy.wait_send)
    for ring in rings.values():
        ring.finish()
    for offset in range(1, nz):
        line_copy(places[2], lax.rem(places[2] + offset, nz)).wait_send()

    def leave(offset, carry):
        plane_copy(me, lax.rem(me + offset, total)).wait_send()
        return carry
    lax.fori_loop(1, total, leave, 0)


def solution(mesh):
    counts = tuple(mesh.shape[axis] for axis in AXES)

    def per_device(right_side, guess):
        shape = right_side.shape
        blocks = [tuple(side >> level for side in shape) for level in range(SHARED + 1)]
        whole = tuple(side * count for side, count in zip(blocks[SHARED], counts))
        coarse = [tuple(side >> level for side in whole) for level in range(LEVELS - SHARED)]
        grids = blocks[:SHARED] + coarse
        scratch = []
        vmem = lambda *dims: scratch.append(pltpu.VMEM(dims, jnp.float32))
        sems = lambda *dims: scratch.append(pltpu.SemaphoreType.DMA(dims))
        for number, (x, y, z) in enumerate(grids):
            _, _, height, planes, tall = layout(number, (x, y, z))
            vmem(planes, tall, LANES)
            if number in REACH:
                vmem(planes, tall, LANES)
            else:
                vmem(x, rows_of(y), LANES)
            vmem(3, height, LANES)
            vmem(2, rows_of(y), LANES)
        x, y, z = blocks[0]
        side = max(x, y)
        vmem(6, 6, side, LANES)
        vmem(6, 6, side, LANES)
        sems(6, 6)
        sems(6, 6)
        vmem(y, LANES)
        for number in REACH:
            n = blocks[number][0]
            _, groups, cut, _, cuts = Ring.sizes(n)
            vmem(groups, n, LANES)
            if cut != n:
                vmem(cuts, n, LANES)
                vmem(cuts, n, LANES)
            for way in WAYS:
                vmem(*Ring.shape(n, way))
            sems(len(WAYS))
            sems(len(WAYS))
        for x, y, z in grids[:-1]:
            vmem(x // 2, max(16, y), LANES)
        for _ in range(2):
            for number in range(LEVELS - 1):
                _, _, _, planes, tall = lift_shape(number, blocks[number + 1] if number < SHARED else grids[number + 1])
                vmem(planes, tall, LANES)
        bx, by, bz = blocks[SHARED]
        vmem(bx, rows_of(by), LANES)
        vmem(bx + 8, 24, LANES)
        vmem(by, LANES)
        vmem(counts[2], by, LANES)
        vmem(by, LANES)
        total = counts[0] * counts[1]
        vmem(total, by, LANES)
        for many in (counts[2], counts[2], total, total):
            sems(many)

        def kernel(*refs):
            solve_kernel(counts, blocks, coarse, refs)

        whole_block = pl.BlockSpec(memory_space=pltpu.VMEM)
        return pl.pallas_call(
            kernel,
            out_shape=(jax.ShapeDtypeStruct(shape, jnp.float32),) * 2,
            in_specs=[whole_block] * 2,
            out_specs=(whole_block,) * 2,
            scratch_shapes=scratch,
            compiler_params=pltpu.CompilerParams(collective_id=0, has_side_effects=True, vmem_limit_bytes=60 * 2**20),
            name="vcycle",
        )(right_side, guess)

    spec = P(*AXES)
    return jax.shard_map(per_device, mesh=mesh, in_specs=(spec, spec), out_specs=(spec, spec), check_vma=False)
```

time: 156 us -> 116 us (0.74)
  Pallas kernels: 150 us -> 111 us
    pallas_call x1, Pallas kernels: 150 us -> 111 us  [per_device(): pl.pallas_call(kernel, out_shape=(jax.ShapeDtypeStruct(shape, jnp.float32...]
where the time goes in v2:
time: 116 us
  Pallas kernels  111 us (96%)
  local copies, waits for them, and re-layouts  4.63 us (4%)
    pallas_call x1, Pallas kernels, per_device(): pl.pallas_call(kernel, out_shape=(jax.ShapeDtypeStruct(shape, jnp.float32...  111 us
    unnamed x4, local copies, waits for them, and re-layouts  4.63 us

profile of v2, /device:TPU:1, one launch (start us, length us, event | category | flops | bytes accessed | tf_op | source)
XLA Modules:
  0.0 116.3 jit_solution(2953990349555854207)
XLA Ops:
  0.6 111.0 %vcycle.1 = (f32[64,64,64]{2,1,0:T(8,128)}, f32[64,64,64]{2,1,0:T(8,128)}) custom-call(f32[64,64,64]{2,1,0:T(8,128)} %refs_0_.1, f32[64,64,64]{2,1,0:T(8,128)} %refs_1_.1), custom_call_target="tpu_custom_call" | custom-call | tf_op jit(solution)/shard_map/vcycle/pallas_call | solution.py:692
  111.7 0.0 copy-start
  111.7 3.3 %copy.6 = f32[64,64,64]{2,1,0:T(8,128)} copy(f32[64,64,64]{2,1,0:T(8,128)} %get-tuple-element.4) | data formatting | bytes 2097152
  115.0 0.0 copy-done
  115.0 1.3 %copy.7 = f32[64,64,64]{2,1,0:T(8,128)} copy(f32[64,64,64]{2,1,0:T(8,128)S(1)} %copy-done) | data formatting | bytes 2097152
Async XLA Ops:
  111.7 3.3 %copy-start = (f32[64,64,64]{2,1,0:T(8,128)S(1)}, f32[64,64,64]{2,1,0:T(8,128)}, u32[]{:S(2)}) copy-start(f32[64,64,64]{2,1,0:T(8,128)} %get-tuple-element.5) | copy-start | bytes 3145732

commit v3 on v2

v3 whole, which is shorter than its diff:
```python
import itertools

import jax
import jax.numpy as jnp
from jax import lax
from jax.experimental import pallas as pl
from jax.experimental.pallas import tpu as pltpu
from jax.sharding import PartitionSpec as P

LEVELS = 7
COARSE_SWEEPS = 4
SHARED = 4
VMEM_LIMIT = 32
LANES = 128
EDGE = 8
AXES = ("gx", "gy", "gz")
MESH = pl.DeviceIdType.MESH
WAYS = [way for way in itertools.product((-1, 0, 1), repeat=3) if any(way)]
FINAL = {0: 1, 1: 2, 2: 3, 3: 3}
REACH = {level: FINAL[level] + 3 for level in range(1, SHARED)}


def rows_of(count):
    return max(8, -(-count // 8) * 8)


def lane_iota(rows):
    return lax.broadcasted_iota(jnp.int32, (rows, LANES), 1)


def row_iota(rows):
    return lax.broadcasted_iota(jnp.int32, (rows, LANES), 0)


def loop(count, body):
    if count == 1:
        body(0)
    else:
        def step(i, carry):
            body(i)
            return carry
        lax.fori_loop(0, count, step, 0)


def turn(value, amount):
    amount = amount % LANES
    return pltpu.roll(value, amount, 1) if amount else value


def exact_dot(value, matrix):
    first = value.astype(jnp.bfloat16)
    rest = value - first.astype(jnp.float32)
    second = rest.astype(jnp.bfloat16)
    third = (rest - second.astype(jnp.float32)).astype(jnp.bfloat16)
    dot = lambda part: jnp.dot(part, matrix, preferred_element_type=jnp.float32)
    return (dot(third) + dot(second)) + dot(first)


def widest(count, most, step=1):
    return max(size for size in range(step, count + 1, step) if count % size == 0 and (size <= most or size == step))


def signed(lane):
    return jnp.where(lane < 96, lane, lane - LANES)


class Grid:
    def __init__(self, number, dims, places, counts, v, s, w, d):
        self.number, self.dims, self.places, self.counts = number, dims, places, counts
        self.v, self.s, self.w, self.d = v, s, w, d
        self.reach = REACH.get(number, 0)
        self.ox, self.start, self.height, _, _ = layout(number, dims)
        self.sx, self.sy = (EDGE, 8) if self.reach else (0, 0)
        self.rows = rows_of(dims[1])

    def prepare(self):
        x, y, z = self.dims
        beyond = EDGE if self.reach else 0

        def base(height, start):
            row, lane = row_iota(height) + (start - 8), signed(lane_iota(height))
            at_y, at_z = self.places[1] * y + row, self.places[2] * z + lane
            last_y, last_z = self.counts[1] * y - 1, self.counts[2] * z - 1
            valid = (lane >= -beyond) & (lane < z + beyond) & (row >= -beyond) & (row < y + beyond)
            valid = valid & (at_y >= 0) & (at_y <= last_y) & (at_z >= 0) & (at_z <= last_z)
            one = lambda at, last: (at == 0).astype(jnp.float32) + (at == last).astype(jnp.float32)
            return valid, 6.0 + one(at_y, last_y) + one(at_z, last_z)
        valid, diagonal = base(self.w.shape[1], self.start)
        for wall in range(2):
            self.w[wall] = jnp.where(valid, 1.0 / (diagonal + wall), 0.0)
        self.w[2] = jnp.zeros_like(diagonal)
        valid, diagonal = base(self.rows, 8)
        for wall in range(2):
            self.d[wall] = jnp.where(valid, diagonal + wall, 0.0)
        self.v[...] = jnp.zeros_like(self.v)
        if self.reach:
            self.s[...] = jnp.zeros_like(self.s)

    def wall(self, plane, beyond=False):
        at = self.places[0] * self.dims[0] + plane
        last = self.counts[0] * self.dims[0] - 1
        if isinstance(at, int):
            return int(at in (0, last))
        kind = jnp.where((at == 0) | (at == last), 1, 0)
        return jnp.where((at < 0) | (at > last), 2, kind) if beyond else kind

    def total(self, plane, count, start, height):
        at = plane + self.ox
        slab = self.v[pl.ds(at - 1, count + 2), pl.ds(start, height), :]
        centre = slab[1:-1]
        total = slab[2:] + slab[:-2]
        total = total + self.v[pl.ds(at, count), pl.ds(start + 1, height), :] + self.v[pl.ds(at, count), pl.ds(start - 1, height), :]
        out = []
        for i in range(count):
            c = centre[i]
            out.append(total[i] + (pltpu.roll(c, 1, 1) + pltpu.roll(c, LANES - 1, 1)))
        return out, [centre[i] for i in range(count)]

    def sweep(self, colour, zero=False, beyond=0):
        start, height = self.start, self.height
        if self.reach and not zero:
            start, height = start + 1, inner_height(self.number, self.dims)
        planes = self.dims[0] + 2 * beyond
        chunk = widest(planes, 112 * 8 // height, 2)
        parity = (row_iota(height) + lane_iota(height) + start) % 2

        def body(step):
            first = step * chunk - beyond
            if not zero:
                totals, centres = self.total(first, chunk, start, height)
            results = []
            for i in range(chunk):
                weight = self.w[self.wall(first + i, beyond > 0), pl.ds(start - self.start, height), :]
                given = self.s[first + i + self.sx, pl.ds(start - 8 + self.sy, height), :]
                mine = parity == (i + colour + beyond) % 2
                if zero:
                    results.append(jnp.where(mine, given * weight, 0.0))
                else:
                    results.append(jnp.where(mine, (given + totals[i]) * weight, centres[i]))
            for i in range(chunk):
                self.v[first + i + self.ox, pl.ds(start, height), :] = results[i]
        loop(planes // chunk, body)

    def remainder(self, first, chunk):
        totals, centres = self.total(first, chunk, 8, self.rows)
        out = []
        for i in range(chunk):
            d = self.d[self.wall(first + i)]
            r = self.s[first + i + self.sx, pl.ds(self.sy, self.rows), :] - (d * centres[i] - totals[i])
            out.append(r if self.dims[1] == self.rows else jnp.where(d > 0, r, 0.0))
        return out

    def restrict_to(self, target, corner, pairs):
        rows = self.rows
        chunk = widest(self.dims[0], 32 * 8 // rows, 2)
        half = chunk // 2
        if rows < 16:
            pairs[...] = jnp.zeros_like(pairs)

        def first(step):
            r = self.remainder(step * chunk, chunk)
            for i in range(half):
                pairs[step * half + i, pl.ds(0, rows), :] = r[2 * i] + r[2 * i + 1]
        loop(self.dims[0] // chunk, first)
        narrow(self.dims, target, corner, pairs)

    def reflect(self):
        (x, y, z), v, ox = self.dims, self.v, self.ox
        margin = 3 if self.reach else 0
        for_all = pl.ds(ox - margin, x + 2 * margin)

        def low_x():
            v[ox - 1] = -v[ox]

        def high_x():
            v[ox + x] = -v[ox + x - 1]

        def low_y():
            v[for_all, pl.ds(7, 1), :] = -v[for_all, pl.ds(8, 1), :]

        def high_y():
            v[for_all, pl.ds(8 + y, 1), :] = -v[for_all, pl.ds(7 + y, 1), :]

        for axis, low, high in ((0, low_x, high_x), (1, low_y, high_y)):
            if isinstance(self.counts[axis], int) and isinstance(self.places[axis], int):
                low()
                high()
            else:
                pl.when(self.places[axis] == 0)(low)
                pl.when(self.places[axis] == self.counts[axis] - 1)(high)


def narrow(dims, target, corner, pairs):
    x, y, z = dims
    coarse_rows = rows_of(y // 2)
    source_lane = lax.broadcasted_iota(jnp.int32, (LANES, LANES), 0)
    target_lane = lax.broadcasted_iota(jnp.int32, (LANES, LANES), 1)
    halve = jnp.where((source_lane // 2 == target_lane) & (source_lane < z), 0.5, 0.0).astype(jnp.bfloat16)
    planes = x // 2
    many = min(planes, max(1, 256 // coarse_rows))

    def second(step):
        at = pl.ds(step * many, many)
        q = pairs[at, pl.ds(0, coarse_rows, stride=2), :] + pairs[at, pl.ds(1, coarse_rows, stride=2), :]
        q = exact_dot(q.reshape(many * coarse_rows, LANES), halve)
        target[pl.ds(step * many + corner[0], many), pl.ds(corner[1], coarse_rows), :] = q.reshape(many, coarse_rows, LANES)
    loop(planes // many, second)


def layout(number, dims):
    x, y, z = dims
    if number in REACH:
        reach = REACH[number]
        height = rows_of(y + 2 * reach)
        return EDGE, 8 - reach, height, x + 2 * EDGE, max(40, y + 24)
    if number == SHARED:
        return EDGE, 8, rows_of(y), x + 2 * EDGE, rows_of(y) + 24
    return 1, 8, rows_of(y), x + 2, rows_of(y) + 16


def inner_height(number, dims):
    return rows_of(dims[1] + 2 * REACH[number] - 2)


def below_zero(number):
    return -((FINAL[number] + 3) // 2) if number in FINAL else 0


def lift_shape(number, coarse):
    low = below_zero(number)
    count = coarse[0] - 2 * low
    height = rows_of(coarse[1] - 2 * low)
    return low, count, height, count + 2, rows_of(8 + low + height + 1)


def widen(v, ox, dims, places, counts, number, spread, centre):
    z = dims[2]
    low, count, height, planes, tall = lift_shape(number, dims)
    beyond = EDGE if number in FINAL else 0
    k = signed(lax.broadcasted_iota(jnp.int32, (LANES, LANES), 0))
    f = signed(lax.broadcasted_iota(jnp.int32, (LANES, LANES), 1))
    at = places[2] * (2 * z) + f
    inside = (f >= -beyond) & (f < 2 * z + beyond) & (at >= 0) & (at < counts[2] * 2 * z)
    parent = (f + LANES) // 2 - LANES // 2
    near = parent + jnp.where((f + LANES) % 2 == 1, 1, -1)
    outside = (places[2] * z + near < 0) | (places[2] * z + near >= counts[2] * z)
    own = jnp.where((k == parent) & inside, 0.25, 0.0)
    beside = jnp.where((k == near) & inside, 0.25, 0.0)
    both = own + jnp.where(outside, -own, beside)
    matrix = jnp.concatenate([own, both], axis=1).astype(jnp.bfloat16)
    many = widest(planes, max(1, 1024 // tall))

    def first(step):
        e = v[pl.ds(step * many + (ox + low - 1), many), pl.ds(0, tall), :]
        product = exact_dot(e.reshape(many * tall, LANES), matrix)
        at = pl.ds(step * many, many)
        spread[at] = product[:, :LANES].reshape(many, tall, LANES)
        centre[at] = product[:, LANES:].reshape(many, tall, LANES)
    loop(planes // many, first)


def lift(v, ox, dims, places, counts, fine, spread, centre):
    x, y, z = dims
    number = fine.number
    low, count, height, planes, tall = lift_shape(number, dims)
    beyond = EDGE if number in FINAL else 0
    widen(v, ox, dims, places, counts, number, spread, centre)
    group = widest(count, max(1, 256 // height))
    row = places[1] * y + row_iota(height) + low
    valid = (row >= 0) & (row < counts[1] * y)
    if not beyond:
        valid = row_iota(height) < y
    masked = beyond > 0 or y < height
    even = lane_iota(height) % 2 == 0

    def second(step):
        for i in range(group):
            plane = step * group + i
            middle = centre[plane + 1, pl.ds(8 + low, height), :]
            ys = (spread[plane + 1, pl.ds(7 + low, height), :], spread[plane + 1, pl.ds(9 + low, height), :])
            xs = [spread[plane + 2 * up_x, pl.ds(8 + low, height), :] for up_x in range(2)]
            here = valid
            if beyond:
                at = places[0] * x + plane + low
                here = valid & ((at >= 0) & (at < counts[0] * x))
            for up_y in range(2):
                rows = pl.ds(8 + 2 * low + up_y, height, stride=2)
                middle_y = middle + ys[up_y]
                if number == 0:
                    q = middle_y + jnp.where(even, xs[1 - up_y], xs[up_y])
                    q = jnp.where(here, q, 0.0)
                    at = (plane + low + fine.ox, rows, slice(None))
                    fine.b[at] = fine.b[at] + q
                    continue
                for up_x in range(2):
                    q = middle_y + xs[up_x]
                    if masked:
                        q = jnp.where(here, q, 0.0)
                    at = (2 * (plane + low) + up_x + fine.ox, rows, slice(None))
                    fine.v[at] = fine.v[at] + q
    loop(count // group, second)


def exists(places, counts, way, sign):
    found = None
    for axis in range(3):
        if way[axis]:
            other = places[axis] + sign * way[axis]
            one = (other >= 0) if sign * way[axis] < 0 else (other < counts[axis])
            found = one if found is None else found & one
    return found


def along(places, way):
    return {name: places[axis] + way[axis] for axis, name in enumerate(AXES) if way[axis]}


class Top:
    number, ox, sets = 0, 2, 4

    def __init__(self, dims, places, counts, r, b, gr, gb, w, d, out, got, sems):
        self.dims, self.places, self.counts = dims, places, counts
        self.r, self.b, self.gr, self.gb, self.w, self.d = r, b, gr, gb, w, d
        self.out, self.got, self.sems = out, got, sems
        self.pairs, self.n = dims[0] // 2, dims[1]

    @staticmethod
    def weights(dims, places, counts, height, start, beyond):
        x, y, z = dims
        row, lane = row_iota(height) + (start - 8), signed(lane_iota(height))
        at_y, at_z = places[1] * y + row, places[2] * z + lane
        last_y, last_z = counts[1] * y - 1, counts[2] * z - 1
        valid = (lane >= -beyond) & (lane < z + beyond) & (at_y >= 0) & (at_y <= last_y) & (at_z >= 0) & (at_z <= last_z)
        one = lambda at, last: (at == 0).astype(jnp.float32) + (at == last).astype(jnp.float32)
        return valid, 6.0 + one(at_y, last_y) + one(at_z, last_z), (row + lane + LANES) % 2 == 0

    def clear(self):
        for ref in (self.r, self.b, self.gr, self.gb):
            ref[...] = jnp.zeros_like(ref)

    def prepare(self):
        valid, diagonal, even = self.weights(self.dims, self.places, self.counts, self.n + 8, 6, 4)
        plain, more = (jnp.where(valid, 1.0 / (diagonal + wall), 0.0) for wall in range(2))
        self.w[0] = plain
        self.w[1] = jnp.where(even, more, plain)
        self.w[2] = jnp.where(even, plain, more)
        self.w[3] = jnp.zeros_like(plain)
        write_diagonals(self.d, self.dims, self.places, self.counts)

    def missing(self):
        for way in WAYS:
            @pl.when(jnp.logical_not(exists(self.places, self.counts, way, -1)))
            def _(way=way):
                self.got[way][...] = jnp.zeros_like(self.got[way])

    def kind(self, pair):
        at = self.places[0] * self.pairs + pair
        last = self.counts[0] * self.pairs - 1
        return jnp.where((at < 0) | (at > last), 3, jnp.where(at == 0, 1, jnp.where(at == last, 2, 0)))

    def sweep(self, colour):
        start, height = 6, self.n + 8
        source, target, given = (self.r, self.b, self.gb) if colour else (self.b, self.r, self.gr)
        count = self.pairs + 2
        chunk = widest(count, 17)
        even = (row_iota(height) + lane_iota(height)) % 2 == 0

        def body(step):
            for i in range(chunk):
                k = step * chunk + i - 1
                at = k + 2
                total = around(source, at, start, height, even, colour)
                kind = self.kind(k)
                if colour:
                    kind = jnp.where(kind == 1, 2, jnp.where(kind == 2, 1, kind))
                target[at, pl.ds(start, height), :] = (given[at, pl.ds(start, height), :] + total) * self.w[kind]
        loop(count // chunk, body)

    def restrict_to(self, target, corner, pairs):
        n = self.n
        even = (row_iota(n) + lane_iota(n)) % 2 == 0
        chunk = 4

        def body(step):
            for i in range(chunk):
                k = step * chunk + i
                red, black = remainders(self.r, self.b, self.gr, self.gb, self.d, k + 2, self.kind(k), even, n)
                pairs[k] = red + black
        loop(self.pairs // chunk, body)
        narrow(self.dims, target, corner, pairs)

    @staticmethod
    def shapes(n):
        face = {0: (2, n, LANES), 1: (n // 4, 8, LANES), 2: (3, n, LANES)}
        sent = [face[0], face[0], face[1], face[1], face[2], face[2], (4, 8, LANES)]
        got = {}
        for way in WAYS:
            if sum(map(abs, way)) == 1:
                got[way] = face[[abs(part) for part in way].index(1)]
            elif not way[2]:
                got[way] = (2, 8, LANES)
            elif not way[0]:
                got[way] = (2, 8, LANES)
            else:
                got[way] = (8, LANES)
        return sent, got

    def copies(self, way, again):
        n, out, got = self.n, self.out, self.got[way]
        high = [part > 0 for part in way]
        if sum(map(abs, way)) == 1:
            axis = [abs(part) for part in way].index(1)
            source = out[2 * axis + high[axis]]
            if again and axis != 1:
                source, got = source.at[pl.ds(0, 1)], got.at[pl.ds(0, 1)]
        elif not way[2]:
            source = out[2 + high[1]].at[pl.ds(n // 4 - 2 if high[0] else 0, 2)]
        elif not way[0]:
            row = pl.ds(n - 8 if high[1] else 0, 8)
            source = out[4 + high[2]].at[pl.ds(0, 2), row]
        else:
            source = out[6].at[2 * high[0] + high[2]]
        k = WAYS.index(way)
        return pltpu.make_async_remote_copy(
            src_ref=source, dst_ref=got, send_sem=self.sems[0].at[k], recv_sem=self.sems[1].at[k],
            device_id=along(self.places, way), device_id_type=MESH)

    def pack(self, again):
        n, pairs = self.n, self.pairs
        arrays = [self.b] if again else [self.b, self.gr, self.gb]
        low, tile = lane_iota(n) < 64, lane_iota(8)
        row = row_iota(8)
        half = pairs // 2
        own = lambda ref, k: ref[k + 2, pl.ds(8, n), :]
        for high in range(2):
            near, far = (pairs - 1, pairs - 2) if high else (0, 1)
            self.out[high][0] = jnp.where(low, own(self.b, near), pltpu.roll(own(self.b, far), 64, 1))
            if not again:
                self.out[high][1] = jnp.where(low, own(self.gr, near), pltpu.roll(own(self.gb, near), 64, 1))

            def edge(k, high=high):
                first = 8 + n - 8 if high else 8
                b = self.b[k + 2, pl.ds(first, 8), :]
                if again:
                    return b
                red, black = (pltpu.roll(ref[k + 2, pl.ds(first, 8), :], by, 0) for ref, by in ((self.gr, 4), (self.gb, 2 if high else 6)))
                if high:
                    return jnp.where(row >= 4, b, jnp.where(row >= 2, red, black))
                return jnp.where(row < 4, b, jnp.where(row < 6, red, black))
            for k in range(half):
                self.out[2 + high][k] = jnp.where(tile < 64, edge(k), pltpu.roll(edge(k + half), 64, 1))
        for index, ref in enumerate(arrays):
            def body(t, ref=ref, index=index):
                at = pl.ds(pl.multiple_of(t * 16, 16), 16)
                lane = lane_iota(16)
                ahead = (lane + (LANES - 60)) % LANES
                first = last = jnp.zeros((16, LANES), jnp.float32)
                for k in range(pairs):
                    moved = turn(ref[k + 2, pl.ds(pl.multiple_of(t * 16 + 8, 8), 16), :], 4 * k)
                    first = jnp.where(lane // 4 == k, moved, first)
                    last = jnp.where(ahead // 4 == k, moved, last)
                self.out[4][index, at] = first
                self.out[5][index, at] = last
            loop(n // 16, body)
        for high_x in range(2):
            for high_z in range(2):
                offset = 60 if high_z else 0
                pair, near = (pairs - 2, pairs - 1) if high_x else (0, 0)
                value = jnp.zeros((8, LANES), jnp.float32)
                for t in range(n // 8):
                    rows = pl.ds(8 * t, 8)
                    moved = turn(self.out[4 + high_z][0, rows], 16 * t - 4 * pair - offset)
                    value = jnp.where((tile >= 16 * t) & (tile < 16 * t + 8), moved, value)
                    if not again:
                        moved = turn(self.out[4 + high_z][1, rows], 16 * t + 8 - 4 * near - offset)
                        value = jnp.where((tile >= 16 * t + 8) & (tile < 16 * t + 16), moved, value)
                self.out[6][2 * high_x + high_z] = value

    def post(self, again=False):
        self.pack(again)
        self.send(again)

    def send(self, again=False):
        for way in WAYS:
            pl.when(exists(self.places, self.counts, way, 1))(self.copies(way, again).start)

    def sent(self, again=False):
        for way in WAYS:
            pl.when(exists(self.places, self.counts, way, 1))(self.copies(way, again).wait_send)

    def land(self, again=False):
        n, pairs, got = self.n, self.pairs, self.got
        half = pairs // 2
        for way in WAYS:
            pl.when(exists(self.places, self.counts, way, -1))(self.copies(way, again).wait_recv)
        arrays = [self.b] if again else [self.b, self.gr, self.gb]
        lane, tile = lane_iota(n), lane_iota(8)

        def ends(high, low, to, k):
            pick = to % 8 < 4
            return turn(jnp.where(pick, high, low) if k % 2 == 0 else jnp.where(pick, low, high), 64 - 4 * k)
        for index, ref in enumerate(arrays):
            high, low = got[(0, 0, -1)], got[(0, 0, 1)]

            def body(t, ref=ref, index=index, high=high, low=low):
                at = pl.ds(pl.multiple_of(t * 16, 16), 16)
                to = lane_iota(16)
                h, l = high[index, at], low[index, at]
                for k in range(pairs):
                    own = (k + 2, pl.ds(pl.multiple_of(t * 16 + 8, 8), 16), slice(None))
                    ref[own] = jnp.where(to < 64, ref[own], ends(h, l, to, k))
            loop(n // 16, body)
        for side in (-1, 1):
            face = got[(0, -side, 0)]
            base = 8 + n if side > 0 else 0
            shifts = (0, 4, 2 if side > 0 else 6)
            for index, ref in enumerate(arrays):
                if index < 2:
                    h, l = got[(0, -side, -1)][index], got[(0, -side, 1)][index]
                for k in range(pairs):
                    value = face[k % half]
                    if k >= half:
                        value = pltpu.roll(value, 64, 1)
                    if shifts[index]:
                        value = pltpu.roll(value, shifts[index], 0)
                    if index < 2:
                        value = jnp.where(tile < 64, value, ends(h, l, tile, k))
                    ref[k + 2, pl.ds(base, 8), :] = value
        for side in (-1, 1):
            face = got[(-side, 0, 0)]
            near, far = (pairs + 2, pairs + 3) if side > 0 else (1, 0)
            high, low = got[(-side, 0, -1)], got[(-side, 0, 1)]
            near_lane, far_lane = (0, 4) if side > 0 else (4, 0)

            def beside(first, at, high=high, low=low):
                out = []
                for t in at:
                    up = turn(high[...], 64 - 16 * t - first)
                    out.append(jnp.where(tile < 96, up, turn(low[...], 124 - 16 * t - first)))
                return jnp.concatenate(out, axis=0) if len(out) > 1 else out[0]
            every = range(n // 8)
            both = face[0]
            self.b[near, pl.ds(8, n), :] = jnp.where(lane < 64, both, beside(near_lane, every))
            self.b[far, pl.ds(8, n), :] = jnp.where(lane < 64, pltpu.roll(both, 64, 1), beside(far_lane, every))
            if not again:
                both = face[1]
                self.gr[near, pl.ds(8, n), :] = jnp.where(lane < 64, both, beside(8, every))
                self.gb[near, pl.ds(8, n), :] = pltpu.roll(both, 64, 1)
            for up in (-1, 1):
                edge = got[(-side, -up, 0)]
                base = 8 + n if up > 0 else 0
                corner = (got[(-side, -up, -1)], got[(-side, -up, 1)])
                t = [0 if up > 0 else n // 8 - 1]
                if side > 0:
                    pieces = {near: (0, False), far: (1, False)}
                else:
                    pieces = {near: (1, True), far: (0, True)}
                for place, (group, upper) in pieces.items():
                    value = edge[group]
                    if upper:
                        value = pltpu.roll(value, 64, 1)
                    first = near_lane if place == near else far_lane
                    self.b[place, pl.ds(base, 8), :] = jnp.where(tile < 64, value, beside(first, t, *corner))
                    if place == near and not again:
                        self.gr[place, pl.ds(base, 8), :] = pltpu.roll(value, 4, 0)


def around(source, at, start, height, even, colour):
    s = source[at, pl.ds(start, height), :]
    left, right = source[at - 1, pl.ds(start, height), :], source[at + 1, pl.ds(start, height), :]
    across = jnp.where(even, right, left) if colour else jnp.where(even, left, right)
    total = (s + across) + (source[at, pl.ds(start + 1, height), :] + source[at, pl.ds(start - 1, height), :])
    return total + (pltpu.roll(s, 1, 1) + pltpu.roll(s, LANES - 1, 1))


def remainders(r, b, gr, gb, d, at, kind, even, n):
    rows = pl.ds(8, n)
    other = jnp.where(kind == 1, 2, jnp.where(kind == 2, 1, kind))
    red = gr[at, rows, :] - (d[kind] * r[at, rows, :] - around(b, at, 8, n, even, 0))
    black = gb[at, rows, :] - (d[other] * b[at, rows, :] - around(r, at, 8, n, even, 1))
    return red, black


def write_diagonals(d, dims, places, counts):
    _, diagonal, even = Top.weights(dims, places, counts, dims[1], 8, 0)
    d[0] = diagonal
    d[1] = jnp.where(even, diagonal + 1.0, diagonal)
    d[2] = jnp.where(even, diagonal, diagonal + 1.0)


class Ring:
    def __init__(self, level, refs, sems):
        self.level, self.sems = level, sems
        self.body, self.parts = refs[0], refs[1:-len(WAYS)]
        self.got = dict(zip(WAYS, refs[-len(WAYS):]))
        self.places, self.counts = level.places, level.counts

    @staticmethod
    def sizes(n):
        each = LANES // n
        cut = n if n <= 16 else 8
        return each, max(1, n // each), cut, LANES // cut, max(1, n * cut // LANES)

    @staticmethod
    def thick(n, reach, way):
        each, groups, _, _, cuts = Ring.sizes(n)
        if not way[0]:
            return cuts if way[2] else groups
        return 1 if way[2] else -(-reach // each)

    @staticmethod
    def shape(n, reach, way):
        return (Ring.thick(n, reach, way), 8 if way[1] else n, LANES)

    def clear(self):
        for way in WAYS:
            @pl.when(jnp.logical_not(exists(self.places, self.counts, way, -1)))
            def _(way=way):
                self.got[way][...] = jnp.zeros_like(self.got[way])

    def copy(self, way):
        n = self.level.dims[0]
        shape = Ring.shape(n, self.level.reach, way)
        source = self.body
        if way[2] and self.parts:
            source = self.parts[0] if way[2] < 0 else self.parts[1]
        groups = source.shape[0]
        group = 0 if way[0] <= 0 else groups - shape[0]
        row = 0 if way[1] <= 0 else n - 8
        k = WAYS.index(way)
        return pltpu.make_async_remote_copy(
            src_ref=source.at[pl.ds(group, shape[0]), pl.ds(row, shape[1])], dst_ref=self.got[way],
            send_sem=self.sems[0].at[k], recv_sem=self.sems[1].at[k],
            device_id={name: self.places[axis] + way[axis] for axis, name in enumerate(AXES) if way[axis]}, device_id_type=MESH)

    def post(self):
        n, s = self.level.dims[0], self.level.s
        each, groups, cut, cuts_each, cuts = Ring.sizes(n)
        plane = lambda x: s[EDGE + x, pl.ds(8, n), :]
        for g in range(groups):
            value = plane(g * each)
            for i in range(1, min(each, n)):
                value = value + turn(plane(g * each + i), i * n)
            self.body[g] = value
        if self.parts:
            lane = lane_iota(n)
            for g in range(cuts):
                low = high = jnp.zeros((n, LANES), jnp.float32)
                for i in range(cuts_each):
                    moved = turn(plane(g * cuts_each + i), cut * i)
                    low = jnp.where(lane // cut == i, moved, low)
                    high = jnp.where((lane + (LANES - n + cut)) % LANES // cut == i, moved, high)
                self.parts[0][g] = low
                self.parts[1][g] = high
        for way in WAYS:
            pl.when(exists(self.places, self.counts, way, 1))(self.copy(way).start)

    def land(self):
        n, s, reach = self.level.dims[0], self.level.s, self.level.reach
        each, groups, cut, cuts_each, cuts = Ring.sizes(n)
        for way in WAYS:
            pl.when(exists(self.places, self.counts, way, -1))(self.copy(way).wait_recv)
        for to_x, to_y in itertools.product((-1, 0, 1), repeat=2):
            height = 8 if to_y else n
            row = {-1: 0, 0: 8, 1: 8 + n}[to_y]
            lane = lane_iota(height)
            body = self.got[(-to_x, -to_y, 0)] if to_x or to_y else None
            high = self.got[(-to_x, -to_y, -1)]
            low = self.got[(-to_x, -to_y, 1)]
            for x in {-1: range(n - reach, n), 0: range(n), 1: range(reach)}[to_x]:
                at = (EDGE + to_x * n + x, pl.ds(row, height), slice(None))
                g, h = x // each, x // cuts_each
                if to_x < 0:
                    g, h = g - (groups - body.shape[0]), h - (cuts - high.shape[0])
                near = turn(body[g], -(x % each) * n) if body is not None else s[at]
                above = turn(high[h], n - cut * (x % cuts_each))
                under = turn(low[h], -n - cut * (x % cuts_each))
                s[at] = jnp.where(lane < n, near, jnp.where(lane < 64, above, under))

    def finish(self):
        for way in WAYS:
            pl.when(exists(self.places, self.counts, way, 1))(self.copy(way).wait_send)


def solve_kernel(counts, blocks, coarse, refs):
    right_side, guess, r, b, gr, gb = refs[:6]
    refs = list(refs[6:])
    take = lambda count=1: [refs.pop(0) for _ in range(count)] if count > 1 else refs.pop(0)
    places = tuple(lax.axis_index(axis) for axis in AXES)
    n0 = blocks[0][0]
    raw_g, raw_v, raw_sems = take(3)
    sent_shapes, got_shapes = Top.shapes(n0)
    w0, d0 = take(2)
    top = Top(blocks[0], places, counts, r, b, gr, gb, w0, d0, take(len(sent_shapes)), dict(zip(WAYS, take(len(WAYS)))), take(2))
    levels = [top]
    for number in range(1, LEVELS):
        if number < SHARED:
            levels.append(Grid(number, blocks[number], places, counts, *take(4)))
        else:
            levels.append(Grid(number, coarse[number - SHARED], (0, 0, 0), (1, 1, 1), *take(4)))
    rings = {}
    for number in REACH:
        n = blocks[number][0]
        members = take(1 + (2 if Ring.sizes(n)[2] != n else 0) + len(WAYS))
        rings[number] = Ring(levels[number], members, take(2))
    pairs = take(LEVELS - 1)
    spreads = take(LEVELS - 1)
    centres = take(LEVELS - 1)
    block_s, block_v, packet, line, joined, packets, line_send, line_recv, gather_send, gather_recv = refs

    loads = [pltpu.make_async_copy(source, target, raw_sems.at[i]) for i, (source, target) in enumerate(((right_side, raw_g), (guess, raw_v)))]
    for load in loads:
        load.start()
    barrier = pltpu.get_barrier_semaphore()
    nx, ny, nz = counts

    def greet(device):
        pl.semaphore_signal(barrier, inc=1, device_id=device, device_id_type=MESH)

    def greet_plane(offset, carry):
        other = lax.rem(places[0] * ny + places[1] + offset, nx * ny)
        greet({AXES[0]: other // ny, AXES[1]: other % ny})
        return carry
    lax.fori_loop(1, nx * ny, greet_plane, 0)
    for offset in range(1, nz):
        greet({AXES[2]: lax.rem(places[2] + offset, nz)})
    for way in WAYS:
        if way[2] and (way[0] or way[1]):
            pl.when(exists(places, counts, way, 1))(lambda way=way: greet(along(places, way)))

    top.clear()
    top.prepare()
    top.missing()
    for load in loads:
        load.wait()
    even = (lax.broadcasted_iota(jnp.int32, (n0, n0), 0) + lax.broadcasted_iota(jnp.int32, (n0, n0), 1)) % 2 == 0

    def convert(step):
        for i in range(4):
            k = step * 4 + i
            at = (k + 2, pl.ds(8, n0), pl.ds(0, n0))
            first, second = raw_g[2 * k], raw_g[2 * k + 1]
            gr[at] = jnp.where(even, first, second)
            gb[at] = jnp.where(even, second, first)
            b[at] = jnp.where(even, raw_v[2 * k + 1], raw_v[2 * k])
    loop(n0 // 8, convert)
    top.pack(False)
    near = [jnp.where(place > 0, 1, 0) + jnp.where(place < count - 1, 1, 0) for place, count in zip(places, counts)]
    pl.semaphore_wait(barrier, nx * ny + nz - 2 + near[2] * ((near[0] + 1) * (near[1] + 1) - 1))
    top.send()
    for level in levels[1:]:
        level.prepare()
    for ring in rings.values():
        ring.clear()
    block_v[...] = jnp.zeros_like(block_v)
    top.land()
    top.sweep(0)
    top.sweep(1)
    top.restrict_to(levels[1].s, (EDGE, 8), pairs[0])
    for number in range(1, SHARED):
        level = levels[number]
        rings[number].post()
        if number == 2:
            top.sent()
            top.post(True)
        rings[number].land()
        level.sweep(0, zero=True, beyond=level.reach)
        level.sweep(1, beyond=level.reach - 1)
        if number + 1 < SHARED:
            level.restrict_to(levels[number + 1].s, (EDGE, 8), pairs[number])
        else:
            level.restrict_to(block_s, (0, 0), pairs[number])

    bx, by, bz = blocks[SHARED]
    wide = LANES // bx
    packed = jnp.zeros((rows_of(by), LANES), jnp.float32)
    for x in range(bx):
        packed = packed + pltpu.roll(block_s[x], x * wide + places[2] * bz, 1)
    packet[...] = packed[:by]

    def line_copy(source, target):
        return pltpu.make_async_remote_copy(
            src_ref=packet, dst_ref=line.at[source], send_sem=line_send.at[target], recv_sem=line_recv.at[source],
            device_id={AXES[2]: target}, device_id_type=MESH)

    for offset in range(1, nz):
        line_copy(places[2], lax.rem(places[2] + offset, nz)).start()
    merged = packed[:by]
    for offset in range(1, nz):
        source = lax.rem(places[2] + nz - offset, nz)
        line_copy(source, lax.rem(places[2] + offset, nz)).wait_recv()
        merged = merged + line[source]
    joined[...] = merged
    total = nx * ny
    me = places[0] * ny + places[1]

    def plane_copy(target):
        return pltpu.make_async_remote_copy(
            src_ref=joined, dst_ref=packets.at[me], send_sem=gather_send, recv_sem=gather_recv,
            device_id={AXES[0]: target // ny, AXES[1]: target % ny}, device_id_type=MESH)

    def post(offset, carry):
        plane_copy(lax.rem(me + offset, total)).start()
        return carry
    lax.fori_loop(1, total, post, 0)
    packets[me] = merged
    top.land(True)
    everyone = pltpu.make_async_remote_copy(
        src_ref=packets.at[pl.ds(0, total - 1)], dst_ref=packets.at[pl.ds(0, total - 1)], send_sem=gather_send, recv_sem=gather_recv,
        device_id={AXES[0]: places[0]}, device_id_type=MESH)
    everyone.wait_recv()
    whole = levels[SHARED]

    def unpack(px):
        for py in range(0, ny, 2):
            pair = jnp.concatenate([packets[px * ny + py], packets[px * ny + py + 1]], axis=0)
            for x in range(bx):
                whole.s[px * bx + x, pl.ds(py * by, 2 * by), :] = turn(pair, -x * wide)
    loop(nx, unpack)

    for number in range(SHARED, LEVELS - 1):
        level = levels[number]
        level.sweep(0, zero=True)
        level.sweep(1)
        level.restrict_to(levels[number + 1].s, (0, 0), pairs[number])
    level = levels[LEVELS - 1]
    level.sweep(0, zero=True)
    level.sweep(1)
    for _ in range(COARSE_SWEEPS - 1):
        level.sweep(0)
        level.sweep(1)
    for number in reversed(range(SHARED, LEVELS - 1)):
        level, below = levels[number], levels[number + 1]
        below.reflect()
        lift(below.v, below.ox, below.dims, (0, 0, 0), (1, 1, 1), level, spreads[number], centres[number])
        level.sweep(0)
        level.sweep(1)

    whole.reflect()
    shift = lax.rem(LANES - places[2] * bz, LANES)
    odd = lax.rem(places[1] + 1, 2) == 1
    for x in range(bx + 8):
        part = whole.v[places[0] * bx + (x - 4 + whole.ox), pl.ds(pl.multiple_of((places[1] + 1) // 2 * 8, 8), 24), :]
        block_v[x, pl.ds(4, 16)] = pltpu.roll(jnp.where(odd, part[4:20], part[:16]), shift, 1)
    lift(block_v, 4, blocks[SHARED], places, counts, levels[SHARED - 1], spreads[SHARED - 1], centres[SHARED - 1])
    for number in reversed(range(1, SHARED)):
        level = levels[number]
        level.sweep(0, beyond=level.reach - (1 if number == 1 else 2))
        level.sweep(1, beyond=level.reach - 3)
        level.reflect()
        lift(level.v, level.ox, level.dims, places, counts, levels[number - 1], spreads[number - 1], centres[number - 1])
    top.sweep(0)
    top.sweep(1)

    top.sent(True)
    for ring in rings.values():
        ring.finish()
    for offset in range(1, nz):
        line_copy(places[2], lax.rem(places[2] + offset, nz)).wait_send()
    everyone.wait_send()


def finish_kernel(counts, dims, r, b, gr, gb, solution, residual, d):
    places = tuple(lax.axis_index(axis) for axis in AXES)
    step = pl.program_id(0)
    n, many = dims[1], dims[0] // 2 // pl.num_programs(0)

    @pl.when(step == 0)
    def _():
        write_diagonals(d, dims, places, counts)
    even = (row_iota(n) + lane_iota(n)) % 2 == 0
    last = counts[0] * (dims[0] // 2) - 1
    group = solution.shape[0] // 2
    for i in range(group):
        k = step * group + i
        at = places[0] * (dims[0] // 2) + k
        kind = jnp.where(at == 0, 1, jnp.where(at == last, 2, 0))
        red, black = remainders(r, b, gr, gb, d, k + 2, kind, even, n)
        own = (k + 2, pl.ds(8, n), slice(None))
        for out, x, y in ((solution, r[own], b[own]), (residual, red, black)):
            out[2 * i] = jnp.where(even, x, y)[:, :n]
            out[2 * i + 1] = jnp.where(even, y, x)[:, :n]


def solution(mesh):
    counts = tuple(mesh.shape[axis] for axis in AXES)

    def per_device(right_side, guess):
        shape = right_side.shape
        blocks = [tuple(side >> level for side in shape) for level in range(SHARED + 1)]
        whole = tuple(side * count for side, count in zip(blocks[SHARED], counts))
        coarse = [tuple(side >> level for side in whole) for level in range(LEVELS - SHARED)]
        grids = blocks[:SHARED] + coarse
        n0 = blocks[0][0]
        scratch = []
        vmem = lambda *dims: scratch.append(pltpu.VMEM(dims, jnp.float32))
        sems = lambda *dims: scratch.append(pltpu.SemaphoreType.DMA(dims))
        vmem(*shape)
        vmem(*shape)
        sems(2)
        vmem(4, n0 + 8, LANES)
        vmem(3, n0, LANES)
        sent, got = Top.shapes(n0)
        for dims in sent:
            vmem(*dims)
        for way in WAYS:
            vmem(*got[way])
        sems(len(WAYS))
        sems(len(WAYS))
        for number, (x, y, z) in enumerate(grids):
            if number == 0:
                continue
            _, _, height, planes, tall = layout(number, (x, y, z))
            vmem(planes, tall, LANES)
            if number in REACH:
                vmem(planes, tall, LANES)
            else:
                vmem(x, rows_of(y), LANES)
            vmem(3, max(height, rows_of(inner_height(number, (x, y, z)) + 1)) if number in REACH else height, LANES)
            vmem(2, rows_of(y), LANES)
        for number in REACH:
            n = blocks[number][0]
            _, groups, cut, _, cuts = Ring.sizes(n)
            vmem(groups, n, LANES)
            if cut != n:
                vmem(cuts, n, LANES)
                vmem(cuts, n, LANES)
            for way in WAYS:
                vmem(*Ring.shape(n, REACH[number], way))
            sems(len(WAYS))
            sems(len(WAYS))
        for x, y, z in grids[:-1]:
            vmem(x // 2, max(16, y), LANES)
        for _ in range(2):
            for number in range(LEVELS - 1):
                _, _, _, planes, tall = lift_shape(number, blocks[number + 1] if number < SHARED else grids[number + 1])
                vmem(planes, tall, LANES)
        bx, by, bz = blocks[SHARED]
        vmem(bx, rows_of(by), LANES)
        vmem(bx + 8, 24, LANES)
        vmem(by, LANES)
        vmem(counts[2], by, LANES)
        vmem(by, LANES)
        total = counts[0] * counts[1]
        vmem(total, by, LANES)
        sems(counts[2])
        sems(counts[2])
        scratch.append(pltpu.SemaphoreType.DMA)
        scratch.append(pltpu.SemaphoreType.DMA)

        def kernel(*refs):
            solve_kernel(counts, blocks, coarse, refs)

        whole_block = pl.BlockSpec(memory_space=pltpu.VMEM)
        field = jax.ShapeDtypeStruct((n0 // 2 + 4, n0 + 24, LANES), jnp.float32)
        fields = pl.pallas_call(
            kernel,
            out_shape=(field,) * 4,
            in_specs=[pl.BlockSpec(memory_space=pltpu.HBM)] * 2,
            out_specs=(whole_block,) * 4,
            scratch_shapes=scratch,
            compiler_params=pltpu.CompilerParams(collective_id=0, has_side_effects=True, vmem_limit_bytes=VMEM_LIMIT * 2**20),
            name="vcycle",
        )(right_side, guess)

        def last(*refs):
            finish_kernel(counts, shape, *refs)
        block = pl.BlockSpec((8,) + shape[1:], lambda i: (i, 0, 0))
        return pl.pallas_call(
            last,
            grid=(n0 // 8,),
            out_shape=(jax.ShapeDtypeStruct(shape, jnp.float32),) * 2,
            in_specs=[whole_block] * 4,
            out_specs=(block,) * 2,
            scratch_shapes=[pltpu.VMEM((3, n0, LANES), jnp.float32)],
            compiler_params=pltpu.CompilerParams(vmem_limit_bytes=8 * 2**20),
            name="finish",
        )(*fields)

    spec = P(*AXES)
    return jax.shard_map(per_device, mesh=mesh, in_specs=(spec, spec), out_specs=(spec, spec), check_vma=False)
```

time: 116 us -> 80.3 us (0.69)
  Pallas kernels: 111 us -> 76.3 us
  local copies, waits for them, and re-layouts: 4.63 us -> 3.17 us
    pallas_call x1 -> x2, Pallas kernels: 111 us -> 76.3 us  [the longest x1 72.3 us: per_device(): pl.pallas_call(kernel, out_shape=(field,) * 4, in_specs=[pl.BlockSpec(mem...]
    unnamed x4, local copies, waits for them, and re-layouts: 4.63 us -> 3.17 us
where the time goes in v3:
time: 80.3 us; the launch traced here: 80.1 us
  Pallas kernels  76.3 us (95%)
  local copies, waits for them, and re-layouts  3.17 us (4%)
    pallas_call x1, Pallas kernels, per_device(): pl.pallas_call(kernel, out_shape=(field,) * 4, in_specs=[pl.BlockSpec(mem...  72.3 us
    pallas_call x1, Pallas kernels, per_device(): pl.pallas_call(last, grid=(n0 // 8,), out_shape=(jax.ShapeDtypeStruct(sha...  4.01 us
    unnamed x4, local copies, waits for them, and re-layouts  3.17 us

profile of v3, /device:TPU:1, one launch (start us, length us, event | category | flops | bytes accessed | tf_op | source)
XLA Modules:
  0.0 80.1 jit_solution(18407409779018085525)
XLA Ops:
  0.6 0.0 copy-start
  0.6 1.6 %copy-done = f32[64,64,64]{2,1,0:T(8,128)S(1)} copy-done((f32[64,64,64]{2,1,0:T(8,128)S(1)}, f32[64,64,64]{2,1,0:T(8,128)}, u32[]{:S(2)}) %copy-start) | copy-done | bytes 1048600
  2.2 0.0 copy-start.1
  2.2 1.6 %copy-done.1 = f32[64,64,64]{2,1,0:T(8,128)S(1)} copy-done((f32[64,64,64]{2,1,0:T(8,128)S(1)}, f32[64,64,64]{2,1,0:T(8,128)}, u32[]{:S(2)}) %copy-start.1) | copy-done | bytes 1048600
  3.8 72.3 %vcycle.1 = (f32[36,88,128]{2,1,0:T(8,128)S(1)}, f32[36,88,128]{2,1,0:T(8,128)S(1)}, f32[36,88,128]{2,1,0:T(8,128)S(1)}, f32[36,88,128]{2,1,0:T(8,128)S(1)}) custom-call(f32[64,64,64]{2,1,0:T(8,128)S(1)} %copy-done, f32[64,64,64]{2,1,0:T(8,128)S(1)} %copy-done.1), custom_call_target="tpu_custom_call" | custom-call | tf_op jit(solution)/shard_map/vcycle/pallas_call | solution.py:956
  76.1 4.0 %finish.1 = (f32[64,64,64]{2,1,0:T(8,128)}, f32[64,64,64]{2,1,0:T(8,128)}) custom-call(f32[36,88,128]{2,1,0:T(8,128)S(1)} %get-tuple-element.6.refs_0_, f32[36,88,128]{2,1,0:T(8,128)S(1)} %get-tuple-element.7.refs_1_, f32[36,88,128]{2,1,0:T(8,128)S(1)} %get-tuple-element.8.refs_2_, f32[36,88,128]{2,1,0:T(8,128)S(1)} %get-tuple-element.9.refs_3_), custom_call_target="tpu_custom_call" | custom-call | tf_op jit(solution)/shard_map/finish/pallas_call | solution.py:969
Async XLA Ops:
  0.6 1.6 %copy-start = (f32[64,64,64]{2,1,0:T(8,128)S(1)}, f32[64,64,64]{2,1,0:T(8,128)}, u32[]{:S(2)}) copy-start(f32[64,64,64]{2,1,0:T(8,128)} %refs_0_.1) | copy-start | bytes 3145732
  2.2 1.6 %copy-start.1 = (f32[64,64,64]{2,1,0:T(8,128)S(1)}, f32[64,64,64]{2,1,0:T(8,128)}, u32[]{:S(2)}) copy-start(f32[64,64,64]{2,1,0:T(8,128)} %refs_1_.1) | copy-start | bytes 3145732

commit v4 on v3

--- a/solution.py
+++ b/solution.py
@@ -10,7 +10,7 @@
 LEVELS = 7
 COARSE_SWEEPS = 4
 SHARED = 4
-VMEM_LIMIT = 32
+VMEM_LIMIT = 46
 LANES = 128
 EDGE = 8
 AXES = ("gx", "gy", "gz")
@@ -18,6 +18,7 @@
 WAYS = [way for way in itertools.product((-1, 0, 1), repeat=3) if any(way)]
 FINAL = {0: 1, 1: 2, 2: 3, 3: 3}
 REACH = {level: FINAL[level] + 3 for level in range(1, SHARED)}
+SPARE = {SHARED - 2: 4}
 
 
 def rows_of(count):
@@ -47,13 +48,11 @@
     return pltpu.roll(value, amount, 1) if amount else value
 
 
-def exact_dot(value, matrix):
+def near_dot(value, matrix):
     first = value.astype(jnp.bfloat16)
-    rest = value - first.astype(jnp.float32)
-    second = rest.astype(jnp.bfloat16)
-    third = (rest - second.astype(jnp.float32)).astype(jnp.bfloat16)
+    second = (value - first.astype(jnp.float32)).astype(jnp.bfloat16)
     dot = lambda part: jnp.dot(part, matrix, preferred_element_type=jnp.float32)
-    return (dot(third) + dot(second)) + dot(first)
+    return dot(second) + dot(first)
 
 
 def widest(count, most, step=1):
@@ -72,6 +71,7 @@
         self.ox, self.start, self.height, _, _ = layout(number, dims)
         self.sx, self.sy = (EDGE, 8) if self.reach else (0, 0)
         self.rows = rows_of(dims[1])
+        self.spare, self.tall = spare_of(number, dims)
 
     def prepare(self):
         x, y, z = self.dims
@@ -89,7 +89,7 @@
         for wall in range(2):
             self.w[wall] = jnp.where(valid, 1.0 / (diagonal + wall), 0.0)
         self.w[2] = jnp.zeros_like(diagonal)
-        valid, diagonal = base(self.rows, 8)
+        valid, diagonal = base(self.tall, 8 - self.spare)
         for wall in range(2):
             self.d[wall] = jnp.where(valid, diagonal + wall, 0.0)
         self.v[...] = jnp.zeros_like(self.v)
@@ -142,27 +142,27 @@
         loop(planes // chunk, body)
 
     def remainder(self, first, chunk):
-        totals, centres = self.total(first, chunk, 8, self.rows)
+        totals, centres = self.total(first, chunk, 8 - self.spare, self.tall)
         out = []
         for i in range(chunk):
             d = self.d[self.wall(first + i)]
-            r = self.s[first + i + self.sx, pl.ds(self.sy, self.rows), :] - (d * centres[i] - totals[i])
-            out.append(r if self.dims[1] == self.rows else jnp.where(d > 0, r, 0.0))
+            r = self.s[first + i + self.sx, pl.ds(self.sy - self.spare, self.tall), :] - (d * centres[i] - totals[i])
+            out.append(r if self.dims[1] >= 8 else jnp.where(d > 0, r, 0.0))
         return out
 
     def restrict_to(self, target, corner, pairs):
-        rows = self.rows
-        chunk = widest(self.dims[0], 32 * 8 // rows, 2)
+        rows, planes = self.tall, self.dims[0] + 2 * self.spare
+        chunk = widest(planes, 96 * 8 // rows, 2)
         half = chunk // 2
         if rows < 16:
             pairs[...] = jnp.zeros_like(pairs)
 
         def first(step):
-            r = self.remainder(step * chunk, chunk)
+            r = self.remainder(step * chunk - self.spare, chunk)
             for i in range(half):
                 pairs[step * half + i, pl.ds(0, rows), :] = r[2 * i] + r[2 * i + 1]
-        loop(self.dims[0] // chunk, first)
-        narrow(self.dims, target, corner, pairs)
+        loop(planes // chunk, first)
+        narrow(planes, rows, self.dims[2], self.spare, target, [at - self.spare // 2 for at in corner], pairs)
 
     def reflect(self):
         (x, y, z), v, ox = self.dims, self.v, self.ox
@@ -190,21 +190,26 @@
                 pl.when(self.places[axis] == self.counts[axis] - 1)(high)
 
 
-def narrow(dims, target, corner, pairs):
-    x, y, z = dims
-    coarse_rows = rows_of(y // 2)
-    source_lane = lax.broadcasted_iota(jnp.int32, (LANES, LANES), 0)
-    target_lane = lax.broadcasted_iota(jnp.int32, (LANES, LANES), 1)
-    halve = jnp.where((source_lane // 2 == target_lane) & (source_lane < z), 0.5, 0.0).astype(jnp.bfloat16)
-    planes = x // 2
-    many = min(planes, max(1, 256 // coarse_rows))
+def narrow(planes, rows, z, spare, target, corner, pairs):
+    coarse_rows = rows_of(rows // 2)
+    source_lane = signed(lax.broadcasted_iota(jnp.int32, (LANES, LANES), 0))
+    target_lane = signed(lax.broadcasted_iota(jnp.int32, (LANES, LANES), 1))
+    inside = (source_lane >= -spare) & (source_lane < z + spare)
+    halve = jnp.where(((source_lane + LANES) // 2 - LANES // 2 == target_lane) & inside, 0.5, 0.0).astype(jnp.bfloat16)
+    planes = planes // 2
+    many = widest(planes, max(1, 512 // coarse_rows))
 
     def second(step):
         at = pl.ds(step * many, many)
         q = pairs[at, pl.ds(0, coarse_rows, stride=2), :] + pairs[at, pl.ds(1, coarse_rows, stride=2), :]
-        q = exact_dot(q.reshape(many * coarse_rows, LANES), halve)
+        q = near_dot(q.reshape(many * coarse_rows, LANES), halve)
         target[pl.ds(step * many + corner[0], many), pl.ds(corner[1], coarse_rows), :] = q.reshape(many, coarse_rows, LANES)
     loop(planes // many, second)
+
+
+def spare_of(number, dims):
+    spare = SPARE.get(number, 0)
+    return spare, -(-(dims[1] + 2 * spare) // 16) * 16 if spare else rows_of(dims[1])
 
 
 def layout(number, dims):
@@ -252,7 +257,7 @@
 
     def first(step):
         e = v[pl.ds(step * many + (ox + low - 1), many), pl.ds(0, tall), :]
-        product = exact_dot(e.reshape(many * tall, LANES), matrix)
+        product = near_dot(e.reshape(many * tall, LANES), matrix)
         at = pl.ds(step * many, many)
         spread[at] = product[:, :LANES].reshape(many, tall, LANES)
         centre[at] = product[:, LANES:].reshape(many, tall, LANES)
@@ -379,7 +384,7 @@
     def restrict_to(self, target, corner, pairs):
         n = self.n
         even = (row_iota(n) + lane_iota(n)) % 2 == 0
-        chunk = 4
+        chunk = 8
 
         def body(step):
             for i in range(chunk):
@@ -387,7 +392,7 @@
                 red, black = remainders(self.r, self.b, self.gr, self.gb, self.d, k + 2, self.kind(k), even, n)
                 pairs[k] = red + black
         loop(self.pairs // chunk, body)
-        narrow(self.dims, target, corner, pairs)
+        narrow(self.dims[0], n, self.dims[2], 0, target, corner, pairs)
 
     @staticmethod
     def shapes(n):
@@ -449,19 +454,20 @@
                 return jnp.where(row < 4, b, jnp.where(row < 6, red, black))
             for k in range(half):
                 self.out[2 + high][k] = jnp.where(tile < 64, edge(k), pltpu.roll(edge(k + half), 64, 1))
-        for index, ref in enumerate(arrays):
-            def body(t, ref=ref, index=index):
-                at = pl.ds(pl.multiple_of(t * 16, 16), 16)
-                lane = lane_iota(16)
-                ahead = (lane + (LANES - 60)) % LANES
-                first = last = jnp.zeros((16, LANES), jnp.float32)
-                for k in range(pairs):
-                    moved = turn(ref[k + 2, pl.ds(pl.multiple_of(t * 16 + 8, 8), 16), :], 4 * k)
-                    first = jnp.where(lane // 4 == k, moved, first)
-                    last = jnp.where(ahead // 4 == k, moved, last)
-                self.out[4][index, at] = first
-                self.out[5][index, at] = last
-            loop(n // 16, body)
+        def body(t):
+            at = pl.ds(pl.multiple_of(t * 8, 8), 8)
+            ahead = (tile + (LANES - 60)) % LANES
+            first = [jnp.zeros((8, LANES), jnp.float32)] * len(arrays)
+            last = list(first)
+            for k in range(pairs):
+                for index, ref in enumerate(arrays):
+                    moved = turn(ref[k + 2, pl.ds(pl.multiple_of(t * 8 + 8, 8), 8), :], 4 * k)
+                    first[index] = jnp.where((tile >= 4 * k) & (tile < 4 * k + 4), moved, first[index])
+                    last[index] = jnp.where(ahead // 4 == k, moved, last[index])
+            for index in range(len(arrays)):
+                self.out[4][index, at] = first[index]
+                self.out[5][index, at] = last[index]
+        loop(n // 8, body)
         for high_x in range(2):
             for high_z in range(2):
                 offset = 60 if high_z else 0
@@ -499,17 +505,16 @@
         def ends(high, low, to, k):
             pick = to % 8 < 4
             return turn(jnp.where(pick, high, low) if k % 2 == 0 else jnp.where(pick, low, high), 64 - 4 * k)
-        for index, ref in enumerate(arrays):
-            high, low = got[(0, 0, -1)], got[(0, 0, 1)]
-
-            def body(t, ref=ref, index=index, high=high, low=low):
-                at = pl.ds(pl.multiple_of(t * 16, 16), 16)
-                to = lane_iota(16)
-                h, l = high[index, at], low[index, at]
-                for k in range(pairs):
-                    own = (k + 2, pl.ds(pl.multiple_of(t * 16 + 8, 8), 16), slice(None))
-                    ref[own] = jnp.where(to < 64, ref[own], ends(h, l, to, k))
-            loop(n // 16, body)
+        high, low = got[(0, 0, -1)], got[(0, 0, 1)]
+
+        def body(t):
+            at = pl.ds(pl.multiple_of(t * 8, 8), 8)
+            packs = [(high[index, at], low[index, at]) for index in range(len(arrays))]
+            for k in range(pairs):
+                own = (k + 2, pl.ds(pl.multiple_of(t * 8 + 8, 8), 8), slice(None))
+                for (h, l), ref in zip(packs, arrays):
+                    ref[own] = jnp.where(tile < 64, ref[own], ends(h, l, tile, k))
+        loop(n // 8, body)
         for side in (-1, 1):
             face = got[(0, -side, 0)]
             base = 8 + n if side > 0 else 0
@@ -636,7 +641,10 @@
     def post(self):
         n, s = self.level.dims[0], self.level.s
         each, groups, cut, cuts_each, cuts = Ring.sizes(n)
-        plane = lambda x: s[EDGE + x, pl.ds(8, n), :]
+
+        def plane(x):
+            value = s[EDGE + x, pl.ds(8, n), :]
+            return jnp.where(lane_iota(n) < n, value, 0.0) if SPARE.get(self.level.number - 1) else value
         for g in range(groups):
             value = plane(g * each)
             for i in range(1, min(each, n)):
@@ -706,7 +714,7 @@
     pairs = take(LEVELS - 1)
     spreads = take(LEVELS - 1)
     centres = take(LEVELS - 1)
-    block_s, block_v, packet, line, joined, packets, line_send, line_recv, gather_send, gather_recv = refs
+    block_s, block_v, packet, line, joined, packets, line_send, line_recv, gather_send, gather_recv, spread_sem = refs
 
     loads = [pltpu.make_async_copy(source, target, raw_sems.at[i]) for i, (source, target) in enumerate(((right_side, raw_g), (guess, raw_v)))]
     for load in loads:
@@ -717,16 +725,19 @@
     def greet(device):
         pl.semaphore_signal(barrier, inc=1, device_id=device, device_id_type=MESH)
 
-    def greet_plane(offset, carry):
-        other = lax.rem(places[0] * ny + places[1] + offset, nx * ny)
-        greet({AXES[0]: other // ny, AXES[1]: other % ny})
-        return carry
-    lax.fori_loop(1, nx * ny, greet_plane, 0)
-    for offset in range(1, nz):
-        greet({AXES[2]: lax.rem(places[2] + offset, nz)})
     for way in WAYS:
-        if way[2] and (way[0] or way[1]):
-            pl.when(exists(places, counts, way, 1))(lambda way=way: greet(along(places, way)))
+        pl.when(exists(places, counts, way, 1))(lambda way=way: greet(along(places, way)))
+    near = [jnp.where(place > 0, 1, 0) + jnp.where(place < count - 1, 1, 0) for place, count in zip(places, counts)]
+
+    def tell(turn):
+        for way in WAYS:
+            if not way[2] or not (way[0] or way[1]):
+                @pl.when(exists(places, counts, way, 1))
+                def _(way=way):
+                    pl.semaphore_signal(spread_sem.at[turn], inc=1, device_id=along(places, way), device_id_type=MESH)
+
+    def hear(turn):
+        pl.semaphore_wait(spread_sem.at[turn], (near[0] + 1) * (near[1] + 1) - 1 + near[2])
 
     top.clear()
     top.prepare()
@@ -745,8 +756,7 @@
             b[at] = jnp.where(even, raw_v[2 * k + 1], raw_v[2 * k])
     loop(n0 // 8, convert)
     top.pack(False)
-    near = [jnp.where(place > 0, 1, 0) + jnp.where(place < count - 1, 1, 0) for place, count in zip(places, counts)]
-    pl.semaphore_wait(barrier, nx * ny + nz - 2 + near[2] * ((near[0] + 1) * (near[1] + 1) - 1))
+    pl.semaphore_wait(barrier, (near[0] + 1) * (near[1] + 1) * (near[2] + 1) - 1)
     top.send()
     for level in levels[1:]:
         level.prepare()
@@ -754,22 +764,24 @@
         ring.clear()
     block_v[...] = jnp.zeros_like(block_v)
     top.land()
+    tell(0)
     top.sweep(0)
     top.sweep(1)
     top.restrict_to(levels[1].s, (EDGE, 8), pairs[0])
-    for number in range(1, SHARED):
+    hear(0)
+    for number in range(1, SHARED - 1):
         level = levels[number]
         rings[number].post()
-        if number == 2:
-            top.sent()
-            top.post(True)
         rings[number].land()
+        tell(number)
         level.sweep(0, zero=True, beyond=level.reach)
         level.sweep(1, beyond=level.reach - 1)
-        if number + 1 < SHARED:
-            level.restrict_to(levels[number + 1].s, (EDGE, 8), pairs[number])
-        else:
-            level.restrict_to(block_s, (0, 0), pairs[number])
+        level.restrict_to(levels[number + 1].s, (EDGE, 8), pairs[number])
+        hear(number)
+    last = levels[SHARED - 1]
+    last.sweep(0, zero=True, beyond=2)
+    last.sweep(1, beyond=1)
+    last.restrict_to(block_s, (0, 0), pairs[SHARED - 1])
 
     bx, by, bz = blocks[SHARED]
     wide = LANES // bx
@@ -785,6 +797,9 @@
 
     for offset in range(1, nz):
         line_copy(places[2], lax.rem(places[2] + offset, nz)).start()
+    rings[SHARED - 1].post()
+    top.sent()
+    top.post(True)
     merged = packed[:by]
     for offset in range(1, nz):
         source = lax.rem(places[2] + nz - offset, nz)
@@ -794,16 +809,20 @@
     total = nx * ny
     me = places[0] * ny + places[1]
 
-    def plane_copy(target):
+    def plane_copy(to_x, to_y):
         return pltpu.make_async_remote_copy(
             src_ref=joined, dst_ref=packets.at[me], send_sem=gather_send, recv_sem=gather_recv,
-            device_id={AXES[0]: target // ny, AXES[1]: target % ny}, device_id_type=MESH)
-
-    def post(offset, carry):
-        plane_copy(lax.rem(me + offset, total)).start()
-        return carry
-    lax.fori_loop(1, total, post, 0)
+            device_id={AXES[0]: to_x, AXES[1]: to_y}, device_id_type=MESH)
+
+    xs = [lax.rem(places[0] + step, nx) for step in range(nx)]
+    ys = [lax.rem(places[1] + step, ny) for step in range(ny)]
+    far = lambda at: min(at[0], nx - at[0]) + min(at[1], ny - at[1])
+    for to_x, to_y in sorted(itertools.product(range(nx), range(ny)), key=far, reverse=True)[:-1]:
+        plane_copy(xs[to_x], ys[to_y]).start()
     packets[me] = merged
+    rings[SHARED - 1].land()
+    last.sweep(0, zero=True, beyond=last.reach)
+    last.sweep(1, beyond=last.reach - 1)
     top.land(True)
     everyone = pltpu.make_async_remote_copy(
         src_ref=packets.at[pl.ds(0, total - 1)], dst_ref=packets.at[pl.ds(0, total - 1)], send_sem=gather_send, recv_sem=gather_recv,
@@ -917,7 +936,7 @@
             else:
                 vmem(x, rows_of(y), LANES)
             vmem(3, max(height, rows_of(inner_height(number, (x, y, z)) + 1)) if number in REACH else height, LANES)
-            vmem(2, rows_of(y), LANES)
+            vmem(2, spare_of(number, (x, y, z))[1], LANES)
         for number in REACH:
             n = blocks[number][0]
             _, groups, cut, _, cuts = Ring.sizes(n)
@@ -929,8 +948,9 @@
                 vmem(*Ring.shape(n, REACH[number], way))
             sems(len(WAYS))
             sems(len(WAYS))
-        for x, y, z in grids[:-1]:
-            vmem(x // 2, max(16, y), LANES)
+        for number, (x, y, z) in enumerate(grids[:-1]):
+            spare, tall = spare_of(number, (x, y, z))
+            vmem(x // 2 + spare, max(16, tall), LANES)
         for _ in range(2):
             for number in range(LEVELS - 1):
                 _, _, _, planes, tall = lift_shape(number, blocks[number + 1] if number < SHARED else grids[number + 1])
@@ -947,6 +967,7 @@
         sems(counts[2])
         scratch.append(pltpu.SemaphoreType.DMA)
         scratch.append(pltpu.SemaphoreType.DMA)
+        scratch.append(pltpu.SemaphoreType.REGULAR((SHARED - 1,)))
 
         def kernel(*refs):
             solve_kernel(counts, blocks, coarse, refs)
@@ -965,10 +986,10 @@
 
         def last(*refs):
             finish_kernel(counts, shape, *refs)
-        block = pl.BlockSpec((8,) + shape[1:], lambda i: (i, 0, 0))
+        block = pl.BlockSpec((16,) + shape[1:], lambda i: (i, 0, 0))
         return pl.pallas_call(
             last,
-            grid=(n0 // 8,),
+            grid=(n0 // 16,),
             out_shape=(jax.ShapeDtypeStruct(shape, jnp.float32),) * 2,
             in_specs=[whole_block] * 4,
             out_specs=(block,) * 2,

time: 80.3 us -> 68.8 us (0.86)
  Pallas kernels: 76.3 us -> 68.1 us
  local copies, waits for them, and re-layouts: 3.17 us -> 0 us
    pallas_call x1, Pallas kernels: 72.3 us -> 65.1 us  [per_device(): pl.pallas_call(kernel, out_shape=(field,) * 4, in_specs=[pl.BlockSpec(mem...]
    unnamed x4 -> x0, local copies, waits for them, and re-layouts: 3.17 us -> none
    pallas_call x1, Pallas kernels: 4.01 us -> 2.95 us  [per_device(): pl.pallas_call(last, grid=(n0 // 16,), out_shape=(jax.ShapeDtypeStruct(sh...]
where the time goes in v4:
time: 68.8 us; the launch traced here: 68.7 us
  Pallas kernels  68.1 us (99%)
    pallas_call x1, Pallas kernels, per_device(): pl.pallas_call(kernel, out_shape=(field,) * 4, in_specs=[pl.BlockSpec(mem...  65.1 us
    pallas_call x1, Pallas kernels, per_device(): pl.pallas_call(last, grid=(n0 // 16,), out_shape=(jax.ShapeDtypeStruct(sh...  2.95 us

profile of v4, /device:TPU:1, one launch (start us, length us, event | category | flops | bytes accessed | tf_op | source)
XLA Modules:
  0.0 68.7 jit_solution(2628062168759208385)
XLA Ops:
  0.6 65.1 %vcycle.1 = (f32[36,88,128]{2,1,0:T(8,128)S(1)}, f32[36,88,128]{2,1,0:T(8,128)S(1)}, f32[36,88,128]{2,1,0:T(8,128)S(1)}, f32[36,88,128]{2,1,0:T(8,128)S(1)}) custom-call(f32[64,64,64]{2,1,0:T(8,128)} %refs_0_.1, f32[64,64,64]{2,1,0:T(8,128)} %refs_1_.1), custom_call_target="tpu_custom_call" | custom-call | tf_op jit(solution)/shard_map/vcycle/pallas_call | solution.py:977
  65.7 2.9 %finish.1 = (f32[64,64,64]{2,1,0:T(8,128)}, f32[64,64,64]{2,1,0:T(8,128)}) custom-call(f32[36,88,128]{2,1,0:T(8,128)S(1)} %get-tuple-element.6.refs_0_, f32[36,88,128]{2,1,0:T(8,128)S(1)} %get-tuple-element.7.refs_1_, f32[36,88,128]{2,1,0:T(8,128)S(1)} %get-tuple-element.8.refs_2_, f32[36,88,128]{2,1,0:T(8,128)S(1)} %get-tuple-element.9.refs_3_), custom_call_target="tpu_custom_call" | custom-call | tf_op jit(solution)/shard_map/finish/pallas_call | solution.py:990

commit v5 on v4

--- a/solution.py
+++ b/solution.py
@@ -11,11 +11,13 @@
 COARSE_SWEEPS = 4
 SHARED = 4
 VMEM_LIMIT = 46
+SWEEP_SHARE, REST_SHARE, LAST_SHARE, GRID_SHARE = 0.4, 0.4, 0.0, 0.4
 LANES = 128
 EDGE = 8
 AXES = ("gx", "gy", "gz")
 MESH = pl.DeviceIdType.MESH
 WAYS = [way for way in itertools.product((-1, 0, 1), repeat=3) if any(way)]
+FLAT = [way for way in WAYS if not way[2] or not (way[0] or way[1])]
 FINAL = {0: 1, 1: 2, 2: 3, 3: 3}
 REACH = {level: FINAL[level] + 3 for level in range(1, SHARED)}
 SPARE = {SHARED - 2: 4}
@@ -55,6 +57,26 @@
     return dot(second) + dot(first)
 
 
+def write_beside(beside):
+    k = lax.broadcasted_iota(jnp.int32, (2 * LANES, LANES), 0)
+    f = lax.broadcasted_iota(jnp.int32, (2 * LANES, LANES), 1)
+    apart = (k - f + 2 * LANES) % LANES
+    beside[...] = jnp.where((apart == 1) | (apart == LANES - 1), 1.0, 0.0).astype(jnp.bfloat16)
+
+
+def lane_sums(values, beside, share):
+    many = int(len(values) * share)
+    out = []
+    if many:
+        height = values[0].shape[0]
+        value = jnp.concatenate(values[:many], axis=0)
+        first = value.astype(jnp.bfloat16)
+        second = (value - first.astype(jnp.float32)).astype(jnp.bfloat16)
+        sums = jnp.dot(jnp.concatenate([first, second], axis=1), beside[...], preferred_element_type=jnp.float32)
+        out = [sums[i * height:(i + 1) * height] for i in range(many)]
+    return out + [pltpu.roll(value, 1, 1) + pltpu.roll(value, LANES - 1, 1) for value in values[many:]]
+
+
 def widest(count, most, step=1):
     return max(size for size in range(step, count + 1, step) if count % size == 0 and (size <= most or size == step))
 
@@ -64,9 +86,9 @@
 
 
 class Grid:
-    def __init__(self, number, dims, places, counts, v, s, w, d):
+    def __init__(self, number, dims, places, counts, beside, v, s, w, d):
         self.number, self.dims, self.places, self.counts = number, dims, places, counts
-        self.v, self.s, self.w, self.d = v, s, w, d
+        self.v, self.s, self.w, self.d, self.beside = v, s, w, d, beside
         self.reach = REACH.get(number, 0)
         self.ox, self.start, self.height, _, _ = layout(number, dims)
         self.sx, self.sy = (EDGE, 8) if self.reach else (0, 0)
@@ -111,10 +133,10 @@
         total = slab[2:] + slab[:-2]
         total = total + self.v[pl.ds(at, count), pl.ds(start + 1, height), :] + self.v[pl.ds(at, count), pl.ds(start - 1, height), :]
         out = []
-        for i in range(count):
-            c = centre[i]
-            out.append(total[i] + (pltpu.roll(c, 1, 1) + pltpu.roll(c, LANES - 1, 1)))
-        return out, [centre[i] for i in range(count)]
+        centres = [centre[i] for i in range(count)]
+        for i, beside in enumerate(lane_sums(centres, self.beside, GRID_SHARE)):
+            out.append(total[i] + beside)
+        return out, centres
 
     def sweep(self, colour, zero=False, beyond=0):
         start, height = self.start, self.height
@@ -323,7 +345,8 @@
 class Top:
     number, ox, sets = 0, 2, 4
 
-    def __init__(self, dims, places, counts, r, b, gr, gb, w, d, out, got, sems):
+    def __init__(self, dims, places, counts, beside, r, b, gr, gb, w, d, out, got, sems):
+        self.beside = beside
         self.dims, self.places, self.counts = dims, places, counts
         self.r, self.b, self.gr, self.gb, self.w, self.d = r, b, gr, gb, w, d
         self.out, self.got, self.sems = out, got, sems
@@ -371,10 +394,9 @@
         even = (row_iota(height) + lane_iota(height)) % 2 == 0
 
         def body(step):
-            for i in range(chunk):
-                k = step * chunk + i - 1
-                at = k + 2
-                total = around(source, at, start, height, even, colour)
+            ats = [step * chunk + i + 1 for i in range(chunk)]
+            for at, total in zip(ats, around(source, ats, start, height, even, colour, self.beside, SWEEP_SHARE)):
+                k = at - 2
                 kind = self.kind(k)
                 if colour:
                     kind = jnp.where(kind == 1, 2, jnp.where(kind == 2, 1, kind))
@@ -387,9 +409,10 @@
         chunk = 8
 
         def body(step):
-            for i in range(chunk):
-                k = step * chunk + i
-                red, black = remainders(self.r, self.b, self.gr, self.gb, self.d, k + 2, self.kind(k), even, n)
+            ks = [step * chunk + i for i in range(chunk)]
+            kinds = [self.kind(k) for k in ks]
+            ats = [k + 2 for k in ks]
+            for k, (red, black) in zip(ks, remainders(self.r, self.b, self.gr, self.gb, self.d, ats, kinds, even, n, self.beside, REST_SHARE)):
                 pairs[k] = red + black
         loop(self.pairs // chunk, body)
         narrow(self.dims[0], n, self.dims[2], 0, target, corner, pairs)
@@ -430,9 +453,27 @@
             src_ref=source, dst_ref=got, send_sem=self.sems[0].at[k], recv_sem=self.sems[1].at[k],
             device_id=along(self.places, way), device_id_type=MESH)
 
+    def pack_ends(self, part, again):
+        tile = lane_iota(8)
+        many = self.pairs // self.sets
+        ahead = (tile + (LANES - 60)) % LANES
+        wide = 4 * many
+        for t in range(self.n // 8):
+            at = pl.ds(8 * t, 8)
+            for index, ref in enumerate([self.b] if again else [self.b, self.gr, self.gb]):
+                first = last = None
+                for k in range(part * many, part * many + many):
+                    moved = turn(ref[k + 2, pl.ds(8 * t + 8, 8), :], 4 * k)
+                    first = moved if first is None else jnp.where(tile // 4 == k, moved, first)
+                    last = moved if last is None else jnp.where(ahead // 4 == k, moved, last)
+                if part:
+                    first = jnp.where(tile // wide == part, first, self.out[4][index, at])
+                    last = jnp.where(ahead // wide == part, last, self.out[5][index, at])
+                self.out[4][index, at] = first
+                self.out[5][index, at] = last
+
     def pack(self, again):
         n, pairs = self.n, self.pairs
-        arrays = [self.b] if again else [self.b, self.gr, self.gb]
         low, tile = lane_iota(n) < 64, lane_iota(8)
         row = row_iota(8)
         half = pairs // 2
@@ -454,20 +495,6 @@
                 return jnp.where(row < 4, b, jnp.where(row < 6, red, black))
             for k in range(half):
                 self.out[2 + high][k] = jnp.where(tile < 64, edge(k), pltpu.roll(edge(k + half), 64, 1))
-        def body(t):
-            at = pl.ds(pl.multiple_of(t * 8, 8), 8)
-            ahead = (tile + (LANES - 60)) % LANES
-            first = [jnp.zeros((8, LANES), jnp.float32)] * len(arrays)
-            last = list(first)
-            for k in range(pairs):
-                for index, ref in enumerate(arrays):
-                    moved = turn(ref[k + 2, pl.ds(pl.multiple_of(t * 8 + 8, 8), 8), :], 4 * k)
-                    first[index] = jnp.where((tile >= 4 * k) & (tile < 4 * k + 4), moved, first[index])
-                    last[index] = jnp.where(ahead // 4 == k, moved, last[index])
-            for index in range(len(arrays)):
-                self.out[4][index, at] = first[index]
-                self.out[5][index, at] = last[index]
-        loop(n // 8, body)
         for high_x in range(2):
             for high_z in range(2):
                 offset = 60 if high_z else 0
@@ -483,6 +510,8 @@
                 self.out[6][2 * high_x + high_z] = value
 
     def post(self, again=False):
+        for part in range(self.sets):
+            self.pack_ends(part, again)
         self.pack(again)
         self.send(again)
 
@@ -494,17 +523,20 @@
         for way in WAYS:
             pl.when(exists(self.places, self.counts, way, 1))(self.copies(way, again).wait_send)
 
+    def wait(self, ways, again):
+        for way in ways:
+            pl.when(exists(self.places, self.counts, way, -1))(self.copies(way, again).wait_recv)
+
     def land(self, again=False):
         n, pairs, got = self.n, self.pairs, self.got
         half = pairs // 2
-        for way in WAYS:
-            pl.when(exists(self.places, self.counts, way, -1))(self.copies(way, again).wait_recv)
         arrays = [self.b] if again else [self.b, self.gr, self.gb]
         lane, tile = lane_iota(n), lane_iota(8)
 
         def ends(high, low, to, k):
             pick = to % 8 < 4
             return turn(jnp.where(pick, high, low) if k % 2 == 0 else jnp.where(pick, low, high), 64 - 4 * k)
+        self.wait([way for way in WAYS if not (way[0] or way[1])], again)
         high, low = got[(0, 0, -1)], got[(0, 0, 1)]
 
         def body(t):
@@ -515,6 +547,7 @@
                 for (h, l), ref in zip(packs, arrays):
                     ref[own] = jnp.where(tile < 64, ref[own], ends(h, l, tile, k))
         loop(n // 8, body)
+        self.wait([way for way in WAYS if way[1] and not way[0]], again)
         for side in (-1, 1):
             face = got[(0, -side, 0)]
             base = 8 + n if side > 0 else 0
@@ -531,6 +564,7 @@
                     if index < 2:
                         value = jnp.where(tile < 64, value, ends(h, l, tile, k))
                     ref[k + 2, pl.ds(base, 8), :] = value
+        self.wait([way for way in WAYS if way[0]], again)
         for side in (-1, 1):
             face = got[(-side, 0, 0)]
             near, far = (pairs + 2, pairs + 3) if side > 0 else (1, 0)
@@ -570,20 +604,25 @@
                         self.gr[place, pl.ds(base, 8), :] = pltpu.roll(value, 4, 0)
 
 
-def around(source, at, start, height, even, colour):
-    s = source[at, pl.ds(start, height), :]
-    left, right = source[at - 1, pl.ds(start, height), :], source[at + 1, pl.ds(start, height), :]
-    across = jnp.where(even, right, left) if colour else jnp.where(even, left, right)
-    total = (s + across) + (source[at, pl.ds(start + 1, height), :] + source[at, pl.ds(start - 1, height), :])
-    return total + (pltpu.roll(s, 1, 1) + pltpu.roll(s, LANES - 1, 1))
-
-
-def remainders(r, b, gr, gb, d, at, kind, even, n):
+def around(source, ats, start, height, even, colour, beside, share):
+    rows = pl.ds(start, height)
+    centres = [source[at, rows, :] for at in ats]
+    out = []
+    for at, s, z_sum in zip(ats, centres, lane_sums(centres, beside, share)):
+        left, right = source[at - 1, rows, :], source[at + 1, rows, :]
+        across = jnp.where(even, right, left) if colour else jnp.where(even, left, right)
+        total = (s + across) + (source[at, pl.ds(start + 1, height), :] + source[at, pl.ds(start - 1, height), :])
+        out.append(total + z_sum)
+    return out
+
+
+def remainders(r, b, gr, gb, d, ats, kinds, even, n, beside, share):
     rows = pl.ds(8, n)
-    other = jnp.where(kind == 1, 2, jnp.where(kind == 2, 1, kind))
-    red = gr[at, rows, :] - (d[kind] * r[at, rows, :] - around(b, at, 8, n, even, 0))
-    black = gb[at, rows, :] - (d[other] * b[at, rows, :] - around(r, at, 8, n, even, 1))
-    return red, black
+    out = []
+    for at, kind, reds, blacks in zip(ats, kinds, around(b, ats, 8, n, even, 0, beside, share), around(r, ats, 8, n, even, 1, beside, share)):
+        other = jnp.where(kind == 1, 2, jnp.where(kind == 2, 1, kind))
+        out.append((gr[at, rows, :] - (d[kind] * r[at, rows, :] - reds), gb[at, rows, :] - (d[other] * b[at, rows, :] - blacks)))
+    return out
 
 
 def write_diagonals(d, dims, places, counts):
@@ -666,24 +705,35 @@
     def land(self):
         n, s, reach = self.level.dims[0], self.level.s, self.level.reach
         each, groups, cut, cuts_each, cuts = Ring.sizes(n)
-        for way in WAYS:
-            pl.when(exists(self.places, self.counts, way, -1))(self.copy(way).wait_recv)
-        for to_x, to_y in itertools.product((-1, 0, 1), repeat=2):
+        for to_x, to_y in sorted(itertools.product((-1, 0, 1), repeat=2), key=lambda at: abs(at[0]) * 3 + abs(at[1])):
+            for way in WAYS:
+                if way[:2] == (-to_x, -to_y):
+                    pl.when(exists(self.places, self.counts, way, -1))(self.copy(way).wait_recv)
             height = 8 if to_y else n
             row = {-1: 0, 0: 8, 1: 8 + n}[to_y]
             lane = lane_iota(height)
             body = self.got[(-to_x, -to_y, 0)] if to_x or to_y else None
             high = self.got[(-to_x, -to_y, -1)]
             low = self.got[(-to_x, -to_y, 1)]
+
+            made = {}
+
+            def merged(h, flip, made=made, high=high, low=low, lane=lane):
+                if (h, flip) not in made:
+                    both = (high[h], turn(low[h], -2 * n))
+                    made[h, flip] = jnp.where(lane % 16 < 8, both[flip], both[1 - flip])
+                return made[h, flip]
             for x in {-1: range(n - reach, n), 0: range(n), 1: range(reach)}[to_x]:
                 at = (EDGE + to_x * n + x, pl.ds(row, height), slice(None))
                 g, h = x // each, x // cuts_each
                 if to_x < 0:
                     g, h = g - (groups - body.shape[0]), h - (cuts - high.shape[0])
                 near = turn(body[g], -(x % each) * n) if body is not None else s[at]
-                above = turn(high[h], n - cut * (x % cuts_each))
-                under = turn(low[h], -n - cut * (x % cuts_each))
-                s[at] = jnp.where(lane < n, near, jnp.where(lane < 64, above, under))
+                if n == 8:
+                    ends = jnp.where(lane < 64, turn(high[h], n - cut * (x % cuts_each)), turn(low[h], -n - cut * (x % cuts_each)))
+                else:
+                    ends = turn(merged(h, x % 2 if n == 32 else 0), n - cut * (x % cuts_each))
+                s[at] = jnp.where(lane < n, near, ends)
 
     def finish(self):
         for way in WAYS:
@@ -698,26 +748,28 @@
     n0 = blocks[0][0]
     raw_g, raw_v, raw_sems = take(3)
     sent_shapes, got_shapes = Top.shapes(n0)
-    w0, d0 = take(2)
-    top = Top(blocks[0], places, counts, r, b, gr, gb, w0, d0, take(len(sent_shapes)), dict(zip(WAYS, take(len(WAYS)))), take(2))
+    w0, d0, beside = take(3)
+    top = Top(blocks[0], places, counts, beside, r, b, gr, gb, w0, d0, take(len(sent_shapes)), dict(zip(WAYS, take(len(WAYS)))), take(2))
     levels = [top]
     for number in range(1, LEVELS):
         if number < SHARED:
-            levels.append(Grid(number, blocks[number], places, counts, *take(4)))
+            levels.append(Grid(number, blocks[number], places, counts, beside, *take(4)))
         else:
-            levels.append(Grid(number, coarse[number - SHARED], (0, 0, 0), (1, 1, 1), *take(4)))
+            levels.append(Grid(number, coarse[number - SHARED], (0, 0, 0), (1, 1, 1), beside, *take(4)))
     rings = {}
     for number in REACH:
         n = blocks[number][0]
         members = take(1 + (2 if Ring.sizes(n)[2] != n else 0) + len(WAYS))
-        rings[number] = Ring(levels[number], members, take(2))
+        rings[number] = Ring(levels[number], members, take(2) if number < SHARED - 1 else rings[1].sems)
     pairs = take(LEVELS - 1)
     spreads = take(LEVELS - 1)
     centres = take(LEVELS - 1)
     block_s, block_v, packet, line, joined, packets, line_send, line_recv, gather_send, gather_recv, spread_sem = refs
 
-    loads = [pltpu.make_async_copy(source, target, raw_sems.at[i]) for i, (source, target) in enumerate(((right_side, raw_g), (guess, raw_v)))]
-    for load in loads:
+    cut = n0 // top.sets
+    loads = [[pltpu.make_async_copy(source.at[pl.ds(part * cut, cut)], target.at[pl.ds(part * cut, cut)], raw_sems.at[i, part])
+              for i, (source, target) in enumerate(((right_side, raw_g), (guess, raw_v)))] for part in range(top.sets)]
+    for load in sum(loads, []):
         load.start()
     barrier = pltpu.get_barrier_semaphore()
     nx, ny, nz = counts
@@ -725,63 +777,61 @@
     def greet(device):
         pl.semaphore_signal(barrier, inc=1, device_id=device, device_id_type=MESH)
 
+    def around_torus(way, far):
+        return {name: lax.rem(places[axis] + way[axis] * far + counts[axis], counts[axis]) for axis, name in enumerate(AXES) if way[axis]}
+
     for way in WAYS:
-        pl.when(exists(places, counts, way, 1))(lambda way=way: greet(along(places, way)))
-    near = [jnp.where(place > 0, 1, 0) + jnp.where(place < count - 1, 1, 0) for place, count in zip(places, counts)]
+        greet(around_torus(way, 1))
 
     def tell(turn):
-        for way in WAYS:
-            if not way[2] or not (way[0] or way[1]):
-                @pl.when(exists(places, counts, way, 1))
-                def _(way=way):
-                    pl.semaphore_signal(spread_sem.at[turn], inc=1, device_id=along(places, way), device_id_type=MESH)
+        for way in FLAT:
+            pl.semaphore_signal(spread_sem.at[turn], inc=1, device_id=around_torus(way, turn + 1), device_id_type=MESH)
 
     def hear(turn):
-        pl.semaphore_wait(spread_sem.at[turn], (near[0] + 1) * (near[1] + 1) - 1 + near[2])
+        pl.semaphore_wait(spread_sem.at[turn], len(FLAT))
 
     top.clear()
     top.prepare()
+    write_beside(beside)
     top.missing()
-    for load in loads:
-        load.wait()
     even = (lax.broadcasted_iota(jnp.int32, (n0, n0), 0) + lax.broadcasted_iota(jnp.int32, (n0, n0), 1)) % 2 == 0
-
-    def convert(step):
-        for i in range(4):
-            k = step * 4 + i
+    for part in range(top.sets):
+        for load in loads[part]:
+            load.wait()
+        for k in range(part * cut // 2, (part + 1) * cut // 2):
             at = (k + 2, pl.ds(8, n0), pl.ds(0, n0))
             first, second = raw_g[2 * k], raw_g[2 * k + 1]
             gr[at] = jnp.where(even, first, second)
             gb[at] = jnp.where(even, second, first)
             b[at] = jnp.where(even, raw_v[2 * k + 1], raw_v[2 * k])
-    loop(n0 // 8, convert)
+        top.pack_ends(part, False)
     top.pack(False)
-    pl.semaphore_wait(barrier, (near[0] + 1) * (near[1] + 1) * (near[2] + 1) - 1)
+    pl.semaphore_wait(barrier, len(WAYS))
     top.send()
+    tell(0)
     for level in levels[1:]:
         level.prepare()
     for ring in rings.values():
         ring.clear()
     block_v[...] = jnp.zeros_like(block_v)
     top.land()
-    tell(0)
+    hear(0)
+    tell(1)
     top.sweep(0)
     top.sweep(1)
     top.restrict_to(levels[1].s, (EDGE, 8), pairs[0])
-    hear(0)
     for number in range(1, SHARED - 1):
         level = levels[number]
         rings[number].post()
         rings[number].land()
-        tell(number)
         level.sweep(0, zero=True, beyond=level.reach)
         level.sweep(1, beyond=level.reach - 1)
         level.restrict_to(levels[number + 1].s, (EDGE, 8), pairs[number])
-        hear(number)
     last = levels[SHARED - 1]
     last.sweep(0, zero=True, beyond=2)
     last.sweep(1, beyond=1)
     last.restrict_to(block_s, (0, 0), pairs[SHARED - 1])
+    hear(1)
 
     bx, by, bz = blocks[SHARED]
     wide = LANES // bx
@@ -797,6 +847,7 @@
 
     for offset in range(1, nz):
         line_copy(places[2], lax.rem(places[2] + offset, nz)).start()
+    rings[1].finish()
     rings[SHARED - 1].post()
     top.sent()
     top.post(True)
@@ -824,6 +875,11 @@
     last.sweep(0, zero=True, beyond=last.reach)
     last.sweep(1, beyond=last.reach - 1)
     top.land(True)
+    top.sent(True)
+    for number in (SHARED - 2, SHARED - 1):
+        rings[number].finish()
+    for offset in range(1, nz):
+        line_copy(places[2], lax.rem(places[2] + offset, nz)).wait_send()
     everyone = pltpu.make_async_remote_copy(
         src_ref=packets.at[pl.ds(0, total - 1)], dst_ref=packets.at[pl.ds(0, total - 1)], send_sem=gather_send, recv_sem=gather_recv,
         device_id={AXES[0]: places[0]}, device_id_type=MESH)
@@ -871,15 +927,10 @@
     top.sweep(0)
     top.sweep(1)
 
-    top.sent(True)
-    for ring in rings.values():
-        ring.finish()
-    for offset in range(1, nz):
-        line_copy(places[2], lax.rem(places[2] + offset, nz)).wait_send()
     everyone.wait_send()
 
 
-def finish_kernel(counts, dims, r, b, gr, gb, solution, residual, d):
+def finish_kernel(counts, dims, r, b, gr, gb, solution, residual, d, beside):
     places = tuple(lax.axis_index(axis) for axis in AXES)
     step = pl.program_id(0)
     n, many = dims[1], dims[0] // 2 // pl.num_programs(0)
@@ -887,14 +938,15 @@
     @pl.when(step == 0)
     def _():
         write_diagonals(d, dims, places, counts)
+        write_beside(beside)
     even = (row_iota(n) + lane_iota(n)) % 2 == 0
     last = counts[0] * (dims[0] // 2) - 1
     group = solution.shape[0] // 2
-    for i in range(group):
-        k = step * group + i
-        at = places[0] * (dims[0] // 2) + k
-        kind = jnp.where(at == 0, 1, jnp.where(at == last, 2, 0))
-        red, black = remainders(r, b, gr, gb, d, k + 2, kind, even, n)
+    ks = [step * group + i for i in range(group)]
+    globally = [places[0] * (dims[0] // 2) + k for k in ks]
+    kinds = [jnp.where(at == 0, 1, jnp.where(at == last, 2, 0)) for at in globally]
+    results = remainders(r, b, gr, gb, d, [k + 2 for k in ks], kinds, even, n, beside, LAST_SHARE)
+    for i, (k, (red, black)) in enumerate(zip(ks, results)):
         own = (k + 2, pl.ds(8, n), slice(None))
         for out, x, y in ((solution, r[own], b[own]), (residual, red, black)):
             out[2 * i] = jnp.where(even, x, y)[:, :n]
@@ -916,9 +968,10 @@
         sems = lambda *dims: scratch.append(pltpu.SemaphoreType.DMA(dims))
         vmem(*shape)
         vmem(*shape)
-        sems(2)
+        sems(2, Top.sets)
         vmem(4, n0 + 8, LANES)
         vmem(3, n0, LANES)
+        scratch.append(pltpu.VMEM((2 * LANES, LANES), jnp.bfloat16))
         sent, got = Top.shapes(n0)
         for dims in sent:
             vmem(*dims)
@@ -946,8 +999,9 @@
                 vmem(cuts, n, LANES)
             for way in WAYS:
                 vmem(*Ring.shape(n, REACH[number], way))
-            sems(len(WAYS))
-            sems(len(WAYS))
+            if number < SHARED - 1:
+                sems(len(WAYS))
+                sems(len(WAYS))
         for number, (x, y, z) in enumerate(grids[:-1]):
             spare, tall = spare_of(number, (x, y, z))
             vmem(x // 2 + spare, max(16, tall), LANES)
@@ -967,7 +1021,7 @@
         sems(counts[2])
         scratch.append(pltpu.SemaphoreType.DMA)
         scratch.append(pltpu.SemaphoreType.DMA)
-        scratch.append(pltpu.SemaphoreType.REGULAR((SHARED - 1,)))
+        scratch.append(pltpu.SemaphoreType.REGULAR((2,)))
 
         def kernel(*refs):
             solve_kernel(counts, blocks, coarse, refs)
@@ -993,7 +1047,7 @@
             out_shape=(jax.ShapeDtypeStruct(shape, jnp.float32),) * 2,
             in_specs=[whole_block] * 4,
             out_specs=(block,) * 2,
-            scratch_shapes=[pltpu.VMEM((3, n0, LANES), jnp.float32)],
+            scratch_shapes=[pltpu.VMEM((3, n0, LANES), jnp.float32), pltpu.VMEM((2 * LANES, LANES), jnp.bfloat16)],
             compiler_params=pltpu.CompilerParams(vmem_limit_bytes=8 * 2**20),
             name="finish",
         )(*fields)

time: 68.8 us -> 63.2 us (0.919)
  Pallas kernels: 68.1 us -> 62.4 us
    pallas_call x1, Pallas kernels: 65.1 us -> 59.2 us  [per_device(): pl.pallas_call(kernel, out_shape=(field,) * 4, in_specs=[pl.BlockSpec(mem...]
where the time goes in v5:
time: 63.2 us; the launch traced here: 63.1 us
  Pallas kernels  62.4 us (99%)
  between operations  0.64 us (1%)
    pallas_call x1, Pallas kernels, per_device(): pl.pallas_call(kernel, out_shape=(field,) * 4, in_specs=[pl.BlockSpec(mem...  59.2 us
    pallas_call x1, Pallas kernels, per_device(): pl.pallas_call(last, grid=(n0 // 16,), out_shape=(jax.ShapeDtypeStruct(sh...  3.21 us

profile of v5, /device:TPU:1, one launch (start us, length us, event | category | flops | bytes accessed | tf_op | source)
XLA Modules:
  0.0 63.1 jit_solution(4760200435507745096)
XLA Ops:
  0.6 59.2 %vcycle.1 = (f32[36,88,128]{2,1,0:T(8,128)S(1)}, f32[36,88,128]{2,1,0:T(8,128)S(1)}, f32[36,88,128]{2,1,0:T(8,128)S(1)}, f32[36,88,128]{2,1,0:T(8,128)S(1)}) custom-call(f32[64,64,64]{2,1,0:T(8,128)} %refs_0_.1, f32[64,64,64]{2,1,0:T(8,128)} %refs_1_.1), custom_call_target="tpu_custom_call" | custom-call | tf_op jit(solution)/shard_map/vcycle/pallas_call | solution.py:1031
  59.9 3.2 %finish.1 = (f32[64,64,64]{2,1,0:T(8,128)}, f32[64,64,64]{2,1,0:T(8,128)}) custom-call(f32[36,88,128]{2,1,0:T(8,128)S(1)} %get-tuple-element.6.refs_0_, f32[36,88,128]{2,1,0:T(8,128)S(1)} %get-tuple-element.7.refs_1_, f32[36,88,128]{2,1,0:T(8,128)S(1)} %get-tuple-element.8.refs_2_, f32[36,88,128]{2,1,0:T(8,128)S(1)} %get-tuple-element.9.refs_3_), custom_call_target="tpu_custom_call" | custom-call | tf_op jit(solution)/shard_map/finish/pallas_call | solution.py:1044

commit v6 on v5

--- a/solution.py
+++ b/solution.py
@@ -85,14 +85,18 @@
     return jnp.where(lane < 96, lane, lane - LANES)
 
 
+def even_cells(height, start=0):
+    return (row_iota(height) + lane_iota(height) + start) % 2 == 0
+
+
 class Grid:
-    def __init__(self, number, dims, places, counts, beside, v, s, w, d):
+    def __init__(self, number, dims, places, counts, beside, r, b, gr, gb, w, d):
         self.number, self.dims, self.places, self.counts = number, dims, places, counts
-        self.v, self.s, self.w, self.d, self.beside = v, s, w, d, beside
+        self.r, self.b, self.gr, self.gb, self.w, self.d, self.beside = r, b, gr, gb, w, d, beside
         self.reach = REACH.get(number, 0)
         self.ox, self.start, self.height, _, _ = layout(number, dims)
-        self.sx, self.sy = (EDGE, 8) if self.reach else (0, 0)
-        self.rows = rows_of(dims[1])
+        self.sx, self.sy = (EDGE // 2, 8) if self.reach else (0, 0)
+        self.pairs = dims[0] // 2
         self.spare, self.tall = spare_of(number, dims)
 
     def prepare(self):
@@ -106,110 +110,105 @@
             valid = (lane >= -beyond) & (lane < z + beyond) & (row >= -beyond) & (row < y + beyond)
             valid = valid & (at_y >= 0) & (at_y <= last_y) & (at_z >= 0) & (at_z <= last_z)
             one = lambda at, last: (at == 0).astype(jnp.float32) + (at == last).astype(jnp.float32)
-            return valid, 6.0 + one(at_y, last_y) + one(at_z, last_z)
-        valid, diagonal = base(self.w.shape[1], self.start)
-        for wall in range(2):
-            self.w[wall] = jnp.where(valid, 1.0 / (diagonal + wall), 0.0)
-        self.w[2] = jnp.zeros_like(diagonal)
-        valid, diagonal = base(self.tall, 8 - self.spare)
-        for wall in range(2):
-            self.d[wall] = jnp.where(valid, diagonal + wall, 0.0)
-        self.v[...] = jnp.zeros_like(self.v)
-        if self.reach:
-            self.s[...] = jnp.zeros_like(self.s)
-
-    def wall(self, plane, beyond=False):
-        at = self.places[0] * self.dims[0] + plane
-        last = self.counts[0] * self.dims[0] - 1
+            return valid, 6.0 + one(at_y, last_y) + one(at_z, last_z), even_cells(height, start)
+        valid, diagonal, even = base(self.w.shape[1], self.start)
+        plain, more = (jnp.where(valid, 1.0 / (diagonal + wall), 0.0) for wall in range(2))
+        self.w[0] = plain
+        self.w[1] = jnp.where(even, more, plain)
+        self.w[2] = jnp.where(even, plain, more)
+        self.w[3] = jnp.zeros_like(plain)
+        valid, diagonal, even = base(self.tall, 8 - self.spare)
+        self.d[0] = jnp.where(valid, diagonal, 0.0)
+        self.d[1] = jnp.where(valid, jnp.where(even, diagonal + 1.0, diagonal), 0.0)
+        self.d[2] = jnp.where(valid, jnp.where(even, diagonal, diagonal + 1.0), 0.0)
+        for ref in (self.r, self.b) + ((self.gr, self.gb) if self.reach else ()):
+            ref[...] = jnp.zeros_like(ref)
+
+    def kind(self, pair, beyond):
+        at = self.places[0] * self.pairs + pair
+        last = self.counts[0] * self.pairs - 1
         if isinstance(at, int):
-            return int(at in (0, last))
-        kind = jnp.where((at == 0) | (at == last), 1, 0)
-        return jnp.where((at < 0) | (at > last), 2, kind) if beyond else kind
-
-    def total(self, plane, count, start, height):
-        at = plane + self.ox
-        slab = self.v[pl.ds(at - 1, count + 2), pl.ds(start, height), :]
-        centre = slab[1:-1]
-        total = slab[2:] + slab[:-2]
-        total = total + self.v[pl.ds(at, count), pl.ds(start + 1, height), :] + self.v[pl.ds(at, count), pl.ds(start - 1, height), :]
-        out = []
-        centres = [centre[i] for i in range(count)]
-        for i, beside in enumerate(lane_sums(centres, self.beside, GRID_SHARE)):
-            out.append(total[i] + beside)
-        return out, centres
+            return {0: 1, last: 2}.get(at, 0)
+        kind = jnp.where(at == 0, 1, jnp.where(at == last, 2, 0))
+        return jnp.where((at < 0) | (at > last), 3, kind) if beyond else kind
 
     def sweep(self, colour, zero=False, beyond=0):
         start, height = self.start, self.height
         if self.reach and not zero:
             start, height = start + 1, inner_height(self.number, self.dims)
-        planes = self.dims[0] + 2 * beyond
-        chunk = widest(planes, 112 * 8 // height, 2)
-        parity = (row_iota(height) + lane_iota(height) + start) % 2
-
-        def body(step):
-            first = step * chunk - beyond
-            if not zero:
-                totals, centres = self.total(first, chunk, start, height)
-            results = []
-            for i in range(chunk):
-                weight = self.w[self.wall(first + i, beyond > 0), pl.ds(start - self.start, height), :]
-                given = self.s[first + i + self.sx, pl.ds(start - 8 + self.sy, height), :]
-                mine = parity == (i + colour + beyond) % 2
-                if zero:
-                    results.append(jnp.where(mine, given * weight, 0.0))
-                else:
-                    results.append(jnp.where(mine, (given + totals[i]) * weight, centres[i]))
-            for i in range(chunk):
-                self.v[first + i + self.ox, pl.ds(start, height), :] = results[i]
-        loop(planes // chunk, body)
-
-    def remainder(self, first, chunk):
-        totals, centres = self.total(first, chunk, 8 - self.spare, self.tall)
-        out = []
-        for i in range(chunk):
-            d = self.d[self.wall(first + i)]
-            r = self.s[first + i + self.sx, pl.ds(self.sy - self.spare, self.tall), :] - (d * centres[i] - totals[i])
-            out.append(r if self.dims[1] >= 8 else jnp.where(d > 0, r, 0.0))
-        return out
+        beyond = -(-beyond // 2)
+        source, target, given = (self.r, self.b, self.gb) if colour else (self.b, self.r, self.gr)
+        even = even_cells(height, start)
+        ks = list(range(-beyond, self.pairs + beyond))
+        if not zero:
+            totals = around(source, [k + self.ox for k in ks], start, height, even, colour, self.beside, GRID_SHARE)
+        for i, k in enumerate(ks):
+            kind = self.kind(k, beyond > 0)
+            weight = self.w[swapped(kind) if colour else kind, pl.ds(start - self.start, height), :]
+            value = given[k + self.sx, pl.ds(start - 8 + self.sy, height), :]
+            target[k + self.ox, pl.ds(start, height), :] = (value if zero else value + totals[i]) * weight
 
     def restrict_to(self, target, corner, pairs):
-        rows, planes = self.tall, self.dims[0] + 2 * self.spare
-        chunk = widest(planes, 96 * 8 // rows, 2)
-        half = chunk // 2
+        rows, extra = self.tall, self.spare // 2
         if rows < 16:
             pairs[...] = jnp.zeros_like(pairs)
-
-        def first(step):
-            r = self.remainder(step * chunk - self.spare, chunk)
-            for i in range(half):
-                pairs[step * half + i, pl.ds(0, rows), :] = r[2 * i] + r[2 * i + 1]
-        loop(planes // chunk, first)
-        narrow(planes, rows, self.dims[2], self.spare, target, [at - self.spare // 2 for at in corner], pairs)
+        ks = list(range(-extra, self.pairs + extra))
+        ats = [k + self.ox for k in ks]
+        first = 8 - self.spare
+        even = even_cells(rows, first)
+        reds = around(self.b, ats, first, rows, even, 0, self.beside, GRID_SHARE)
+        blacks = around(self.r, ats, first, rows, even, 1, self.beside, GRID_SHARE)
+        for i, k in enumerate(ks):
+            kind = self.kind(k, False)
+            at = (k + self.ox, pl.ds(first, rows), slice(None))
+            own = (k + self.sx, pl.ds(self.sy - self.spare, rows), slice(None))
+            red = self.gr[own] - (self.d[kind] * self.r[at] - reds[i])
+            black = self.gb[own] - (self.d[swapped(kind)] * self.b[at] - blacks[i])
+            pairs[i, pl.ds(0, rows), :] = red + black
+        narrow(2 * len(ks), rows, self.dims[2], self.spare, target, [at - self.spare // 2 for at in corner], pairs)
 
     def reflect(self):
-        (x, y, z), v, ox = self.dims, self.v, self.ox
-        margin = 3 if self.reach else 0
-        for_all = pl.ds(ox - margin, x + 2 * margin)
-
-        def low_x():
-            v[ox - 1] = -v[ox]
-
-        def high_x():
-            v[ox + x] = -v[ox + x - 1]
-
-        def low_y():
-            v[for_all, pl.ds(7, 1), :] = -v[for_all, pl.ds(8, 1), :]
-
-        def high_y():
-            v[for_all, pl.ds(8 + y, 1), :] = -v[for_all, pl.ds(7 + y, 1), :]
-
-        for axis, low, high in ((0, low_x, high_x), (1, low_y, high_y)):
-            if isinstance(self.counts[axis], int) and isinstance(self.places[axis], int):
-                low()
-                high()
+        (x, y, z), r, b, ox = self.dims, self.r, self.b, self.ox
+        margin = 2 if self.reach else 0
+        for_all = pl.ds(ox - margin, self.pairs + 2 * margin)
+
+        def across(to, at):
+            r[to] = -b[at]
+            b[to] = -r[at]
+        sides = (
+            (0, 0, lambda: across(ox - 1, ox)),
+            (0, 1, lambda: across(ox + self.pairs, ox + self.pairs - 1)),
+            (1, 0, lambda: across((for_all, pl.ds(7, 1)), (for_all, pl.ds(8, 1)))),
+            (1, 1, lambda: across((for_all, pl.ds(8 + y, 1)), (for_all, pl.ds(7 + y, 1)))),
+        )
+        for axis, high, step in sides:
+            if isinstance(self.places[axis], int):
+                step()
             else:
-                pl.when(self.places[axis] == 0)(low)
-                pl.when(self.places[axis] == self.counts[axis] - 1)(high)
+                pl.when(self.places[axis] == (self.counts[axis] - 1 if high else 0))(step)
+
+    def planes(self, step, many, low, tall):
+        even = even_cells(tall)
+        out = []
+        for i in range(many // 2):
+            at = (step * (many // 2) + (low // 2 + i + self.ox), pl.ds(0, tall), slice(None))
+            r, b = self.r[at], self.b[at]
+            out += [jnp.where(even, r, b), jnp.where(even, b, r)]
+        return out
+
+
+def swapped(kind):
+    if isinstance(kind, int):
+        return {1: 2, 2: 1}.get(kind, kind)
+    return jnp.where(kind == 1, 2, jnp.where(kind == 2, 1, kind))
+
+
+class Block:
+    def __init__(self, v, dims, places, counts):
+        self.v, self.dims, self.places, self.counts = v, dims, places, counts
+
+    def planes(self, step, many, low, tall):
+        return [self.v[step * many + (low + 4 + i), pl.ds(0, tall), :] for i in range(many)]
 
 
 def narrow(planes, rows, z, spare, target, corner, pairs):
@@ -219,13 +218,21 @@
     inside = (source_lane >= -spare) & (source_lane < z + spare)
     halve = jnp.where(((source_lane + LANES) // 2 - LANES // 2 == target_lane) & inside, 0.5, 0.0).astype(jnp.bfloat16)
     planes = planes // 2
-    many = widest(planes, max(1, 512 // coarse_rows))
+    many = widest(planes, max(2, 512 // coarse_rows), 2)
 
     def second(step):
         at = pl.ds(step * many, many)
         q = pairs[at, pl.ds(0, coarse_rows, stride=2), :] + pairs[at, pl.ds(1, coarse_rows, stride=2), :]
         q = near_dot(q.reshape(many * coarse_rows, LANES), halve)
-        target[pl.ds(step * many + corner[0], many), pl.ds(corner[1], coarse_rows), :] = q.reshape(many, coarse_rows, LANES)
+        q = q.reshape(many, coarse_rows, LANES)
+        if not isinstance(target, tuple):
+            target[pl.ds(step * many + corner[0], many), pl.ds(corner[1], coarse_rows), :] = q
+            return
+        even = even_cells(coarse_rows, corner[1])
+        for i in range(many // 2):
+            at = (step * (many // 2) + (corner[0] // 2 + i), pl.ds(corner[1], coarse_rows), slice(None))
+            target[0][at] = jnp.where(even, q[2 * i], q[2 * i + 1])
+            target[1][at] = jnp.where(even, q[2 * i + 1], q[2 * i])
     loop(planes // many, second)
 
 
@@ -239,10 +246,10 @@
     if number in REACH:
         reach = REACH[number]
         height = rows_of(y + 2 * reach)
-        return EDGE, 8 - reach, height, x + 2 * EDGE, max(40, y + 24)
+        return EDGE // 2, 8 - reach, height, x // 2 + EDGE, max(40, y + 24)
     if number == SHARED:
-        return EDGE, 8, rows_of(y), x + 2 * EDGE, rows_of(y) + 24
-    return 1, 8, rows_of(y), x + 2, rows_of(y) + 16
+        return EDGE // 2, 8, rows_of(y), x // 2 + EDGE, rows_of(y) + 24
+    return 1, 8, rows_of(y), x // 2 + 2, rows_of(y) + 16
 
 
 def inner_height(number, dims):
@@ -257,12 +264,14 @@
     low = below_zero(number)
     count = coarse[0] - 2 * low
     height = rows_of(coarse[1] - 2 * low)
-    return low, count, height, count + 2, rows_of(8 + low + height + 1)
-
-
-def widen(v, ox, dims, places, counts, number, spread, centre):
+    first = (low - 1) // 2 * 2
+    return low, count, height, first, -(-(low + count + 1 - first) // 2) * 2, rows_of(8 + low + height + 1)
+
+
+def widen(below, number, spread, centre):
+    dims, places, counts = below.dims, below.places, below.counts
     z = dims[2]
-    low, count, height, planes, tall = lift_shape(number, dims)
+    _, _, _, start, planes, tall = lift_shape(number, dims)
     beyond = EDGE if number in FINAL else 0
     k = signed(lax.broadcasted_iota(jnp.int32, (LANES, LANES), 0))
     f = signed(lax.broadcasted_iota(jnp.int32, (LANES, LANES), 1))
@@ -275,56 +284,45 @@
     beside = jnp.where((k == near) & inside, 0.25, 0.0)
     both = own + jnp.where(outside, -own, beside)
     matrix = jnp.concatenate([own, both], axis=1).astype(jnp.bfloat16)
-    many = widest(planes, max(1, 1024 // tall))
+    many = widest(planes, max(2, 1024 // tall), 2)
 
     def first(step):
-        e = v[pl.ds(step * many + (ox + low - 1), many), pl.ds(0, tall), :]
-        product = near_dot(e.reshape(many * tall, LANES), matrix)
+        e = jnp.concatenate(below.planes(step, many, start, tall), axis=0)
+        product = near_dot(e, matrix)
         at = pl.ds(step * many, many)
         spread[at] = product[:, :LANES].reshape(many, tall, LANES)
         centre[at] = product[:, LANES:].reshape(many, tall, LANES)
     loop(planes // many, first)
 
 
-def lift(v, ox, dims, places, counts, fine, spread, centre):
-    x, y, z = dims
+def lift(below, fine, spread, centre):
+    (x, y, z), places, counts = below.dims, below.places, below.counts
     number = fine.number
-    low, count, height, planes, tall = lift_shape(number, dims)
-    beyond = EDGE if number in FINAL else 0
-    widen(v, ox, dims, places, counts, number, spread, centre)
-    group = widest(count, max(1, 256 // height))
+    low, count, height, start, _, _ = lift_shape(number, below.dims)
+    beyond = number in FINAL
+    widen(below, number, spread, centre)
+    group = widest(count, max(1, 512 // height))
     row = places[1] * y + row_iota(height) + low
     valid = (row >= 0) & (row < counts[1] * y)
-    if not beyond:
-        valid = row_iota(height) < y
-    masked = beyond > 0 or y < height
     even = lane_iota(height) % 2 == 0
+    skip = low - start
 
     def second(step):
         for i in range(group):
             plane = step * group + i
-            middle = centre[plane + 1, pl.ds(8 + low, height), :]
-            ys = (spread[plane + 1, pl.ds(7 + low, height), :], spread[plane + 1, pl.ds(9 + low, height), :])
-            xs = [spread[plane + 2 * up_x, pl.ds(8 + low, height), :] for up_x in range(2)]
+            middle = centre[plane + skip, pl.ds(8 + low, height), :]
+            ys = (spread[plane + skip, pl.ds(7 + low, height), :], spread[plane + skip, pl.ds(9 + low, height), :])
+            xs = [spread[plane + skip + 2 * up_x - 1, pl.ds(8 + low, height), :] for up_x in range(2)]
             here = valid
             if beyond:
                 at = places[0] * x + plane + low
                 here = valid & ((at >= 0) & (at < counts[0] * x))
             for up_y in range(2):
-                rows = pl.ds(8 + 2 * low + up_y, height, stride=2)
-                middle_y = middle + ys[up_y]
-                if number == 0:
-                    q = middle_y + jnp.where(even, xs[1 - up_y], xs[up_y])
+                q = (middle + ys[up_y]) + jnp.where(even, xs[1 - up_y], xs[up_y])
+                if beyond or y < height:
                     q = jnp.where(here, q, 0.0)
-                    at = (plane + low + fine.ox, rows, slice(None))
-                    fine.b[at] = fine.b[at] + q
-                    continue
-                for up_x in range(2):
-                    q = middle_y + xs[up_x]
-                    if masked:
-                        q = jnp.where(here, q, 0.0)
-                    at = (2 * (plane + low) + up_x + fine.ox, rows, slice(None))
-                    fine.v[at] = fine.v[at] + q
+                at = (plane + low + fine.ox, pl.ds(8 + 2 * low + up_y, height, stride=2), slice(None))
+                fine.b[at] = fine.b[at] + q
     loop(count // group, second)
 
 
@@ -620,7 +618,7 @@
     rows = pl.ds(8, n)
     out = []
     for at, kind, reds, blacks in zip(ats, kinds, around(b, ats, 8, n, even, 0, beside, share), around(r, ats, 8, n, even, 1, beside, share)):
-        other = jnp.where(kind == 1, 2, jnp.where(kind == 2, 1, kind))
+        other = swapped(kind)
         out.append((gr[at, rows, :] - (d[kind] * r[at, rows, :] - reds), gb[at, rows, :] - (d[other] * b[at, rows, :] - blacks)))
     return out
 
@@ -678,11 +676,13 @@
             device_id={name: self.places[axis] + way[axis] for axis, name in enumerate(AXES) if way[axis]}, device_id_type=MESH)
 
     def post(self):
-        n, s = self.level.dims[0], self.level.s
+        n, gr, gb = self.level.dims[0], self.level.gr, self.level.gb
         each, groups, cut, cuts_each, cuts = Ring.sizes(n)
+        even = even_cells(n)
 
         def plane(x):
-            value = s[EDGE + x, pl.ds(8, n), :]
+            at = (x // 2 + EDGE // 2, pl.ds(8, n), slice(None))
+            value = jnp.where(even, gb[at], gr[at]) if x % 2 else jnp.where(even, gr[at], gb[at])
             return jnp.where(lane_iota(n) < n, value, 0.0) if SPARE.get(self.level.number - 1) else value
         for g in range(groups):
             value = plane(g * each)
@@ -703,7 +703,8 @@
             pl.when(exists(self.places, self.counts, way, 1))(self.copy(way).start)
 
     def land(self):
-        n, s, reach = self.level.dims[0], self.level.s, self.level.reach
+        n, gr, gb, reach = self.level.dims[0], self.level.gr, self.level.gb, self.level.reach
+        reach += reach % 2
         each, groups, cut, cuts_each, cuts = Ring.sizes(n)
         for to_x, to_y in sorted(itertools.product((-1, 0, 1), repeat=2), key=lambda at: abs(at[0]) * 3 + abs(at[1])):
             for way in WAYS:
@@ -723,17 +724,25 @@
                     both = (high[h], turn(low[h], -2 * n))
                     made[h, flip] = jnp.where(lane % 16 < 8, both[flip], both[1 - flip])
                 return made[h, flip]
-            for x in {-1: range(n - reach, n), 0: range(n), 1: range(reach)}[to_x]:
-                at = (EDGE + to_x * n + x, pl.ds(row, height), slice(None))
+            even = even_cells(height, row)
+
+            def value(x, body=body, high=high, low=low, lane=lane, merged=merged, to_x=to_x):
                 g, h = x // each, x // cuts_each
                 if to_x < 0:
                     g, h = g - (groups - body.shape[0]), h - (cuts - high.shape[0])
-                near = turn(body[g], -(x % each) * n) if body is not None else s[at]
                 if n == 8:
                     ends = jnp.where(lane < 64, turn(high[h], n - cut * (x % cuts_each)), turn(low[h], -n - cut * (x % cuts_each)))
                 else:
                     ends = turn(merged(h, x % 2 if n == 32 else 0), n - cut * (x % cuts_each))
-                s[at] = jnp.where(lane < n, near, ends)
+                return ends if body is None else jnp.where(lane < n, turn(body[g], -(x % each) * n), ends)
+            for x in {-1: range(n - reach, n, 2), 0: range(0, n, 2), 1: range(0, reach, 2)}[to_x]:
+                at = (EDGE // 2 + (to_x * n + x) // 2, pl.ds(row, height), slice(None))
+                first, second = value(x), value(x + 1)
+                red, black = jnp.where(even, first, second), jnp.where(even, second, first)
+                if body is None:
+                    red, black = jnp.where(lane < n, gr[at], red), jnp.where(lane < n, gb[at], black)
+                gr[at] = red
+                gb[at] = black
 
     def finish(self):
         for way in WAYS:
@@ -753,9 +762,9 @@
     levels = [top]
     for number in range(1, LEVELS):
         if number < SHARED:
-            levels.append(Grid(number, blocks[number], places, counts, beside, *take(4)))
+            levels.append(Grid(number, blocks[number], places, counts, beside, *take(6)))
         else:
-            levels.append(Grid(number, coarse[number - SHARED], (0, 0, 0), (1, 1, 1), beside, *take(4)))
+            levels.append(Grid(number, coarse[number - SHARED], (0, 0, 0), (1, 1, 1), beside, *take(6)))
     rings = {}
     for number in REACH:
         n = blocks[number][0]
@@ -819,14 +828,14 @@
     tell(1)
     top.sweep(0)
     top.sweep(1)
-    top.restrict_to(levels[1].s, (EDGE, 8), pairs[0])
+    top.restrict_to((levels[1].gr, levels[1].gb), (EDGE, 8), pairs[0])
     for number in range(1, SHARED - 1):
         level = levels[number]
         rings[number].post()
         rings[number].land()
         level.sweep(0, zero=True, beyond=level.reach)
         level.sweep(1, beyond=level.reach - 1)
-        level.restrict_to(levels[number + 1].s, (EDGE, 8), pairs[number])
+        level.restrict_to((levels[number + 1].gr, levels[number + 1].gb), (EDGE, 8), pairs[number])
     last = levels[SHARED - 1]
     last.sweep(0, zero=True, beyond=2)
     last.sweep(1, beyond=1)
@@ -889,15 +898,19 @@
     def unpack(px):
         for py in range(0, ny, 2):
             pair = jnp.concatenate([packets[px * ny + py], packets[px * ny + py + 1]], axis=0)
-            for x in range(bx):
-                whole.s[px * bx + x, pl.ds(py * by, 2 * by), :] = turn(pair, -x * wide)
+            cells = even_cells(2 * by)
+            for x in range(0, bx, 2):
+                first, second = turn(pair, -x * wide), turn(pair, -(x + 1) * wide)
+                at = (px * (bx // 2) + x // 2, pl.ds(py * by, 2 * by), slice(None))
+                whole.gr[at] = jnp.where(cells, first, second)
+                whole.gb[at] = jnp.where(cells, second, first)
     loop(nx, unpack)
 
     for number in range(SHARED, LEVELS - 1):
         level = levels[number]
         level.sweep(0, zero=True)
         level.sweep(1)
-        level.restrict_to(levels[number + 1].s, (0, 0), pairs[number])
+        level.restrict_to((levels[number + 1].gr, levels[number + 1].gb), (0, 0), pairs[number])
     level = levels[LEVELS - 1]
     level.sweep(0, zero=True)
     level.sweep(1)
@@ -907,23 +920,27 @@
     for number in reversed(range(SHARED, LEVELS - 1)):
         level, below = levels[number], levels[number + 1]
         below.reflect()
-        lift(below.v, below.ox, below.dims, (0, 0, 0), (1, 1, 1), level, spreads[number], centres[number])
+        lift(below, level, spreads[number], centres[number])
         level.sweep(0)
         level.sweep(1)
 
     whole.reflect()
     shift = lax.rem(LANES - places[2] * bz, LANES)
     odd = lax.rem(places[1] + 1, 2) == 1
-    for x in range(bx + 8):
-        part = whole.v[places[0] * bx + (x - 4 + whole.ox), pl.ds(pl.multiple_of((places[1] + 1) // 2 * 8, 8), 24), :]
-        block_v[x, pl.ds(4, 16)] = pltpu.roll(jnp.where(odd, part[4:20], part[:16]), shift, 1)
-    lift(block_v, 4, blocks[SHARED], places, counts, levels[SHARED - 1], spreads[SHARED - 1], centres[SHARED - 1])
+    cells = even_cells(24)
+    for x in range(0, bx + 8, 2):
+        at = (places[0] * (bx // 2) + (x // 2 - 2 + whole.ox), pl.ds(pl.multiple_of((places[1] + 1) // 2 * 8, 8), 24), slice(None))
+        r_part, b_part = whole.r[at], whole.b[at]
+        for i, part in enumerate((jnp.where(cells, r_part, b_part), jnp.where(cells, b_part, r_part))):
+            block_v[x + i, pl.ds(4, 16)] = pltpu.roll(jnp.where(odd, part[4:20], part[:16]), shift, 1)
+    around_block = Block(block_v, blocks[SHARED], places, counts)
+    lift(around_block, levels[SHARED - 1], spreads[SHARED - 1], centres[SHARED - 1])
     for number in reversed(range(1, SHARED)):
         level = levels[number]
-        level.sweep(0, beyond=level.reach - (1 if number == 1 else 2))
+        level.sweep(0, beyond=level.reach - 2)
         level.sweep(1, beyond=level.reach - 3)
         level.reflect()
-        lift(level.v, level.ox, level.dims, places, counts, levels[number - 1], spreads[number - 1], centres[number - 1])
+        lift(level, levels[number - 1], spreads[number - 1], centres[number - 1])
     top.sweep(0)
     top.sweep(1)
 
@@ -982,14 +999,13 @@
         for number, (x, y, z) in enumerate(grids):
             if number == 0:
                 continue
-            _, _, height, planes, tall = layout(number, (x, y, z))
-            vmem(planes, tall, LANES)
-            if number in REACH:
-                vmem(planes, tall, LANES)
-            else:
-                vmem(x, rows_of(y), LANES)
-            vmem(3, max(height, rows_of(inner_height(number, (x, y, z)) + 1)) if number in REACH else height, LANES)
-            vmem(2, spare_of(number, (x, y, z))[1], LANES)
+            _, _, height, extent, tall = layout(number, (x, y, z))
+            vmem(extent, tall, LANES)
+            vmem(extent, tall, LANES)
+            for _ in range(2):
+                vmem(*((extent, tall) if number in REACH else (x // 2, rows_of(y))), LANES)
+            vmem(4, max(height, rows_of(inner_height(number, (x, y, z)) + 1)) if number in REACH else height, LANES)
+            vmem(3, spare_of(number, (x, y, z))[1], LANES)
         for number in REACH:
             n = blocks[number][0]
             _, groups, cut, _, cuts = Ring.sizes(n)
@@ -1007,7 +1023,7 @@
             vmem(x // 2 + spare, max(16, tall), LANES)
         for _ in range(2):
             for number in range(LEVELS - 1):
-                _, _, _, planes, tall = lift_shape(number, blocks[number + 1] if number < SHARED else grids[number + 1])
+                _, _, _, _, planes, tall = lift_shape(number, blocks[number + 1] if number < SHARED else grids[number + 1])
                 vmem(planes, tall, LANES)
         bx, by, bz = blocks[SHARED]
         vmem(bx, rows_of(by), LANES)

time: 63.2 us -> 60.7 us (0.960)
  Pallas kernels: 62.4 us -> 60 us
    pallas_call x1, Pallas kernels: 59.2 us -> 56.7 us  [per_device(): pl.pallas_call(kernel, out_shape=(field,) * 4, in_specs=[pl.BlockSpec(mem...]
where the time goes in v6:
time: 60.7 us; the launch traced here: 60.6 us
  Pallas kernels  60 us (99%)
  between operations  0.64 us (1%)
    pallas_call x1, Pallas kernels, per_device(): pl.pallas_call(kernel, out_shape=(field,) * 4, in_specs=[pl.BlockSpec(mem...  56.7 us
    pallas_call x1, Pallas kernels, per_device(): pl.pallas_call(last, grid=(n0 // 16,), out_shape=(jax.ShapeDtypeStruct(sh...  3.21 us

profile of v6, /device:TPU:1, one launch (start us, length us, event | category | flops | bytes accessed | tf_op | source)
XLA Modules:
  0.0 60.6 jit_solution(16723645815048650074)
XLA Ops:
  0.6 56.7 %vcycle.1 = (f32[36,88,128]{2,1,0:T(8,128)S(1)}, f32[36,88,128]{2,1,0:T(8,128)S(1)}, f32[36,88,128]{2,1,0:T(8,128)S(1)}, f32[36,88,128]{2,1,0:T(8,128)S(1)}) custom-call(f32[64,64,64]{2,1,0:T(8,128)} %refs_0_.1, f32[64,64,64]{2,1,0:T(8,128)} %refs_1_.1), custom_call_target="tpu_custom_call" | custom-call | tf_op jit(solution)/shard_map/vcycle/pallas_call | solution.py:1047
  57.4 3.2 %finish.1 = (f32[64,64,64]{2,1,0:T(8,128)}, f32[64,64,64]{2,1,0:T(8,128)}) custom-call(f32[36,88,128]{2,1,0:T(8,128)S(1)} %get-tuple-element.6.refs_0_, f32[36,88,128]{2,1,0:T(8,128)S(1)} %get-tuple-element.7.refs_1_, f32[36,88,128]{2,1,0:T(8,128)S(1)} %get-tuple-element.8.refs_2_, f32[36,88,128]{2,1,0:T(8,128)S(1)} %get-tuple-element.9.refs_3_), custom_call_target="tpu_custom_call" | custom-call | tf_op jit(solution)/shard_map/finish/pallas_call | solution.py:1060

commit v7 on v6

--- a/solution.py
+++ b/solution.py
@@ -53,8 +53,8 @@
 def near_dot(value, matrix):
     first = value.astype(jnp.bfloat16)
     second = (value - first.astype(jnp.float32)).astype(jnp.bfloat16)
-    dot = lambda part: jnp.dot(part, matrix, preferred_element_type=jnp.float32)
-    return dot(second) + dot(first)
+    both = jnp.concatenate([first, second], axis=1)
+    return jnp.dot(both, jnp.concatenate([matrix, matrix], axis=0), preferred_element_type=jnp.float32)
 
 
 def write_beside(beside):
@@ -65,7 +65,7 @@
 
 
 def lane_sums(values, beside, share):
-    many = int(len(values) * share)
+    many = int(len(values) * share) if len(values) * values[0].shape[0] >= 60 * 8 else 0
     out = []
     if many:
         height = values[0].shape[0]
@@ -538,13 +538,14 @@
         high, low = got[(0, 0, -1)], got[(0, 0, 1)]
 
         def body(t):
-            at = pl.ds(pl.multiple_of(t * 8, 8), 8)
+            at = pl.ds(t * 8, 8)
             packs = [(high[index, at], low[index, at]) for index in range(len(arrays))]
             for k in range(pairs):
-                own = (k + 2, pl.ds(pl.multiple_of(t * 8 + 8, 8), 8), slice(None))
+                own = (k + 2, pl.ds(t * 8 + 8, 8), slice(None))
                 for (h, l), ref in zip(packs, arrays):
                     ref[own] = jnp.where(tile < 64, ref[own], ends(h, l, tile, k))
-        loop(n // 8, body)
+        for t in range(n // 8):
+            body(t)
         self.wait([way for way in WAYS if way[1] and not way[0]], again)
         for side in (-1, 1):
             face = got[(0, -side, 0)]
@@ -699,16 +700,16 @@
                     high = jnp.where((lane + (LANES - n + cut)) % LANES // cut == i, moved, high)
                 self.parts[0][g] = low
                 self.parts[1][g] = high
-        for way in WAYS:
+        for way in sorted(WAYS, key=all):
             pl.when(exists(self.places, self.counts, way, 1))(self.copy(way).start)
 
-    def land(self):
+    def land(self, near=False, rest=False):
         n, gr, gb, reach = self.level.dims[0], self.level.gr, self.level.gb, self.level.reach
-        reach += reach % 2
+        reach = 2 if near else reach + reach % 2
         each, groups, cut, cuts_each, cuts = Ring.sizes(n)
         for to_x, to_y in sorted(itertools.product((-1, 0, 1), repeat=2), key=lambda at: abs(at[0]) * 3 + abs(at[1])):
             for way in WAYS:
-                if way[:2] == (-to_x, -to_y):
+                if way[:2] == (-to_x, -to_y) and not (near and all(way)) and (all(way) or not rest):
                     pl.when(exists(self.places, self.counts, way, -1))(self.copy(way).wait_recv)
             height = 8 if to_y else n
             row = {-1: 0, 0: 8, 1: 8 + n}[to_y]
@@ -730,6 +731,8 @@
                 g, h = x // each, x // cuts_each
                 if to_x < 0:
                     g, h = g - (groups - body.shape[0]), h - (cuts - high.shape[0])
+                if near and to_x and to_y:
+                    return jnp.where(lane < n, turn(body[g], -(x % each) * n), 0.0)
                 if n == 8:
                     ends = jnp.where(lane < 64, turn(high[h], n - cut * (x % cuts_each)), turn(low[h], -n - cut * (x % cuts_each)))
                 else:
@@ -769,7 +772,7 @@
     for number in REACH:
         n = blocks[number][0]
         members = take(1 + (2 if Ring.sizes(n)[2] != n else 0) + len(WAYS))
-        rings[number] = Ring(levels[number], members, take(2) if number < SHARED - 1 else rings[1].sems)
+        rings[number] = Ring(levels[number], members, take(2))
     pairs = take(LEVELS - 1)
     spreads = take(LEVELS - 1)
     centres = take(LEVELS - 1)
@@ -832,9 +835,17 @@
     for number in range(1, SHARED - 1):
         level = levels[number]
         rings[number].post()
-        rings[number].land()
-        level.sweep(0, zero=True, beyond=level.reach)
-        level.sweep(1, beyond=level.reach - 1)
+        if number == 1:
+            rings[1].land(near=True)
+            level.sweep(0, zero=True, beyond=2)
+            level.sweep(1, beyond=1)
+        else:
+            rings[1].land(rest=True)
+            levels[1].sweep(0, zero=True, beyond=levels[1].reach)
+            levels[1].sweep(1, beyond=levels[1].reach - 1)
+            rings[number].land()
+            level.sweep(0, zero=True, beyond=level.reach)
+            level.sweep(1, beyond=level.reach - 1)
         level.restrict_to((levels[number + 1].gr, levels[number + 1].gb), (EDGE, 8), pairs[number])
     last = levels[SHARED - 1]
     last.sweep(0, zero=True, beyond=2)
@@ -947,27 +958,36 @@
     everyone.wait_send()
 
 
-def finish_kernel(counts, dims, r, b, gr, gb, solution, residual, d, beside):
+def finish_kernel(counts, dims, r, b, gr, gb, solution, residual, out_v, out_r, d, beside, sems):
     places = tuple(lax.axis_index(axis) for axis in AXES)
-    step = pl.program_id(0)
-    n, many = dims[1], dims[0] // 2 // pl.num_programs(0)
-
-    @pl.when(step == 0)
-    def _():
-        write_diagonals(d, dims, places, counts)
-        write_beside(beside)
-    even = (row_iota(n) + lane_iota(n)) % 2 == 0
-    last = counts[0] * (dims[0] // 2) - 1
-    group = solution.shape[0] // 2
-    ks = [step * group + i for i in range(group)]
-    globally = [places[0] * (dims[0] // 2) + k for k in ks]
-    kinds = [jnp.where(at == 0, 1, jnp.where(at == last, 2, 0)) for at in globally]
-    results = remainders(r, b, gr, gb, d, [k + 2 for k in ks], kinds, even, n, beside, LAST_SHARE)
-    for i, (k, (red, black)) in enumerate(zip(ks, results)):
-        own = (k + 2, pl.ds(8, n), slice(None))
-        for out, x, y in ((solution, r[own], b[own]), (residual, red, black)):
-            out[2 * i] = jnp.where(even, x, y)[:, :n]
-            out[2 * i + 1] = jnp.where(even, y, x)[:, :n]
+    n, half = dims[1], dims[0] // 2
+    write_diagonals(d, dims, places, counts)
+    write_beside(beside)
+    even = even_cells(n)
+    last = counts[0] * half - 1
+    group = 8
+
+    def copies(step):
+        part = pl.ds(step * 2 * group, 2 * group)
+        return [pltpu.make_async_copy(source.at[part], target.at[part], sems.at[i, step])
+                for i, (source, target) in enumerate(((out_v, solution), (out_r, residual)))]
+
+    def compute(step):
+        ks = [step * group + i for i in range(group)]
+        globally = [places[0] * half + k for k in ks]
+        kinds = [jnp.where(at == 0, 1, jnp.where(at == last, 2, 0)) for at in globally]
+        results = remainders(r, b, gr, gb, d, [k + 2 for k in ks], kinds, even, n, beside, LAST_SHARE)
+        for k, (red, black) in zip(ks, results):
+            own = (k + 2, pl.ds(8, n), slice(None))
+            for out, x, y in ((out_v, r[own], b[own]), (out_r, red, black)):
+                out[2 * k] = jnp.where(even, x, y)[:, :n]
+                out[2 * k + 1] = jnp.where(even, y, x)[:, :n]
+        for copy in copies(step):
+            copy.start()
+    loop(half // group, compute)
+    for step in range(half // group):
+        for copy in copies(step):
+            copy.wait()
 
 
 def solution(mesh):
@@ -1015,9 +1035,8 @@
                 vmem(cuts, n, LANES)
             for way in WAYS:
                 vmem(*Ring.shape(n, REACH[number], way))
-            if number < SHARED - 1:
-                sems(len(WAYS))
-                sems(len(WAYS))
+            sems(len(WAYS))
+            sems(len(WAYS))
         for number, (x, y, z) in enumerate(grids[:-1]):
             spare, tall = spare_of(number, (x, y, z))
             vmem(x // 2 + spare, max(16, tall), LANES)
@@ -1056,14 +1075,15 @@
 
         def last(*refs):
             finish_kernel(counts, shape, *refs)
-        block = pl.BlockSpec((16,) + shape[1:], lambda i: (i, 0, 0))
+        in_hbm = pl.BlockSpec(memory_space=pltpu.HBM)
         return pl.pallas_call(
             last,
-            grid=(n0 // 16,),
             out_shape=(jax.ShapeDtypeStruct(shape, jnp.float32),) * 2,
             in_specs=[whole_block] * 4,
-            out_specs=(block,) * 2,
-            scratch_shapes=[pltpu.VMEM((3, n0, LANES), jnp.float32), pltpu.VMEM((2 * LANES, LANES), jnp.bfloat16)],
+            out_specs=(in_hbm,) * 2,
+            scratch_shapes=[
+                pltpu.VMEM(shape, jnp.float32), pltpu.VMEM(shape, jnp.float32), pltpu.VMEM((3, n0, LANES), jnp.float32),
+                pltpu.VMEM((2 * LANES, LANES), jnp.bfloat16), pltpu.SemaphoreType.DMA((2, n0 // 16))],
             compiler_params=pltpu.CompilerParams(vmem_limit_bytes=8 * 2**20),
             name="finish",
         )(*fields)

time: 60.7 us -> 58.7 us (0.967)
  Pallas kernels: 60 us -> 57.7 us
    pallas_call x1, Pallas kernels: 56.7 us -> 55 us  [per_device(): pl.pallas_call(kernel, out_shape=(field,) * 4, in_specs=[pl.BlockSpec(mem...]
where the time goes in v7:
time: 58.7 us; the launch traced here: 58.5 us
  Pallas kernels  57.7 us (98%)
  between operations  0.8 us (1%)
    pallas_call x1, Pallas kernels, per_device(): pl.pallas_call(kernel, out_shape=(field,) * 4, in_specs=[pl.BlockSpec(mem...  55 us
    pallas_call x1, Pallas kernels, per_device(): pl.pallas_call(last, out_shape=(jax.ShapeDtypeStruct(shape, jnp.float32),...  2.72 us

profile of v7, /device:TPU:1, one launch (start us, length us, event | category | flops | bytes accessed | tf_op | source)
XLA Modules:
  0.0 58.5 jit_solution(2108085664998313209)
XLA Ops:
  0.6 55.0 %vcycle.1 = (f32[36,88,128]{2,1,0:T(8,128)S(1)}, f32[36,88,128]{2,1,0:T(8,128)S(1)}, f32[36,88,128]{2,1,0:T(8,128)S(1)}, f32[36,88,128]{2,1,0:T(8,128)S(1)}) custom-call(f32[64,64,64]{2,1,0:T(8,128)} %refs_0_.1, f32[64,64,64]{2,1,0:T(8,128)} %refs_1_.1), custom_call_target="tpu_custom_call" | custom-call | tf_op jit(solution)/shard_map/vcycle/pallas_call | solution.py:1066
  55.7 2.7 %finish.1 = (f32[64,64,64]{2,1,0:T(8,128)}, f32[64,64,64]{2,1,0:T(8,128)}) custom-call(f32[36,88,128]{2,1,0:T(8,128)S(1)} %get-tuple-element.6.refs_0_, f32[36,88,128]{2,1,0:T(8,128)S(1)} %get-tuple-element.7.refs_1_, f32[36,88,128]{2,1,0:T(8,128)S(1)} %get-tuple-element.8.refs_2_, f32[36,88,128]{2,1,0:T(8,128)S(1)} %get-tuple-element.9.refs_3_), custom_call_target="tpu_custom_call" | custom-call | tf_op jit(solution)/shard_map/finish/pallas_call | solution.py:1079

commit v8 on v7

--- a/solution.py
+++ b/solution.py
@@ -11,7 +11,7 @@
 COARSE_SWEEPS = 4
 SHARED = 4
 VMEM_LIMIT = 46
-SWEEP_SHARE, REST_SHARE, LAST_SHARE, GRID_SHARE = 0.4, 0.4, 0.0, 0.4
+SWEEP_SHARE, REST_SHARE, LAST_SHARE, GRID_SHARE = 0.4, 0.4, 0.3, 0.4
 LANES = 128
 EDGE = 8
 AXES = ("gx", "gy", "gz")
@@ -218,7 +218,7 @@
     inside = (source_lane >= -spare) & (source_lane < z + spare)
     halve = jnp.where(((source_lane + LANES) // 2 - LANES // 2 == target_lane) & inside, 0.5, 0.0).astype(jnp.bfloat16)
     planes = planes // 2
-    many = widest(planes, max(2, 512 // coarse_rows), 2)
+    many = widest(planes, max(2, 1024 // coarse_rows), 2)
 
     def second(step):
         at = pl.ds(step * many, many)
@@ -284,7 +284,7 @@
     beside = jnp.where((k == near) & inside, 0.25, 0.0)
     both = own + jnp.where(outside, -own, beside)
     matrix = jnp.concatenate([own, both], axis=1).astype(jnp.bfloat16)
-    many = widest(planes, max(2, 1024 // tall), 2)
+    many = widest(planes, max(2, 2048 // tall), 2)
 
     def first(step):
         e = jnp.concatenate(below.planes(step, many, start, tall), axis=0)
@@ -301,7 +301,7 @@
     low, count, height, start, _, _ = lift_shape(number, below.dims)
     beyond = number in FINAL
     widen(below, number, spread, centre)
-    group = widest(count, max(1, 512 // height))
+    group = widest(count, max(1, 1536 // height))
     row = places[1] * y + row_iota(height) + low
     valid = (row >= 0) & (row < counts[1] * y)
     even = lane_iota(height) % 2 == 0
@@ -388,7 +388,7 @@
         start, height = 6, self.n + 8
         source, target, given = (self.r, self.b, self.gb) if colour else (self.b, self.r, self.gr)
         count = self.pairs + 2
-        chunk = widest(count, 17)
+        chunk = widest(count, 34)
         even = (row_iota(height) + lane_iota(height)) % 2 == 0
 
         def body(step):
@@ -404,7 +404,7 @@
     def restrict_to(self, target, corner, pairs):
         n = self.n
         even = (row_iota(n) + lane_iota(n)) % 2 == 0
-        chunk = 8
+        chunk = 16
 
         def body(step):
             ks = [step * chunk + i for i in range(chunk)]
@@ -984,7 +984,8 @@
                 out[2 * k + 1] = jnp.where(even, y, x)[:, :n]
         for copy in copies(step):
             copy.start()
-    loop(half // group, compute)
+    for step in range(half // group):
+        compute(step)
     for step in range(half // group):
         for copy in copies(step):
             copy.wait()

time: 58.7 us -> 57.3 us (0.976)
  Pallas kernels: 57.7 us -> 56.4 us
    pallas_call x1, Pallas kernels: 55 us -> 53.8 us  [per_device(): pl.pallas_call(kernel, out_shape=(field,) * 4, in_specs=[pl.BlockSpec(mem...]
where the time goes in v8:
time: 57.3 us; the launch traced here: 57.2 us
  Pallas kernels  56.4 us (98%)
  between operations  0.82 us (1%)
    pallas_call x1, Pallas kernels, per_device(): pl.pallas_call(kernel, out_shape=(field,) * 4, in_specs=[pl.BlockSpec(mem...  53.8 us
    pallas_call x1, Pallas kernels, per_device(): pl.pallas_call(last, out_shape=(jax.ShapeDtypeStruct(shape, jnp.float32),...  2.63 us

profile of v8, /device:TPU:1, one launch (start us, length us, event | category | flops | bytes accessed | tf_op | source)
XLA Modules:
  0.0 57.2 jit_solution(257738542892707626)
XLA Ops:
  0.6 53.8 %vcycle.1 = (f32[36,88,128]{2,1,0:T(8,128)S(1)}, f32[36,88,128]{2,1,0:T(8,128)S(1)}, f32[36,88,128]{2,1,0:T(8,128)S(1)}, f32[36,88,128]{2,1,0:T(8,128)S(1)}) custom-call(f32[64,64,64]{2,1,0:T(8,128)} %refs_0_.1, f32[64,64,64]{2,1,0:T(8,128)} %refs_1_.1), custom_call_target="tpu_custom_call" | custom-call | tf_op jit(solution)/shard_map/vcycle/pallas_call | solution.py:1067
  54.4 2.6 %finish.1 = (f32[64,64,64]{2,1,0:T(8,128)}, f32[64,64,64]{2,1,0:T(8,128)}) custom-call(f32[36,88,128]{2,1,0:T(8,128)S(1)} %get-tuple-element.6.refs_0_, f32[36,88,128]{2,1,0:T(8,128)S(1)} %get-tuple-element.7.refs_1_, f32[36,88,128]{2,1,0:T(8,128)S(1)} %get-tuple-element.8.refs_2_, f32[36,88,128]{2,1,0:T(8,128)S(1)} %get-tuple-element.9.refs_3_), custom_call_target="tpu_custom_call" | custom-call | tf_op jit(solution)/shard_map/finish/pallas_call | solution.py:1080
